TPU v7x, 256 devices: a whole 4x4x8 slice. The times are simulated.
256 devices in a mesh: layer: 4 (over y), row: 8 (over x, core), col: 8 (over z).
Axes of the slice: x: 4, y: 4, z: 8, core: 2. Of those that a mesh axis runs over, the one named last changes fastest.
Arguments:
- hidden: bfloat16 [1536, 2304], P(('layer', 'row')), may hold values from -60 to 60
- embedding: bfloat16 [131072, 2304], P(('row', 'col'), 'layer'), may hold values from -0.3 to 0.3
- teacher: bfloat16 [1536, 131072], P('layer', ('row', 'col')), may hold values from -80 to 240
Outputs:
- grad_embedding: float32 [131072, 2304], P(('row', 'col'), 'layer')
- grad_hidden: float32 [1536, 2304], P(('layer', 'row', 'col'))
All inputs are finite; a program needn't handle non-finite values.
Results may differ from a plain program's by a relative error of at most 0.0041.
Values may be sent and summed in bfloat16 or wider, within the bound.
No kernel may reach another device: no remote copies, remote signals or barrier semaphores. Data moves between devices by JAX's collectives and lax.ppermute only.
A program may use at most 192 MiB of HBM per device.

v0:
```python
import jax
import jax.numpy as jnp
from jax import lax
from jax.sharding import PartitionSpec as P

LOSS_SCALE = 256

def shift_x(x, s):
    n = lax.axis_size("row")
    return lax.ppermute(x, "row", [(i, (i + 2 * s) % n) for i in range(n)])

def swap_core(x):
    n = lax.axis_size("row")
    return lax.ppermute(x, "row", [(i, i ^ 1) for i in range(n)])

def at(x, k, dim=0):
    return lax.dynamic_index_in_dim(x, k, dim, keepdims=False)

def put(buf, x, k, dim=0):
    return lax.dynamic_update_slice_in_dim(buf, jnp.expand_dims(x, dim), k, dim)

def ring_gather(block, shift):
    half = block.shape[0] // 2
    back = shift(block, 1)
    front = shift(block, -1)
    far = (shift(back[:half], 1), shift(front[half:], -1))
    return ((0, block), (3, back), (1, front), (2, jnp.concatenate(far)))

def ring_sum(piece, shift):
    f32, bf16 = jnp.float32, jnp.bfloat16
    far = piece(2)
    half = far.shape[0] // 2
    right, left = shift(far[:half], 1), shift(far[half:], -1)
    ahead, behind = piece(1), piece(3)
    back_b = shift(ahead[half:], 1)
    front_a = shift(behind[:half], -1)
    back_a = shift((ahead[:half].astype(f32) + right.astype(f32)).astype(bf16), 1)
    front_b = shift((behind[half:].astype(f32) + left.astype(f32)).astype(bf16), -1)
    own = piece(0).astype(f32)
    first = own[:half] + back_a.astype(f32) + front_a.astype(f32)
    second = own[half:] + back_b.astype(f32) + front_b.astype(f32)
    return jnp.concatenate([first, second])

def spread(x, axis):
    n = lax.axis_size(axis)
    return lax.all_to_all(jnp.broadcast_to(x[None], (n, *x.shape)), axis, 0, 0, tiled=True)

def joined(top, total, dim):
    best = jnp.max(top, axis=dim)
    scale = jnp.exp(top - jnp.expand_dims(best, dim))
    return best, jnp.sum(total * scale, axis=dim)

def local(hidden, embedding, teacher):
    f32, bf16 = jnp.float32, jnp.bfloat16
    layers, cols = lax.axis_size("layer"), lax.axis_size("col")
    rows = lax.axis_size("row")
    xs = rows // 2
    row = lax.axis_index("row")
    x, core = row // 2, row % 2
    strip, width = hidden.shape
    quarter = embedding.shape[1]
    block = embedding.shape[0] // layers
    home = strip * rows
    tokens = home * layers

    mine = spread(hidden, "layer")
    held = jnp.zeros((layers, xs, strip, width), bf16)
    for k, p in ring_gather(mine.reshape(layers * strip, width), shift_x):
        held = put(held, p.reshape(layers, strip, width), (x + k) % xs, 1)
    states = jnp.zeros((layers, xs, 2, strip, width), bf16)
    states = put(states, held, core, 2)
    states = put(states, swap_core(held), 1 - core, 2)
    states = states.reshape(tokens, width)

    table = embedding.T.reshape(quarter, layers, block).swapaxes(0, 1)
    table = lax.all_to_all(table, "layer", 0, 0, tiled=True).reshape(width, block)

    taught = teacher.reshape(home, layers, block).swapaxes(0, 1)
    taught = lax.all_to_all(taught, "layer", 0, 0, tiled=True)
    taught = taught.reshape(tokens, block).astype(f32)

    home_f = teacher.astype(f32)
    top_t = jnp.max(home_f, axis=1)
    sum_t = jnp.sum(jnp.exp(home_f - top_t[:, None]), axis=1)
    logits = jnp.dot(states, table, preferred_element_type=f32)
    top_s = jnp.max(logits, axis=1)
    sum_s = jnp.sum(jnp.exp(logits - top_s[:, None]), axis=1)
    stats = jnp.stack([jnp.concatenate([top_s, top_t]), jnp.concatenate([sum_s, sum_t])])
    got = spread(stats, ("layer", "row"))
    top_s, sum_s = joined(got[:, 0, :tokens], got[:, 1, :tokens], 0)
    got = got[:, :, tokens:].reshape(layers, rows, 2, home)
    top_t, sum_t = joined(got[:, :, 0], got[:, :, 1], 1)
    stats = jnp.stack([top_s, sum_s, top_t.reshape(tokens), sum_t.reshape(tokens)])
    got = spread(stats, "col")
    top_s, sum_s = joined(got[:, 0], got[:, 1], 0)
    top_t, sum_t = joined(got[:, 2], got[:, 3], 0)
    lse_s = top_s + jnp.log(sum_s)
    lse_t = top_t + jnp.log(sum_t)
    prob_s = jnp.exp(logits - lse_s[:, None])
    prob_t = jnp.exp(taught - lse_t[:, None])
    grads = ((prob_s - prob_t) * LOSS_SCALE).astype(bf16)

    halves = grads.reshape(layers, xs, 2, strip, block)
    half = lambda c: at(halves, c, 2).swapaxes(0, 1).reshape(tokens // 2, block)
    both = jnp.concatenate([half(core), swap_core(half(1 - core))], axis=1)
    both = both.reshape(xs, layers * strip, 2 * block)
    tables = jnp.concatenate([table, swap_core(table)], axis=1)

    def part(k):
        lines = at(both, (x + k) % xs)
        return lax.dot_general(
            lines, tables, (((1,), (1,)), ((), ())), preferred_element_type=f32
        ).astype(bf16)

    parts = {k: part(k) for k in (2, 1, 3)}
    grads, parts = lax.optimization_barrier((grads, parts))
    parts[0] = part(0)
    summed = ring_sum(lambda k: parts[k], shift_x).astype(bf16)
    summed = summed.reshape(layers * cols, strip // cols, width)
    summed = lax.all_to_all(summed, ("layer", "col"), 0, 0, tiled=True)
    grad_hidden = jnp.sum(summed.astype(f32), axis=0)

    grad_table = lax.dot_general(
        states, grads, (((0,), (0,)), ((), ())), preferred_element_type=f32
    ).astype(bf16)
    grad_table = grad_table.reshape(layers, quarter, block)
    grad_table = lax.all_to_all(grad_table, "layer", 0, 0, tiled=True)
    grad_table = grad_table.astype(f32).swapaxes(0, 1).reshape(quarter, layers * block)
    return grad_table.T, grad_hidden


def solution(mesh):
    placed = (P(("layer", "row"), None), P(("row", "col"), "layer"), P("layer", ("row", "col")))
    return jax.shard_map(
        local,
        mesh=mesh,
        in_specs=placed,
        out_specs=(P(("row", "col"), "layer"), P(("layer", "row", "col"), None)),
        check_vma=False,
    )
```

profile of v0, /device:TPU:1, one launch (start us, length us, event | category | flops | bytes accessed | tf_op | source)
XLA Modules:
  0.0 267.6 jit_solution(8343050298898237279)
XLA Ops:
  0.6 1.0 broadcast_in_dim.16
  1.6 16.8 %all_to_all.35 = bf16[4,48,2304]{2,1,0:T(8,128)(2,1)} all-to-all(bf16[4,48,2304]{2,1,0:T(8,128)(2,1)S(1)} %broadcast_in_dim.16), channel_id=1, replica_groups=mesh['layer'=4,'row'=8,'col'=8] {'layer'}, dimensions={0} | all-to-all | bytes 1769472 | tf_op jit(solution)/shard_map/all_to_all | solution.py:46
  18.4 1.8 collective-permute-start
  20.2 1.3 collective-permute-start.1
  21.5 0.2 broadcast_in_dim.15
  21.7 1.2 bitcast_dynamic-update-slice_fusion.2
  23.0 16.6 %collective-permute-done = bf16[192,2304]{1,0:T(8,128)(2,1)} collective-permute-done((bf16[192,2304]{1,0:T(8,128)(2,1)}, bf16[192,2304]{1,0:T(8,128)(2,1)}, u32[]{:S(2)}, u32[]{:S(2)}) %collective-permute-start) | collective-permute-done | bytes 884768 | tf_op jit(solution)/shard_map/ppermute | solution.py:10
  39.5 1.0 slice.76
  40.6 0.5 collective-permute-start.2
  41.1 1.0 slice.77
  42.1 2.4 collective-permute-start.3
  44.5 1.2 constant_dynamic-update-slice_fusion.2
  45.7 1.2 constant_dynamic-update-slice_fusion.1
  47.0 3.8 %collective-permute-done.2 = bf16[96,2304]{1,0:T(8,128)(2,1)S(1)} collective-permute-done((bf16[96,2304]{1,0:T(8,128)(2,1)S(1)}, bf16[96,2304]{1,0:T(8,128)(2,1)S(1)}, u32[]{:S(2)}, u32[]{:S(2)}) %collective-permute-start.2) | collective-permute-done | bytes 442400 | tf_op jit(solution)/shard_map/ppermute | solution.py:10
  50.7 0.2 collective-permute-done.3
  51.1 4.0 %collective-permute-start.4 = (bf16[4,4,48,2304]{3,2,1,0:T(8,128)(2,1)S(1)}, bf16[4,4,48,2304]{3,2,1,0:T(8,128)(2,1)}, u32[]{:S(2)}, u32[]{:S(2)}) collective-permute-start(bf16[4,4,48,2304]{3,2,1,0:T(8,128)(2,1)S(1)} %constant_dynamic-update-slice_fusion), channel_id=1, source_target_pairs={{0,8},{8,0},{16,24},{24,16},{32,40},{40,32},{48,56},{56,48},{1,9},... | collective-permute-start | bytes 10616840 | tf_op jit(solution)/shard_map/ppermute | solution.py:14
  55.1 6.2 %reshape.71 = bf16[576,4,512]{2,1,0:T(4,128)(2,1)} reshape(bf16[576,2048]{1,0:T(8,128)(2,1)} %bitcast.124) | data formatting | bytes 4718592 | tf_op jit(solution)/shard_map/reshape | solution.py:75
  61.3 3.5 %copy.48 = bf16[4,576,512]{2,1,0:T(8,128)(2,1)} copy(bf16[4,576,512]{2,0,1:T(4,128)(2,1)} %bitcast.119) | data formatting | bytes 4718592 | tf_op jit(solution)/shard_map/transpose | solution.py:75
  64.8 4.5 %all-to-all-start.1 = ((bf16[4,576,512]{2,1,0:T(8,128)(2,1)}), bf16[4,576,512]{2,1,0:T(8,128)(2,1)}, u32[]{:S(2)}, u32[]{:S(2)}) async-start(bf16[4,576,512]{2,1,0:T(8,128)(2,1)} %copy.48), calls=%async_computation.1 | async-start | bytes 4718592 | tf_op jit(solution)/shard_map/all_to_all | solution.py:76
  69.3 1.7 reduce_max.60
  71.0 2.1 exponential_reduce_fusion
  73.1 3.6 %broadcast_in_dim.14 = bf16[4,4,2,48,2304]{4,3,2,1,0:T(8,128)(2,1)} broadcast(bf16[]{:T(256)} %constant.77.clone.1), dimensions={} | broadcast | bytes 7077890 | tf_op jit(solution)/shard_map/broadcast_in_dim | solution.py:70
  76.7 2.0 bitcast_dynamic-update-slice_fusion
  78.7 4.1 %bitcast_dynamic-update-slice_fusion.1 = bf16[4,4,2,48,2304]{4,3,2,1,0:T(8,128)(2,1)} fusion(bf16[4,4,2,48,2304]{4,3,2,1,0:T(8,128)(2,1)} %bitcast_dynamic-update-slice_fusion, s32[]{:T(128)S(6)} %select_n.72, bf16[4,4,48,2304]{3,2,1,0:T(8,128)(2,1)} %collective-permute-done.4), kind=kLoop, calls=%fused_computation.9 | loop fusion | bytes 7077892 | tf_op jit(solution)/shard_map/dynamic_update_slice | solution.py:20
  82.8 15.8 %all-to-all-done.1 = bf16[4,576,512]{2,1,0:T(8,128)(2,1)} async-done(((bf16[4,576,512]{2,1,0:T(8,128)(2,1)}), bf16[4,576,512]{2,1,0:T(8,128)(2,1)}, u32[]{:S(2)}, u32[]{:S(2)}) %all-to-all-start.1) | async-done | bytes 2359328 | tf_op jit(solution)/shard_map/all_to_all | solution.py:76
  98.5 6.9 %fusion.46 = (f32[1536]{0:T(1024)S(1)}, f32[1536,512]{1,0:T(8,128)S(1)}) fusion(bf16[1536,2304]{1,0:T(8,128)(2,1)} %bitcast.8, bf16[2304,512]{1,0:T(8,128)(2,1)} %bitcast.11), kind=kOutput, calls=%fused_computation.91 | convolution fusion | flops 3624663552 | bytes 12589056 | tf_op jit(solution)/shard_map/dot_general | solution.py:85
  105.5 0.9 exponential_reduce_fusion.1
  106.6 17.6 %all_to_all.36 = f32[32,2,1920]{2,1,0:T(2,128)S(1)} all-to-all(f32[32,2,1920]{2,1,0:T(2,128)S(1)} %broadcast_in_dim.19), channel_id=1, replica_groups=mesh['layer'=4,'row'=8,'col'=8] {'layer','row'}, dimensions={0} | all-to-all | bytes 983040 | tf_op jit(solution)/shard_map/all_to_all | solution.py:46
  124.2 0.4 slice_reduce_fusion.3
  124.9 0.7 broadcast_in_dim.20
  125.6 8.6 %all-to-all-start.3 = ((f32[8,4,1536]{2,1,0:T(4,128)}), f32[8,4,1536]{2,1,0:T(4,128)S(1)}, u32[]{:S(2)}, u32[]{:S(2)}) async-start(f32[8,4,1536]{2,1,0:T(4,128)} %broadcast_in_dim.20), calls=%async_computation.3 | async-start | bytes 393216 | tf_op jit(solution)/shard_map/all_to_all | solution.py:46
  134.2 1.4 copy.117
  135.6 8.0 %all-to-all-done.3 = f32[8,4,1536]{2,1,0:T(4,128)S(1)} async-done(((f32[8,4,1536]{2,1,0:T(4,128)}), f32[8,4,1536]{2,1,0:T(4,128)S(1)}, u32[]{:S(2)}, u32[]{:S(2)}) %all-to-all-start.3) | async-done | bytes 196640 | tf_op jit(solution)/shard_map/all_to_all | solution.py:46
  143.7 4.4 %all-to-all-start.4 = ((bf16[4,384,512]{2,1,0:T(8,128)(2,1)}), bf16[4,384,512]{2,1,0:T(8,128)(2,1)}, u32[]{:S(2)}, u32[]{:S(2)}) async-start(bf16[4,384,512]{2,1,0:T(8,128)(2,1)} %bitcast.120), calls=%async_computation.4 | async-start | bytes 3145728 | tf_op jit(solution)/shard_map/all_to_all | solution.py:79
  148.0 2.3 collective-permute-start.6
  150.6 16.3 %all-to-all-done.4 = bf16[4,384,512]{2,1,0:T(8,128)(2,1)} async-done(((bf16[4,384,512]{2,1,0:T(8,128)(2,1)}), bf16[4,384,512]{2,1,0:T(8,128)(2,1)}, u32[]{:S(2)}, u32[]{:S(2)}) %all-to-all-start.4) | async-done | bytes 1572896 | tf_op jit(solution)/shard_map/all_to_all | solution.py:79
  166.9 2.3 fusion.4
  169.5 2.9 %collective-permute-start.5 = (bf16[768,512]{1,0:T(8,128)(2,1)S(1)}, bf16[768,512]{1,0:T(8,128)(2,1)S(1)}, u32[]{:S(2)}, u32[]{:S(2)}) collective-permute-start(bf16[768,512]{1,0:T(8,128)(2,1)S(1)} %bitcast.130), channel_id=1, source_target_pairs={{0,8},{8,0},{16,24},{24,16},{32,40},{40,32},{48,56},{56,48},{1,9},... | collective-permute-start | bytes 2359304 | tf_op jit(solution)/shard_map/ppermute | solution.py:14
  172.5 1.8 collective-permute-done.5
  174.3 4.3 %convolution_convert_fusion.2 = bf16[192,2304]{1,0:T(8,128)(2,1)S(1)} fusion(s32[]{:T(128)S(6)} %select_n.65, bf16[4,192,512]{2,1,0:T(8,128)(2,1)S(1)} %bitcast.126, bf16[4,192,512]{2,1,0:T(8,128)(2,1)S(1)} %bitcast.136, bf16[2304,512]{1,0:T(8,128)(2,1)} %collective-permute-done.6, bf16[2304,512]{1,0:T(8,128)(2,1)} %bitcast.11), kind=kOutput, calls=%fused_computation.5 | convolution fusion | flops 916635648 | bytes 7176196 | tf_op jit(solution)/shard_map/dot_general | solution.py:111
  178.7 4.4 %convolution_convert_fusion.3 = bf16[192,2304]{1,0:T(8,128)(2,1)S(1)} fusion(s32[]{:T(128)S(6)} %select_n.69, bf16[4,192,512]{2,1,0:T(8,128)(2,1)S(1)} %bitcast.127, bf16[4,192,512]{2,1,0:T(8,128)(2,1)S(1)} %bitcast.137, bf16[2304,512]{1,0:T(8,128)(2,1)} %collective-permute-done.6, bf16[2304,512]{1,0:T(8,128)(2,1)} %bitcast.11), kind=kOutput, calls=%fused_computation.6 | convolution fusion | flops 916635648 | bytes 7176196 | tf_op jit(solution)/shard_map/dot_general | solution.py:111
  183.1 4.1 %convolution_convert_fusion.4 = bf16[192,2304]{1,0:T(8,128)(2,1)S(1)} fusion(s32[]{:T(128)S(6)} %select_n.67, bf16[4,192,512]{2,1,0:T(8,128)(2,1)S(1)} %bitcast.128, bf16[4,192,512]{2,1,0:T(8,128)(2,1)S(1)} %bitcast.138, bf16[2304,512]{1,0:T(8,128)(2,1)} %collective-permute-done.6, bf16[2304,512]{1,0:T(8,128)(2,1)} %bitcast.11), kind=kOutput, calls=%fused_computation.7 | convolution fusion | flops 916635648 | bytes 7176196 | tf_op jit(solution)/shard_map/dot_general | solution.py:111
  187.2 1.0 fusion.45
  188.2 2.9 %collective-permute-start.11 = (bf16[96,2304]{1,0:T(8,128)(2,1)}, bf16[96,2304]{1,0:T(8,128)(2,1)}, u32[]{:S(2)}, u32[]{:S(2)}) collective-permute-start(bf16[96,2304]{1,0:T(8,128)(2,1)} %get-tuple-element.17), channel_id=1, source_target_pairs={{0,48},{8,56},{16,0},{24,8},{32,16},{40,24},{48,32},{56,40},{1,49}... | collective-permute-start | bytes 1327112 | tf_op jit(solution)/shard_map/ppermute | solution.py:10
  191.1 0.8 slice.73
  191.9 0.8 slice.71
  192.8 2.7 collective-permute-start.9
  195.4 8.1 %convolution_convert_fusion = bf16[2304,512]{1,0:T(8,128)(2,1)} fusion(bf16[1536,2304]{1,0:T(8,128)(2,1)} %bitcast.8, bf16[1536,512]{1,0:T(8,128)(2,1)S(1)} %fusion.4), kind=kOutput, calls=%fused_computation.2 | convolution fusion | flops 3625058304 | bytes 11010048 | tf_op jit(solution)/shard_map/dot_general | solution.py:123
  203.6 3.6 %all-to-all-start.5 = ((bf16[4,576,512]{2,1,0:T(8,128)(2,1)}), bf16[4,576,512]{2,1,0:T(8,128)(2,1)S(1)}, u32[]{:S(2)}, u32[]{:S(2)}) async-start(bf16[4,576,512]{2,1,0:T(8,128)(2,1)} %bitcast.125), calls=%async_computation.5 | async-start | bytes 4718592 | tf_op jit(solution)/shard_map/all_to_all | solution.py:127
  207.2 1.3 add_convert_fusion
  208.5 1.5 collective-permute-start.12
  210.0 1.1 add_convert_fusion.1
  211.1 0.3 collective-permute-start.8
  211.4 4.3 %fusion = f32[192,2304]{1,0:T(8,128)S(1)} fusion(s32[]{:T(128)S(6)} %select_n.63, bf16[4,192,512]{2,1,0:T(8,128)(2,1)} %bitcast.129, bf16[4,192,512]{2,1,0:T(8,128)(2,1)} %bitcast.139, bf16[2304,512]{1,0:T(8,128)(2,1)} %collective-permute-done.6, bf16[2304,512]{1,0:T(8,128)(2,1)} %bitcast.11), kind=kOutput, calls=%fused_computation.4 | convolution fusion | flops 917078016 | bytes 8060932 | tf_op jit(solution)/shard_map/dot_general | solution.py:111
  215.7 3.3 %collective-permute-done.12 = bf16[96,2304]{1,0:T(8,128)(2,1)S(1)} collective-permute-done((bf16[96,2304]{1,0:T(8,128)(2,1)S(1)}, bf16[96,2304]{1,0:T(8,128)(2,1)S(1)}, u32[]{:S(2)}, u32[]{:S(2)}) %collective-permute-start.12) | collective-permute-done | bytes 442400 | tf_op jit(solution)/shard_map/ppermute | solution.py:10
  219.0 3.5 %collective-permute-done.8 = bf16[96,2304]{1,0:T(8,128)(2,1)S(1)} collective-permute-done((bf16[96,2304]{1,0:T(8,128)(2,1)S(1)}, bf16[96,2304]{1,0:T(8,128)(2,1)S(1)}, u32[]{:S(2)}, u32[]{:S(2)}) %collective-permute-start.8) | collective-permute-done | bytes 442400 | tf_op jit(solution)/shard_map/ppermute | solution.py:10
  222.6 1.5 fusion.8
  224.1 1.3 convert_element_type.89
  225.4 9.8 %all-to-all-done.5 = bf16[4,576,512]{2,1,0:T(8,128)(2,1)S(1)} async-done(((bf16[4,576,512]{2,1,0:T(8,128)(2,1)}), bf16[4,576,512]{2,1,0:T(8,128)(2,1)S(1)}, u32[]{:S(2)}, u32[]{:S(2)}) %all-to-all-start.5) | async-done | bytes 2359328 | tf_op jit(solution)/shard_map/all_to_all | solution.py:127
  235.2 3.9 %all-to-all-start.6 = ((bf16[32,6,2304]{2,1,0:T(8,128)(2,1)}), bf16[32,6,2304]{2,1,0:T(8,128)(2,1)S(1)}, u32[]{:S(2)}, u32[]{:S(2)}) async-start(bf16[32,6,2304]{2,1,0:T(8,128)(2,1)} %convert_element_type.89), calls=%async_computation.6 | async-start | bytes 2359296 | tf_op jit(solution)/shard_map/all_to_all | solution.py:120
  239.1 0.7 convert_bitcast_fusion
  239.8 2.9 %copy.71 = f32[4,72,8,512]{3,2,0,1:T(8,128)} copy(f32[4,72,8,512]{3,2,1,0:T(8,128)S(1)} %convert_bitcast_fusion) | data formatting | bytes 9437184 | tf_op jit(solution)/shard_map/transpose | solution.py:129
  242.7 24.0 %all-to-all-done.6 = bf16[32,6,2304]{2,1,0:T(8,128)(2,1)S(1)} async-done(((bf16[32,6,2304]{2,1,0:T(8,128)(2,1)}), bf16[32,6,2304]{2,1,0:T(8,128)(2,1)S(1)}, u32[]{:S(2)}, u32[]{:S(2)}) %all-to-all-start.6) | async-done | bytes 884768 | tf_op jit(solution)/shard_map/all_to_all | solution.py:120
  266.8 0.9 convert_reduce_fusion
  (47 shorter events, 1.2 us)
Async XLA Ops:
  18.4 21.1 %collective-permute-start = (bf16[192,2304]{1,0:T(8,128)(2,1)}, bf16[192,2304]{1,0:T(8,128)(2,1)}, u32[]{:S(2)}, u32[]{:S(2)}) collective-permute-start(bf16[192,2304]{1,0:T(8,128)(2,1)} %bitcast.1), channel_id=1, source_target_pairs={{0,16},{8,24},{16,32},{24,40},{32,48},{40,56},{48,0},{56,8},{1,17}... | collective-permute-start | bytes 2654216 | tf_op jit(solution)/shard_map/ppermute | solution.py:10
  20.2 20.8 %collective-permute-start.1 = (bf16[192,2304]{1,0:T(8,128)(2,1)}, bf16[192,2304]{1,0:T(8,128)(2,1)}, u32[]{:S(2)}, u32[]{:S(2)}) collective-permute-start(bf16[192,2304]{1,0:T(8,128)(2,1)} %bitcast.1), channel_id=1, source_target_pairs={{0,48},{8,56},{16,0},{24,8},{32,16},{40,24},{48,32},{56,40},{1,49}... | collective-permute-start | bytes 2654216 | tf_op jit(solution)/shard_map/ppermute | solution.py:10
  40.6 10.2 %collective-permute-start.2 = (bf16[96,2304]{1,0:T(8,128)(2,1)S(1)}, bf16[96,2304]{1,0:T(8,128)(2,1)S(1)}, u32[]{:S(2)}, u32[]{:S(2)}) collective-permute-start(bf16[96,2304]{1,0:T(8,128)(2,1)S(1)} %slice.76), channel_id=1, source_target_pairs={{0,16},{8,24},{16,32},{24,40},{32,48},{40,56},{48,0},{56,8},{1,17}... | collective-permute-start | bytes 1327112 | tf_op jit(solution)/shard_map/ppermute | solution.py:10
  42.1 8.9 %collective-permute-start.3 = (bf16[96,2304]{1,0:T(8,128)(2,1)S(1)}, bf16[96,2304]{1,0:T(8,128)(2,1)S(1)}, u32[]{:S(2)}, u32[]{:S(2)}) collective-permute-start(bf16[96,2304]{1,0:T(8,128)(2,1)S(1)} %slice.77), channel_id=1, source_target_pairs={{0,48},{8,56},{16,0},{24,8},{32,16},{40,24},{48,32},{56,40},{1,49}... | collective-permute-start | bytes 1327112 | tf_op jit(solution)/shard_map/ppermute | solution.py:10
  51.1 27.6 %collective-permute-start.4 = (bf16[4,4,48,2304]{3,2,1,0:T(8,128)(2,1)S(1)}, bf16[4,4,48,2304]{3,2,1,0:T(8,128)(2,1)}, u32[]{:S(2)}, u32[]{:S(2)}) collective-permute-start(bf16[4,4,48,2304]{3,2,1,0:T(8,128)(2,1)S(1)} %constant_dynamic-update-slice_fusion), channel_id=1, source_target_pairs={{0,8},{8,0},{16,24},{24,16},{32,40},{40,32},{48,56},{56,48},{1,9},... | collective-permute-start | bytes 10616840 | tf_op jit(solution)/shard_map/ppermute | solution.py:14
  64.8 33.8 %all-to-all-start.1 = ((bf16[4,576,512]{2,1,0:T(8,128)(2,1)}), bf16[4,576,512]{2,1,0:T(8,128)(2,1)}, u32[]{:S(2)}, u32[]{:S(2)}) async-start(bf16[4,576,512]{2,1,0:T(8,128)(2,1)} %copy.48), calls=%async_computation.1 | async-start | bytes 4718592 | tf_op jit(solution)/shard_map/all_to_all | solution.py:76
  105.4 19.4 %copy-start.1 = (f32[1536,512]{1,0:T(8,128)}, f32[1536,512]{1,0:T(8,128)S(1)}, u32[]{:S(2)}) copy-start(f32[1536,512]{1,0:T(8,128)S(1)} %get-tuple-element.29) | copy-start | bytes 9437188
  105.5 28.8 %copy-start = (bf16[384,2048]{1,0:T(8,128)(2,1)S(1)}, bf16[384,2048]{1,0:T(8,128)(2,1)}, u32[]{:S(2)}) copy-start(bf16[384,2048]{1,0:T(8,128)(2,1)} %param.5) | copy-start | bytes 4718596
  125.6 18.0 %all-to-all-start.3 = ((f32[8,4,1536]{2,1,0:T(4,128)}), f32[8,4,1536]{2,1,0:T(4,128)S(1)}, u32[]{:S(2)}, u32[]{:S(2)}) async-start(f32[8,4,1536]{2,1,0:T(4,128)} %broadcast_in_dim.20), calls=%async_computation.3 | async-start | bytes 393216 | tf_op jit(solution)/shard_map/all_to_all | solution.py:46
  135.6 31.3 %copy-start.2 = (f32[1536,512]{1,0:T(8,128)S(1)}, f32[1536,512]{1,0:T(8,128)}, u32[]{:S(2)}) copy-start(f32[1536,512]{1,0:T(8,128)} %copy-done.1) | copy-start | bytes 9437188
  143.7 23.3 %all-to-all-start.4 = ((bf16[4,384,512]{2,1,0:T(8,128)(2,1)}), bf16[4,384,512]{2,1,0:T(8,128)(2,1)}, u32[]{:S(2)}, u32[]{:S(2)}) async-start(bf16[4,384,512]{2,1,0:T(8,128)(2,1)} %bitcast.120), calls=%async_computation.4 | async-start | bytes 3145728 | tf_op jit(solution)/shard_map/all_to_all | solution.py:79
  148.0 24.5 %collective-permute-start.6 = (bf16[2304,512]{1,0:T(8,128)(2,1)}, bf16[2304,512]{1,0:T(8,128)(2,1)}, u32[]{:S(2)}, u32[]{:S(2)}) collective-permute-start(bf16[2304,512]{1,0:T(8,128)(2,1)} %bitcast.11), channel_id=1, source_target_pairs={{0,8},{8,0},{16,24},{24,16},{32,40},{40,32},{48,56},{56,48},{1,9},... | collective-permute-start | bytes 7077896 | tf_op jit(solution)/shard_map/ppermute | solution.py:14
  169.5 4.8 %collective-permute-start.5 = (bf16[768,512]{1,0:T(8,128)(2,1)S(1)}, bf16[768,512]{1,0:T(8,128)(2,1)S(1)}, u32[]{:S(2)}, u32[]{:S(2)}) collective-permute-start(bf16[768,512]{1,0:T(8,128)(2,1)S(1)} %bitcast.130), channel_id=1, source_target_pairs={{0,8},{8,0},{16,24},{24,16},{32,40},{40,32},{48,56},{56,48},{1,9},... | collective-permute-start | bytes 2359304 | tf_op jit(solution)/shard_map/ppermute | solution.py:14
  172.5 10.6 %copy-start.4 = (bf16[4,4,1,48,512]{4,3,0,1,2:T(8,128)(2,1)}, bf16[4,4,1,48,512]{4,3,0,1,2:T(8,128)(2,1)S(1)}, u32[]{:S(2)}) copy-start(bf16[4,4,1,48,512]{4,3,0,1,2:T(8,128)(2,1)S(1)} %copy.55) | copy-start | bytes 2359300
  174.3 8.8 %copy-start.5 = (bf16[768,512]{1,0:T(8,128)(2,1)}, bf16[768,512]{1,0:T(8,128)(2,1)S(1)}, u32[]{:S(2)}) copy-start(bf16[768,512]{1,0:T(8,128)(2,1)S(1)} %collective-permute-done.5) | copy-start | bytes 2359300
  178.7 13.3 %copy-start.3 = (bf16[192,2304]{1,0:T(8,128)(2,1)}, bf16[192,2304]{1,0:T(8,128)(2,1)S(1)}, u32[]{:S(2)}) copy-start(bf16[192,2304]{1,0:T(8,128)(2,1)S(1)} %convolution_convert_fusion.2) | copy-start | bytes 2654212
  188.2 19.0 %collective-permute-start.11 = (bf16[96,2304]{1,0:T(8,128)(2,1)}, bf16[96,2304]{1,0:T(8,128)(2,1)}, u32[]{:S(2)}, u32[]{:S(2)}) collective-permute-start(bf16[96,2304]{1,0:T(8,128)(2,1)} %get-tuple-element.17), channel_id=1, source_target_pairs={{0,48},{8,56},{16,0},{24,8},{32,16},{40,24},{48,32},{56,40},{1,49}... | collective-permute-start | bytes 1327112 | tf_op jit(solution)/shard_map/ppermute | solution.py:10
  191.1 18.9 %collective-permute-start.7 = (bf16[96,2304]{1,0:T(8,128)(2,1)}, bf16[96,2304]{1,0:T(8,128)(2,1)}, u32[]{:S(2)}, u32[]{:S(2)}) collective-permute-start(bf16[96,2304]{1,0:T(8,128)(2,1)} %get-tuple-element.16), channel_id=1, source_target_pairs={{0,16},{8,24},{16,32},{24,40},{32,48},{40,56},{48,0},{56,8},{1,17}... | collective-permute-start | bytes 1327112 | tf_op jit(solution)/shard_map/ppermute | solution.py:10
  191.9 23.8 %collective-permute-start.10 = (bf16[96,2304]{1,0:T(8,128)(2,1)}, bf16[96,2304]{1,0:T(8,128)(2,1)}, u32[]{:S(2)}, u32[]{:S(2)}) collective-permute-start(bf16[96,2304]{1,0:T(8,128)(2,1)} %slice.73), channel_id=1, source_target_pairs={{0,16},{8,24},{16,32},{24,40},{32,48},{40,56},{48,0},{56,8},{1,17}... | collective-permute-start | bytes 1327112 | tf_op jit(solution)/shard_map/ppermute | solution.py:10
  192.8 23.0 %collective-permute-start.9 = (bf16[96,2304]{1,0:T(8,128)(2,1)}, bf16[96,2304]{1,0:T(8,128)(2,1)}, u32[]{:S(2)}, u32[]{:S(2)}) collective-permute-start(bf16[96,2304]{1,0:T(8,128)(2,1)} %slice.71), channel_id=1, source_target_pairs={{0,48},{8,56},{16,0},{24,8},{32,16},{40,24},{48,32},{56,40},{1,49}... | collective-permute-start | bytes 1327112 | tf_op jit(solution)/shard_map/ppermute | solution.py:10
  203.6 31.6 %all-to-all-start.5 = ((bf16[4,576,512]{2,1,0:T(8,128)(2,1)}), bf16[4,576,512]{2,1,0:T(8,128)(2,1)S(1)}, u32[]{:S(2)}, u32[]{:S(2)}) async-start(bf16[4,576,512]{2,1,0:T(8,128)(2,1)} %bitcast.125), calls=%async_computation.5 | async-start | bytes 4718592 | tf_op jit(solution)/shard_map/all_to_all | solution.py:127
  208.5 10.6 %collective-permute-start.12 = (bf16[96,2304]{1,0:T(8,128)(2,1)S(1)}, bf16[96,2304]{1,0:T(8,128)(2,1)S(1)}, u32[]{:S(2)}, u32[]{:S(2)}) collective-permute-start(bf16[96,2304]{1,0:T(8,128)(2,1)S(1)} %add_convert_fusion), channel_id=1, source_target_pairs={{0,48},{8,56},{16,0},{24,8},{32,16},{40,24},{48,32},{56,40},{1,49}... | collective-permute-start | bytes 1327112 | tf_op jit(solution)/shard_map/ppermute | solution.py:10
  211.1 11.5 %collective-permute-start.8 = (bf16[96,2304]{1,0:T(8,128)(2,1)S(1)}, bf16[96,2304]{1,0:T(8,128)(2,1)S(1)}, u32[]{:S(2)}, u32[]{:S(2)}) collective-permute-start(bf16[96,2304]{1,0:T(8,128)(2,1)S(1)} %add_convert_fusion.1), channel_id=1, source_target_pairs={{0,16},{8,24},{16,32},{24,40},{32,48},{40,56},{48,0},{56,8},{1,17}... | collective-permute-start | bytes 1327112 | tf_op jit(solution)/shard_map/ppermute | solution.py:10
  235.2 31.6 %all-to-all-start.6 = ((bf16[32,6,2304]{2,1,0:T(8,128)(2,1)}), bf16[32,6,2304]{2,1,0:T(8,128)(2,1)S(1)}, u32[]{:S(2)}, u32[]{:S(2)}) async-start(bf16[32,6,2304]{2,1,0:T(8,128)(2,1)} %convert_element_type.89), calls=%async_computation.6 | async-start | bytes 2359296 | tf_op jit(solution)/shard_map/all_to_all | solution.py:120
where the time goes:
time: 272 us; the launch traced here: 268 us
  waiting for transfers between devices  103 us (38%)
  starting transfers between devices  47.5 us (17%)
  local copies, waits for them, and re-layouts  35.9 us (13%)
  blocking collectives  34.4 us (13%)
  matrix products  32.1 us (12%)
  other arithmetic  13.3 us (5%)
    all_to_all x2, blocking collectives, spread(): lax.all_to_all(jnp.broadcast_to(x[None], (n, *x.shape)), axis, 0, 0, tile...  34.4 us
    ppermute x10, waiting for transfers between devices, shift_x(): return lax.ppermute(x, 'row', [(i, (i + 2 * s) % n) for i in range(n)])  27.4 us
    all_to_all x1, waiting for transfers between devices, local(): summed = lax.all_to_all(summed, ('layer', 'col'), 0, 0, tiled=True)  24 us
    dot_general x4, matrix products, part(): lax.dot_general(lines, tables, (((1,), (1,)), ((), ())), preferred_elemen...  17.1 us
    all_to_all x1, waiting for transfers between devices, local(): taught = lax.all_to_all(taught, 'layer', 0, 0, tiled=True)  16.3 us
    all_to_all x1, waiting for transfers between devices, local(): lax.all_to_all(table, 'layer', 0, 0, tiled=True).reshape(width, block)  15.8 us
    ppermute x10, starting transfers between devices, shift_x(): return lax.ppermute(x, 'row', [(i, (i + 2 * s) % n) for i in range(n)])  13.4 us
    dynamic_update_slice x6, local copies, waits for them, and re-layouts, put(): return lax.dynamic_update_slice_in_dim(buf, jnp.expand_dims(x, dim), k, dim)  9.88 us
  transfers between devices with their start and end apart: 18, of which 11 were waited for; matrix products, arithmetic and copies ran while one was open for 21% of the time, Pallas kernels for 0%

commit v1 on v0

v1 whole, which is shorter than its diff:
```python
import jax
import jax.numpy as jnp
from jax import lax
from jax.sharding import PartitionSpec as P

LOSS_SCALE = 256


def shift_y(x, s):
    n = lax.axis_size("layer")
    return lax.ppermute(x, "layer", [(i, (i + s) % n) for i in range(n)])


def shift_x(x, s):
    n = lax.axis_size("row")
    return lax.ppermute(x, "row", [(i, (i + 2 * s) % n) for i in range(n)])


def swap_core(x):
    n = lax.axis_size("row")
    return lax.ppermute(x, "row", [(i, i ^ 1) for i in range(n)])


def at(x, k, dim=0):
    return lax.dynamic_index_in_dim(x, k, dim, keepdims=False)


def put(buf, x, k, dim=0):
    return lax.dynamic_update_slice_in_dim(buf, jnp.expand_dims(x, dim), k, dim)


def ring_gather(block, shift):
    half = block.shape[0] // 2
    back = shift(block, 1)
    front = shift(block, -1)
    far = (shift(back[:half], 1), shift(front[half:], -1))
    return ((0, block), (3, back), (1, front), (2, jnp.concatenate(far)))


def ring_sum_far(far, shift):
    half = far.shape[0] // 2
    return shift(far[:half], 1), shift(far[half:], -1)


def ring_sum(own, ahead, behind, far, shift):
    right, left = far
    none = jnp.zeros_like(right)
    back = shift(ahead + jnp.concatenate([right, none]), 1)
    front = shift(behind + jnp.concatenate([none, left]), -1)
    f32 = jnp.float32
    return own.astype(f32) + back.astype(f32) + front.astype(f32)


def spread(x, axis):
    n = lax.axis_size(axis)
    return lax.all_to_all(jnp.broadcast_to(x[None], (n, *x.shape)), axis, 0, 0, tiled=True)


def logsum(values, dim):
    top = jnp.max(values, axis=dim)
    return top + jnp.log(jnp.sum(jnp.exp(values - jnp.expand_dims(top, dim)), axis=dim))


def ordered(core, own, other):
    return jnp.where(core == 0, jnp.stack([own, other]), jnp.stack([other, own]))


def local(hidden, embedding, teacher):
    f32, bf16 = jnp.float32, jnp.bfloat16
    layers, cols = lax.axis_size("layer"), lax.axis_size("col")
    rows = lax.axis_size("row")
    xs = rows // 2
    y, row = lax.axis_index("layer"), lax.axis_index("row")
    x, core = row // 2, row % 2
    strip, width = hidden.shape
    quarter = embedding.shape[1]
    block = embedding.shape[0] // layers
    half = strip * xs * layers

    moved = [shift_y(hidden, k) for k in (1, 3, 2)]
    mine = jnp.zeros((layers, strip, width), bf16)
    for k, p in ((0, hidden), (3, moved[0]), (1, moved[1]), (2, moved[2])):
        mine = put(mine, p, (y + k) % layers)

    table = embedding.T
    table = jnp.stack([table[:, k * block : (k + 1) * block] for k in range(layers)])
    table = lax.all_to_all(table, "layer", 0, 0, tiled=True).reshape(width, block)

    taught = jnp.stack([teacher[:, k * block : (k + 1) * block] for k in range(layers)])
    taught = lax.all_to_all(taught, "layer", 0, 0, tiled=True)
    taught = taught.reshape(layers, xs, 2, strip, block)

    own = jnp.zeros((xs, layers * strip, width), bf16)
    pieces = ring_gather(mine.reshape(layers * strip, width), shift_x)
    for k, p in pieces:
        own = put(own, p, (x + k) % xs)
    own = own.reshape(half, width)
    other = swap_core(own)

    side = lambda c: at(taught, c, 2).swapaxes(0, 1).reshape(half, block).astype(f32)
    taught_own, taught_other = side(core), side(1 - core)
    logits_own = jnp.dot(own, table, preferred_element_type=f32)
    logits_other = jnp.dot(other, table, preferred_element_type=f32)
    lse = ordered(
        core,
        jnp.stack([logsum(logits_own, 1), logsum(taught_own, 1)]),
        jnp.stack([logsum(logits_other, 1), logsum(taught_other, 1)]),
    )
    lse = lse.reshape(2, 2, xs, layers, strip).transpose(3, 2, 0, 1, 4)
    got = lax.all_to_all(lse.reshape(layers * rows, 2 * strip), ("layer", "row"), 0, 0, tiled=True)
    lse = logsum(got, 0)
    got = spread(lse, ("layer", "row", "col"))
    lse = logsum(got.reshape(layers * rows, cols, 2 * strip), 1)
    lse = lse.reshape(layers, xs, 2, 2, strip).transpose(2, 3, 1, 0, 4).reshape(2, 2, half)

    def gradient(logits, taught, lse):
        prob_s = jnp.exp(logits - lse[0][:, None])
        prob_t = jnp.exp(taught - lse[1][:, None])
        return ((prob_s - prob_t) * LOSS_SCALE).astype(bf16)

    grads_other = gradient(logits_other, taught_other, at(lse, 1 - core))
    crossed = swap_core(grads_other)
    grads_own = gradient(logits_own, taught_own, at(lse, core))
    other_table = swap_core(table)

    both = jnp.concatenate([grads_own, crossed], axis=1).reshape(xs, layers * strip, 2 * block)
    tables = jnp.concatenate([table, other_table], axis=1)

    def part(k):
        lines = at(both, (x + k) % xs)
        return lax.dot_general(
            lines, tables, (((1,), (1,)), ((), ())), preferred_element_type=f32
        ).astype(bf16)

    grads = jnp.concatenate([grads_own, grads_other])
    states = jnp.concatenate([own, other])
    far = ring_sum_far(part(2), shift_x)
    grad_table = lax.dot_general(
        states, grads, (((0,), (0,)), ((), ())), preferred_element_type=f32
    ).astype(bf16)
    both, grad_table = lax.optimization_barrier((both, grad_table))
    grad_table = grad_table.reshape(layers, quarter, block)
    grad_table = lax.all_to_all(grad_table, "layer", 0, 0, tiled=True)
    grad_table = jnp.concatenate([grad_table[k].astype(f32) for k in range(layers)], axis=1)

    near = part(1), part(3)
    both, near = lax.optimization_barrier((both, near))
    summed = ring_sum(lax.optimization_barrier(part(0)), *near, far, shift_x).astype(bf16)
    summed = summed.reshape(layers, strip, width)
    summed = lax.all_to_all(summed, "layer", 0, 0, tiled=True)
    summed = jnp.sum(summed.astype(f32), axis=0).astype(bf16)
    summed = summed.reshape(cols, strip // cols, width)
    summed = lax.all_to_all(summed, "col", 0, 0, tiled=True)
    grad_hidden = jnp.sum(summed.astype(f32), axis=0)
    return grad_table.T, grad_hidden


def solution(mesh):
    placed = (P(("layer", "row"), None), P(("row", "col"), "layer"), P("layer", ("row", "col")))
    return jax.shard_map(
        local,
        mesh=mesh,
        in_specs=placed,
        out_specs=(P(("row", "col"), "layer"), P(("layer", "row", "col"), None)),
        check_vma=False,
    )
```

time: 272 us -> 262 us (0.963)
  blocking collectives: 34.4 us -> 14.2 us
  waiting for transfers between devices: 103 us -> 120 us
  local copies, waits for them, and re-layouts: 35.9 us -> 19.9 us
  starting transfers between devices: 47.5 us -> 52.6 us
    all_to_all x2 -> x1, blocking collectives: 34.4 us -> 14.2 us  [local(): summed = lax.all_to_all(summed, 'layer', 0, 0, tiled=True)]
    all_to_all x1, waiting for transfers between devices: 16.3 us -> 0.01 us  [local(): taught = lax.all_to_all(taught, 'layer', 0, 0, tiled=True)]
    ppermute x10 -> x8, waiting for transfers between devices: 27.4 us -> 43.1 us  [shift_x(): return lax.ppermute(x, 'row', [(i, (i + 2 * s) % n) for i in range(n)])]
    all_to_all x1, waiting for transfers between devices: 9.77 us -> 25.1 us  [local(): grad_table = lax.all_to_all(grad_table, 'layer', 0, 0, tiled=True)]
    all_to_all x1, waiting for transfers between devices: 15.8 us -> 27.6 us  [local(): lax.all_to_all(table, 'layer', 0, 0, tiled=True).reshape(width, block)]
    all_to_all x1 -> x2, waiting for transfers between devices: 24 us -> 13.8 us  [the longest x1 7 us: local(): lax.all_to_all(lse.reshape(layers * rows, 2 * strip), ('layer', 'row'), 0...]
    ppermute x0 -> x3, waiting for transfers between devices: none -> 8.22 us  [shift_y(): return lax.ppermute(x, 'layer', [(i, (i + s) % n) for i in range(n)])]
    reshape x2, local copies, waits for them, and re-layouts: 7.54 us -> 0.88 us  [the longest x1 0.78 us: local(): summed = summed.reshape(cols, strip // cols, width)]
  transfers between devices with their start and end apart: 18 -> 20, of which waited for: 11 -> 15; matrix products, arithmetic and copies ran while one was open for 21% -> 22% of each run, Pallas kernels for 0% -> 0%
where the time goes in v1:
time: 262 us; the launch traced here: 257 us
  waiting for transfers between devices  120 us (46%)
  starting transfers between devices  52.6 us (20%)
  matrix products  34.3 us (13%)
  local copies, waits for them, and re-layouts  19.9 us (8%)
  other arithmetic  15 us (6%)
  blocking collectives  14.2 us (5%)
    ppermute x8, waiting for transfers between devices, shift_x(): return lax.ppermute(x, 'row', [(i, (i + 2 * s) % n) for i in range(n)])  43.1 us
    all_to_all x1, waiting for transfers between devices, local(): lax.all_to_all(table, 'layer', 0, 0, tiled=True).reshape(width, block)  27.6 us
    all_to_all x1, waiting for transfers between devices, local(): grad_table = lax.all_to_all(grad_table, 'layer', 0, 0, tiled=True)  25.1 us
    dot_general x4, matrix products, part(): lax.dot_general(lines, tables, (((1,), (1,)), ((), ())), preferred_elemen...  16.2 us
    all_to_all x1, blocking collectives, local(): summed = lax.all_to_all(summed, 'layer', 0, 0, tiled=True)  14.2 us
    all_to_all x1, starting transfers between devices, spread(): lax.all_to_all(jnp.broadcast_to(x[None], (n, *x.shape)), axis, 0, 0, tile...  11 us
    ppermute x8, starting transfers between devices, shift_x(): return lax.ppermute(x, 'row', [(i, (i + 2 * s) % n) for i in range(n)])  9.63 us
    dot_general x1, matrix products, local(): lax.dot_general(states, grads, (((0,), (0,)), ((), ())), preferred_elemen...  8.45 us
  transfers between devices with their start and end apart: 20, of which 15 were waited for; matrix products, arithmetic and copies ran while one was open for 22% of the time, Pallas kernels for 0%

profile of v1, /device:TPU:1, one launch (start us, length us, event | category | flops | bytes accessed | tf_op | source)
XLA Modules:
  0.0 257.4 jit_solution(12888677648092499714)
XLA Ops:
  0.6 2.2 collective-permute-start
  2.8 1.5 collective-permute-start.1
  4.4 1.6 collective-permute-start.2
  6.0 1.0 bitcast_dynamic-update-slice_fusion.6
  7.0 0.8 collective-permute-done
  7.8 1.0 collective-permute-done.1
  8.9 6.4 %collective-permute-done.2 = bf16[48,2304]{1,0:T(8,128)(2,1)S(1)} collective-permute-done((bf16[48,2304]{1,0:T(8,128)(2,1)}, bf16[48,2304]{1,0:T(8,128)(2,1)S(1)}, u32[]{:S(2)}, u32[]{:S(2)}) %collective-permute-start.2) | collective-permute-done | bytes 221216 | tf_op jit(solution)/shard_map/ppermute | solution.py:11
  15.3 2.6 collective-permute-start.4
  18.0 1.4 pad_maximum_fusion.2
  19.3 3.6 %all-to-all-start.1 = ((bf16[4,384,512]{2,1,0:T(8,128)(2,1)}), bf16[4,384,512]{2,1,0:T(8,128)(2,1)S(1)}, u32[]{:S(2)}, u32[]{:S(2)}) async-start(bf16[4,384,512]{2,1,0:T(8,128)(2,1)} %pad_maximum_fusion.2), calls=%async_computation.1 | async-start | bytes 3145728 | tf_op jit(solution)/shard_map/all_to_all | solution.py:90
  23.0 2.0 broadcast_in_dim.40
  25.0 1.0 bitcast_dynamic-update-slice_fusion.2
  26.0 9.3 %collective-permute-done.4 = bf16[192,2304]{1,0:T(8,128)(2,1)S(1)} collective-permute-done((bf16[192,2304]{1,0:T(8,128)(2,1)S(1)}, bf16[192,2304]{1,0:T(8,128)(2,1)S(1)}, u32[]{:S(2)}, u32[]{:S(2)}) %collective-permute-start.4) | collective-permute-done | bytes 884768 | tf_op jit(solution)/shard_map/ppermute | solution.py:16
  35.3 3.5 %collective-permute-start.6 = (bf16[96,2304]{1,0:T(8,128)(2,1)S(1)}, bf16[96,2304]{1,0:T(8,128)(2,1)S(1)}, u32[]{:S(2)}, u32[]{:S(2)}) collective-permute-start(bf16[96,2304]{1,0:T(8,128)(2,1)S(1)} %slice.85), channel_id=1, source_target_pairs={{0,48},{8,56},{16,0},{24,8},{32,16},{40,24},{48,32},{56,40},{1,49}... | collective-permute-start | bytes 1327112 | tf_op jit(solution)/shard_map/ppermute | solution.py:16
  38.8 1.0 slice.84
  40.0 2.3 bitcast_dynamic-update-slice_fusion.1
  42.3 1.0 bitcast_dynamic-update-slice_fusion
  43.2 2.7 %collective-permute-done.6 = bf16[96,2304]{1,0:T(8,128)(2,1)S(1)} collective-permute-done((bf16[96,2304]{1,0:T(8,128)(2,1)S(1)}, bf16[96,2304]{1,0:T(8,128)(2,1)S(1)}, u32[]{:S(2)}, u32[]{:S(2)}) %collective-permute-start.6) | collective-permute-done | bytes 442400 | tf_op jit(solution)/shard_map/ppermute | solution.py:16
  46.0 4.3 %collective-permute-done.5 = bf16[96,2304]{1,0:T(8,128)(2,1)S(1)} collective-permute-done((bf16[96,2304]{1,0:T(8,128)(2,1)S(1)}, bf16[96,2304]{1,0:T(8,128)(2,1)S(1)}, u32[]{:S(2)}, u32[]{:S(2)}) %collective-permute-start.5) | collective-permute-done | bytes 442400 | tf_op jit(solution)/shard_map/ppermute | solution.py:16
  50.2 1.0 fusion.10
  51.2 3.5 %collective-permute-start.7 = (bf16[768,2304]{1,0:T(8,128)(2,1)}, bf16[768,2304]{1,0:T(8,128)(2,1)}, u32[]{:S(2)}, u32[]{:S(2)}) collective-permute-start(bf16[768,2304]{1,0:T(8,128)(2,1)} %bitcast.9), channel_id=1, source_target_pairs={{0,8},{8,0},{16,24},{24,16},{32,40},{40,32},{48,56},{56,48},{1,9},... | collective-permute-start | bytes 10616840 | tf_op jit(solution)/shard_map/ppermute | solution.py:21
  54.9 1.7 pad_maximum_fusion.1
  56.6 4.7 %all-to-all-start = ((bf16[4,576,512]{2,1,0:T(8,128)(2,1)}), bf16[4,576,512]{2,1,0:T(8,128)(2,1)}, u32[]{:S(2)}, u32[]{:S(2)}) async-start(bf16[4,576,512]{2,1,0:T(8,128)(2,1)} %pad_maximum_fusion.1), calls=%async_computation | async-start | bytes 4718592 | tf_op jit(solution)/shard_map/all_to_all | solution.py:87
  61.9 0.9 exponential_reduce_fusion
  62.8 27.6 %all-to-all-done = bf16[4,576,512]{2,1,0:T(8,128)(2,1)} async-done(((bf16[4,576,512]{2,1,0:T(8,128)(2,1)}), bf16[4,576,512]{2,1,0:T(8,128)(2,1)}, u32[]{:S(2)}, u32[]{:S(2)}) %all-to-all-start) | async-done | bytes 2359328 | tf_op jit(solution)/shard_map/all_to_all | solution.py:87
  90.4 4.8 %fusion.37 = (f32[768]{0:T(1024)S(1)}, f32[768,512]{0,1:T(8,128)S(1)}) fusion(bf16[768,2304]{1,0:T(8,128)(2,1)} %bitcast.9, bf16[2304,512]{1,0:T(8,128)(2,1)} %bitcast.15), kind=kOutput, calls=%fused_computation.92 | convolution fusion | flops 1812331776 | bytes 7474176 | tf_op jit(solution)/shard_map/dot_general | solution.py:102
  95.6 4.8 %fusion.36 = (f32[768]{0:T(1024)S(1)}, f32[768,512]{0,1:T(8,128)S(1)}) fusion(bf16[768,2304]{1,0:T(8,128)(2,1)} %collective-permute-done.7, bf16[2304,512]{1,0:T(8,128)(2,1)} %bitcast.15), kind=kOutput, calls=%fused_computation.91 | convolution fusion | flops 1812331776 | bytes 7474176 | tf_op jit(solution)/shard_map/dot_general | solution.py:103
  100.4 1.2 copy-done
  102.0 0.7 all_to_all.29
  102.7 4.3 %all-to-all-start.2 = ((f32[32,1,96]{2,1,0:T(1,128)}), f32[32,1,96]{2,1,0:T(1,128)S(1)}, u32[]{:S(2)}, u32[]{:S(2)}) async-start(f32[32,1,96]{2,1,0:T(1,128)} %bitcast.30), calls=%async_computation.2 | async-start | bytes 32768 | tf_op jit(solution)/shard_map/all_to_all | solution.py:110
  107.1 7.0 %all-to-all-done.2 = f32[32,1,96]{2,1,0:T(1,128)S(1)} async-done(((f32[32,1,96]{2,1,0:T(1,128)}), f32[32,1,96]{2,1,0:T(1,128)S(1)}, u32[]{:S(2)}, u32[]{:S(2)}) %all-to-all-start.2) | async-done | bytes 12320 | tf_op jit(solution)/shard_map/all_to_all | solution.py:110
  114.2 0.7 broadcast_in_dim.49
  114.9 11.0 %all-to-all-start.3 = ((f32[256,1,96]{2,1,0:T(1,128)}), f32[256,1,96]{2,1,0:T(1,128)S(1)}, u32[]{:S(2)}, u32[]{:S(2)}) async-start(f32[256,1,96]{2,1,0:T(1,128)} %broadcast_in_dim.49), calls=%async_computation.3 | async-start | bytes 262144 | tf_op jit(solution)/shard_map/all_to_all | solution.py:56
  125.9 2.2 fusion.11
  128.1 3.0 %copy.43 = f32[768,512]{0,1:T(8,128)} copy(f32[768,512]{1,0:T(8,128)} %bitcast.111) | data formatting | bytes 3145728 | tf_op jit(solution)/shard_map/convert_element_type | solution.py:100
  131.1 3.2 %copy.42 = f32[768,512]{0,1:T(8,128)} copy(f32[768,512]{1,0:T(8,128)} %bitcast.110) | data formatting | bytes 3145728 | tf_op jit(solution)/shard_map/convert_element_type | solution.py:100
  134.3 2.1 collective-permute-start.9
  136.4 2.5 all-to-all-done.3
  139.3 2.0 multiply_convert_fusion
  141.3 0.8 collective-permute-start.8
  142.2 0.5 multiply_convert_fusion.1
  142.6 8.5 %fusion.4 = bf16[2304,512]{1,0:T(8,128)(2,1)} fusion(bf16[768,2304]{1,0:T(8,128)(2,1)} %collective-permute-done.7, bf16[768,2304]{1,0:T(8,128)(2,1)} %bitcast.9, bf16[768,512]{0,1:T(8,128)(2,1)S(1)} %multiply_convert_fusion, bf16[768,512]{0,1:T(8,128)(2,1)S(1)} %multiply_convert_fusion.1), kind=kOutput, calls=%fused_computation.6 | convolution fusion | flops 3642359808 | bytes 11010048 | tf_op jit(solution)/shard_map/dot_general | solution.py:138
  151.2 0.8 copy.44
  152.0 4.1 %convolution_convert_fusion = bf16[192,2304]{1,0:T(8,128)(2,1)S(1)} fusion(bf16[4,192,1024]{2,1,0:T(8,128)(2,1)S(1)} %bitcast.118, s32[]{:T(128)S(6)} %select_n.115, bf16[2304,512]{1,0:T(8,128)(2,1)} %collective-permute-done.9, bf16[2304,512]{1,0:T(8,128)(2,1)} %bitcast.15), kind=kOutput, calls=%fused_computation.7 | convolution fusion | flops 915849216 | bytes 5996548 | tf_op jit(solution)/shard_map/dot_general | solution.py:131
  156.1 0.5 collective-permute-start.12
  156.6 4.1 %convolution_convert_fusion.3 = bf16[192,2304]{1,0:T(8,128)(2,1)S(1)} fusion(bf16[4,192,1024]{2,1,0:T(8,128)(2,1)S(1)} %bitcast.119, s32[]{:T(128)S(6)} %select_n.113, bf16[2304,512]{1,0:T(8,128)(2,1)} %collective-permute-done.9, bf16[2304,512]{1,0:T(8,128)(2,1)} %bitcast.15), kind=kOutput, calls=%fused_computation.10 | convolution fusion | flops 915849216 | bytes 5996548 | tf_op jit(solution)/shard_map/dot_general | solution.py:131
  160.7 4.1 %convolution_convert_fusion.2 = bf16[192,2304]{1,0:T(8,128)(2,1)S(1)} fusion(bf16[4,192,1024]{2,1,0:T(8,128)(2,1)S(1)} %bitcast.120, s32[]{:T(128)S(6)} %select_n.111, bf16[2304,512]{1,0:T(8,128)(2,1)} %collective-permute-done.9, bf16[2304,512]{1,0:T(8,128)(2,1)} %bitcast.15), kind=kOutput, calls=%fused_computation.9 | convolution fusion | flops 915849216 | bytes 5996548 | tf_op jit(solution)/shard_map/dot_general | solution.py:131
  164.7 1.1 collective-permute-start.10
  165.8 2.0 collective-permute-done.12
  168.0 1.5 collective-permute-start.13
  169.5 7.7 %collective-permute-done.10 = bf16[96,2304]{1,0:T(8,128)(2,1)S(1)} collective-permute-done((bf16[96,2304]{1,0:T(8,128)(2,1)S(1)}, bf16[96,2304]{1,0:T(8,128)(2,1)S(1)}, u32[]{:S(2)}, u32[]{:S(2)}) %collective-permute-start.10) | collective-permute-done | bytes 442400 | tf_op jit(solution)/shard_map/ppermute | solution.py:16
  177.3 0.4 collective-permute-start.11
  177.7 4.1 %convolution_convert_fusion.1 = bf16[192,2304]{1,0:T(8,128)(2,1)S(1)} fusion(bf16[4,192,1024]{2,1,0:T(8,128)(2,1)S(1)} %bitcast.121, s32[]{:T(128)S(6)} %select_n.109, bf16[2304,512]{1,0:T(8,128)(2,1)} %collective-permute-done.9, bf16[2304,512]{1,0:T(8,128)(2,1)} %bitcast.15), kind=kOutput, calls=%fused_computation.8 | convolution fusion | flops 915849216 | bytes 5996548 | tf_op jit(solution)/shard_map/dot_general | solution.py:131
  181.8 6.6 %collective-permute-done.13 = bf16[192,2304]{1,0:T(8,128)(2,1)S(1)} collective-permute-done((bf16[192,2304]{1,0:T(8,128)(2,1)S(1)}, bf16[192,2304]{1,0:T(8,128)(2,1)S(1)}, u32[]{:S(2)}, u32[]{:S(2)}) %collective-permute-start.13) | collective-permute-done | bytes 884768 | tf_op jit(solution)/shard_map/ppermute | solution.py:16
  188.4 10.3 %collective-permute-done.11 = bf16[192,2304]{1,0:T(8,128)(2,1)S(1)} collective-permute-done((bf16[192,2304]{1,0:T(8,128)(2,1)S(1)}, bf16[192,2304]{1,0:T(8,128)(2,1)S(1)}, u32[]{:S(2)}, u32[]{:S(2)}) %collective-permute-start.11) | collective-permute-done | bytes 884768 | tf_op jit(solution)/shard_map/ppermute | solution.py:16
  198.7 0.3 add_convert_fusion
  199.0 14.2 %all_to_all.43 = bf16[4,48,2304]{2,1,0:T(8,128)(2,1)S(1)} all-to-all(bf16[4,48,2304]{2,1,0:T(8,128)(2,1)S(1)} %bitcast.112), channel_id=1, replica_groups=mesh['layer'=4,'row'=8,'col'=8] {'layer'}, dimensions={0} | all-to-all | bytes 1769472 | tf_op jit(solution)/shard_map/all_to_all | solution.py:150
  213.3 3.6 %all-to-all-start.4 = ((bf16[4,576,512]{2,1,0:T(8,128)(2,1)}), bf16[4,576,512]{2,1,0:T(8,128)(2,1)S(1)}, u32[]{:S(2)}, u32[]{:S(2)}) async-start(bf16[4,576,512]{2,1,0:T(8,128)(2,1)} %bitcast.117), calls=%async_computation.4 | async-start | bytes 4718592 | tf_op jit(solution)/shard_map/all_to_all | solution.py:143
  217.1 0.8 reshape.231
  217.8 25.1 %all-to-all-done.4 = bf16[4,576,512]{2,1,0:T(8,128)(2,1)S(1)} async-done(((bf16[4,576,512]{2,1,0:T(8,128)(2,1)}), bf16[4,576,512]{2,1,0:T(8,128)(2,1)S(1)}, u32[]{:S(2)}, u32[]{:S(2)}) %all-to-all-start.4) | async-done | bytes 2359328 | tf_op jit(solution)/shard_map/all_to_all | solution.py:143
  242.9 4.0 %all-to-all-start.6 = ((bf16[8,6,2304]{2,1,0:T(8,128)(2,1)}), bf16[8,6,2304]{2,1,0:T(8,128)(2,1)S(1)}, u32[]{:S(2)}, u32[]{:S(2)}) async-start(bf16[8,6,2304]{2,1,0:T(8,128)(2,1)} %reshape.231), calls=%async_computation.6 | async-start | bytes 589824 | tf_op jit(solution)/shard_map/all_to_all | solution.py:153
  247.1 2.8 %convert_bitcast_fusion = f32[2048,576]{0,1:T(8,128)} fusion(bf16[576,512]{1,0:T(8,128)(2,1)S(1)} %get-tuple-element.17, bf16[576,512]{1,0:T(8,128)(2,1)S(1)} %get-tuple-element.18, bf16[576,512]{1,0:T(8,128)(2,1)S(1)} %get-tuple-element.19, bf16[576,512]{1,0:T(8,128)(2,1)S(1)} %get-tuple-element.16), kind=kLoop, calls=%fused_computation.5 | loop fusion | flops 9437184 | bytes 7077888 | tf_op jit(solution)/shard_map/transpose | solution.py:155
  249.9 6.8 %all-to-all-done.6 = bf16[8,6,2304]{2,1,0:T(8,128)(2,1)S(1)} async-done(((bf16[8,6,2304]{2,1,0:T(8,128)(2,1)}), bf16[8,6,2304]{2,1,0:T(8,128)(2,1)S(1)}, u32[]{:S(2)}, u32[]{:S(2)}) %all-to-all-start.6) | async-done | bytes 221216 | tf_op jit(solution)/shard_map/all_to_all | solution.py:153
  256.7 0.7 convert_reduce_fusion
  (54 shorter events, 3.0 us)
Async XLA Ops:
  0.6 17.2 %copy-start.4 = (bf16[384,2048]{1,0:T(8,128)(2,1)S(1)}, bf16[384,2048]{1,0:T(8,128)(2,1)}, u32[]{:S(2)}) copy-start(bf16[384,2048]{1,0:T(8,128)(2,1)} %param.5) | copy-start | bytes 4718596
  0.6 7.2 %collective-permute-start = (bf16[48,2304]{1,0:T(8,128)(2,1)}, bf16[48,2304]{1,0:T(8,128)(2,1)S(1)}, u32[]{:S(2)}, u32[]{:S(2)}) collective-permute-start(bf16[48,2304]{1,0:T(8,128)(2,1)} %param.3), channel_id=1, source_target_pairs={{0,64},{64,128},{128,192},{192,0},{1,65},{65,129},{129,193},{193,1... | collective-permute-start | bytes 663560 | tf_op jit(solution)/shard_map/ppermute | solution.py:11
  2.8 6.0 %collective-permute-start.1 = (bf16[48,2304]{1,0:T(8,128)(2,1)}, bf16[48,2304]{1,0:T(8,128)(2,1)S(1)}, u32[]{:S(2)}, u32[]{:S(2)}) collective-permute-start(bf16[48,2304]{1,0:T(8,128)(2,1)} %param.3), channel_id=1, source_target_pairs={{0,192},{64,0},{128,64},{192,128},{1,193},{65,1},{129,65},{193,129... | collective-permute-start | bytes 663560 | tf_op jit(solution)/shard_map/ppermute | solution.py:11
  4.4 10.9 %collective-permute-start.2 = (bf16[48,2304]{1,0:T(8,128)(2,1)}, bf16[48,2304]{1,0:T(8,128)(2,1)S(1)}, u32[]{:S(2)}, u32[]{:S(2)}) collective-permute-start(bf16[48,2304]{1,0:T(8,128)(2,1)} %param.3), channel_id=1, source_target_pairs={{0,128},{64,192},{128,0},{192,64},{1,129},{65,193},{129,1},{193,65... | collective-permute-start | bytes 663560 | tf_op jit(solution)/shard_map/ppermute | solution.py:11
  15.3 20.0 %collective-permute-start.4 = (bf16[192,2304]{1,0:T(8,128)(2,1)S(1)}, bf16[192,2304]{1,0:T(8,128)(2,1)S(1)}, u32[]{:S(2)}, u32[]{:S(2)}) collective-permute-start(bf16[192,2304]{1,0:T(8,128)(2,1)S(1)} %bitcast.113), channel_id=1, source_target_pairs={{0,48},{8,56},{16,0},{24,8},{32,16},{40,24},{48,32},{56,40},{1,49}... | collective-permute-start | bytes 2654216 | tf_op jit(solution)/shard_map/ppermute | solution.py:16
  17.8 21.0 %collective-permute-start.3 = (bf16[192,2304]{1,0:T(8,128)(2,1)S(1)}, bf16[192,2304]{1,0:T(8,128)(2,1)}, u32[]{:S(2)}, u32[]{:S(2)}) collective-permute-start(bf16[192,2304]{1,0:T(8,128)(2,1)S(1)} %bitcast.114), channel_id=1, source_target_pairs={{0,16},{8,24},{16,32},{24,40},{32,48},{40,56},{48,0},{56,8},{1,17}... | collective-permute-start | bytes 2654216 | tf_op jit(solution)/shard_map/ppermute | solution.py:16
  19.3 37.3 %all-to-all-start.1 = ((bf16[4,384,512]{2,1,0:T(8,128)(2,1)}), bf16[4,384,512]{2,1,0:T(8,128)(2,1)S(1)}, u32[]{:S(2)}, u32[]{:S(2)}) async-start(bf16[4,384,512]{2,1,0:T(8,128)(2,1)} %pad_maximum_fusion.2), calls=%async_computation.1 | async-start | bytes 3145728 | tf_op jit(solution)/shard_map/all_to_all | solution.py:90
  35.3 10.6 %collective-permute-start.6 = (bf16[96,2304]{1,0:T(8,128)(2,1)S(1)}, bf16[96,2304]{1,0:T(8,128)(2,1)S(1)}, u32[]{:S(2)}, u32[]{:S(2)}) collective-permute-start(bf16[96,2304]{1,0:T(8,128)(2,1)S(1)} %slice.85), channel_id=1, source_target_pairs={{0,48},{8,56},{16,0},{24,8},{32,16},{40,24},{48,32},{56,40},{1,49}... | collective-permute-start | bytes 1327112 | tf_op jit(solution)/shard_map/ppermute | solution.py:16
  39.9 14.9 %copy-start.3 = (bf16[2048,576]{0,1:T(8,128)(2,1)S(1)}, bf16[2048,576]{0,1:T(8,128)(2,1)}, u32[]{:S(2)}) copy-start(bf16[2048,576]{0,1:T(8,128)(2,1)} %param.4) | copy-start | bytes 7077892
  39.9 10.3 %collective-permute-start.5 = (bf16[96,2304]{1,0:T(8,128)(2,1)S(1)}, bf16[96,2304]{1,0:T(8,128)(2,1)S(1)}, u32[]{:S(2)}, u32[]{:S(2)}) collective-permute-start(bf16[96,2304]{1,0:T(8,128)(2,1)S(1)} %slice.84), channel_id=1, source_target_pairs={{0,16},{8,24},{16,32},{24,40},{32,48},{40,56},{48,0},{56,8},{1,17}... | collective-permute-start | bytes 1327112 | tf_op jit(solution)/shard_map/ppermute | solution.py:16
  51.2 44.4 %collective-permute-start.7 = (bf16[768,2304]{1,0:T(8,128)(2,1)}, bf16[768,2304]{1,0:T(8,128)(2,1)}, u32[]{:S(2)}, u32[]{:S(2)}) collective-permute-start(bf16[768,2304]{1,0:T(8,128)(2,1)} %bitcast.9), channel_id=1, source_target_pairs={{0,8},{8,0},{16,24},{24,16},{32,40},{40,32},{48,56},{56,48},{1,9},... | collective-permute-start | bytes 10616840 | tf_op jit(solution)/shard_map/ppermute | solution.py:21
  56.6 33.8 %all-to-all-start = ((bf16[4,576,512]{2,1,0:T(8,128)(2,1)}), bf16[4,576,512]{2,1,0:T(8,128)(2,1)}, u32[]{:S(2)}, u32[]{:S(2)}) async-start(bf16[4,576,512]{2,1,0:T(8,128)(2,1)} %pad_maximum_fusion.1), calls=%async_computation | async-start | bytes 4718592 | tf_op jit(solution)/shard_map/all_to_all | solution.py:87
  100.4 1.2 copy-start
  102.7 11.4 %all-to-all-start.2 = ((f32[32,1,96]{2,1,0:T(1,128)}), f32[32,1,96]{2,1,0:T(1,128)S(1)}, u32[]{:S(2)}, u32[]{:S(2)}) async-start(f32[32,1,96]{2,1,0:T(1,128)} %bitcast.30), calls=%async_computation.2 | async-start | bytes 32768 | tf_op jit(solution)/shard_map/all_to_all | solution.py:110
  114.9 24.0 %all-to-all-start.3 = ((f32[256,1,96]{2,1,0:T(1,128)}), f32[256,1,96]{2,1,0:T(1,128)S(1)}, u32[]{:S(2)}, u32[]{:S(2)}) async-start(f32[256,1,96]{2,1,0:T(1,128)} %broadcast_in_dim.49), calls=%async_computation.3 | async-start | bytes 262144 | tf_op jit(solution)/shard_map/all_to_all | solution.py:56
  131.1 8.3 %copy-start.1 = (f32[768,512]{0,1:T(8,128)S(1)}, f32[768,512]{0,1:T(8,128)}, u32[]{:S(2)}) copy-start(f32[768,512]{0,1:T(8,128)} %copy-done) | copy-start | bytes 4718596
  134.3 17.7 %collective-permute-start.9 = (bf16[2304,512]{1,0:T(8,128)(2,1)}, bf16[2304,512]{1,0:T(8,128)(2,1)}, u32[]{:S(2)}, u32[]{:S(2)}) collective-permute-start(bf16[2304,512]{1,0:T(8,128)(2,1)} %bitcast.15), channel_id=1, source_target_pairs={{0,8},{8,0},{16,24},{24,16},{32,40},{40,32},{48,56},{56,48},{1,9},... | collective-permute-start | bytes 7077896 | tf_op jit(solution)/shard_map/ppermute | solution.py:21
  139.3 2.9 %copy-start.2 = (f32[768,512]{0,1:T(8,128)S(1)}, f32[768,512]{0,1:T(8,128)}, u32[]{:S(2)}) copy-start(f32[768,512]{0,1:T(8,128)} %copy.42) | copy-start | bytes 4718596
  141.3 9.8 %collective-permute-start.8 = (bf16[768,512]{0,1:T(8,128)(2,1)S(1)}, bf16[768,512]{0,1:T(8,128)(2,1)S(1)}, u32[]{:S(2)}, u32[]{:S(2)}) collective-permute-start(bf16[768,512]{0,1:T(8,128)(2,1)S(1)} %multiply_convert_fusion), channel_id=1, source_target_pairs={{0,8},{8,0},{16,24},{24,16},{32,40},{40,32},{48,56},{56,48},{1,9},... | collective-permute-start | bytes 2359304 | tf_op jit(solution)/shard_map/ppermute | solution.py:21
  156.1 11.8 %collective-permute-start.12 = (bf16[96,2304]{1,0:T(8,128)(2,1)S(1)}, bf16[96,2304]{1,0:T(8,128)(2,1)S(1)}, u32[]{:S(2)}, u32[]{:S(2)}) collective-permute-start(bf16[96,2304]{1,0:T(8,128)(2,1)S(1)} %get-tuple-element.31), channel_id=1, source_target_pairs={{0,48},{8,56},{16,0},{24,8},{32,16},{40,24},{48,32},{56,40},{1,49}... | collective-permute-start | bytes 1327112 | tf_op jit(solution)/shard_map/ppermute | solution.py:16
  164.7 12.5 %collective-permute-start.10 = (bf16[96,2304]{1,0:T(8,128)(2,1)S(1)}, bf16[96,2304]{1,0:T(8,128)(2,1)S(1)}, u32[]{:S(2)}, u32[]{:S(2)}) collective-permute-start(bf16[96,2304]{1,0:T(8,128)(2,1)S(1)} %get-tuple-element.30), channel_id=1, source_target_pairs={{0,16},{8,24},{16,32},{24,40},{32,48},{40,56},{48,0},{56,8},{1,17}... | collective-permute-start | bytes 1327112 | tf_op jit(solution)/shard_map/ppermute | solution.py:16
  168.0 20.4 %collective-permute-start.13 = (bf16[192,2304]{1,0:T(8,128)(2,1)S(1)}, bf16[192,2304]{1,0:T(8,128)(2,1)S(1)}, u32[]{:S(2)}, u32[]{:S(2)}) collective-permute-start(bf16[192,2304]{1,0:T(8,128)(2,1)S(1)} %pad_add_fusion), channel_id=1, source_target_pairs={{0,48},{8,56},{16,0},{24,8},{32,16},{40,24},{48,32},{56,40},{1,49}... | collective-permute-start | bytes 2654216 | tf_op jit(solution)/shard_map/ppermute | solution.py:16
  177.3 21.4 %collective-permute-start.11 = (bf16[192,2304]{1,0:T(8,128)(2,1)S(1)}, bf16[192,2304]{1,0:T(8,128)(2,1)S(1)}, u32[]{:S(2)}, u32[]{:S(2)}) collective-permute-start(bf16[192,2304]{1,0:T(8,128)(2,1)S(1)} %pad_add_fusion.1), channel_id=1, source_target_pairs={{0,16},{8,24},{16,32},{24,40},{32,48},{40,56},{48,0},{56,8},{1,17}... | collective-permute-start | bytes 2654216 | tf_op jit(solution)/shard_map/ppermute | solution.py:16
  213.3 29.7 %all-to-all-start.4 = ((bf16[4,576,512]{2,1,0:T(8,128)(2,1)}), bf16[4,576,512]{2,1,0:T(8,128)(2,1)S(1)}, u32[]{:S(2)}, u32[]{:S(2)}) async-start(bf16[4,576,512]{2,1,0:T(8,128)(2,1)} %bitcast.117), calls=%async_computation.4 | async-start | bytes 4718592 | tf_op jit(solution)/shard_map/all_to_all | solution.py:143
  242.9 13.8 %all-to-all-start.6 = ((bf16[8,6,2304]{2,1,0:T(8,128)(2,1)}), bf16[8,6,2304]{2,1,0:T(8,128)(2,1)S(1)}, u32[]{:S(2)}, u32[]{:S(2)}) async-start(bf16[8,6,2304]{2,1,0:T(8,128)(2,1)} %reshape.231), calls=%async_computation.6 | async-start | bytes 589824 | tf_op jit(solution)/shard_map/all_to_all | solution.py:153

commit v2 on v1

--- a/solution.py
+++ b/solution.py
@@ -83,12 +83,11 @@
         mine = put(mine, p, (y + k) % layers)
 
     table = embedding.T
-    table = jnp.stack([table[:, k * block : (k + 1) * block] for k in range(layers)])
-    table = lax.all_to_all(table, "layer", 0, 0, tiled=True).reshape(width, block)
-
-    taught = jnp.stack([teacher[:, k * block : (k + 1) * block] for k in range(layers)])
-    taught = lax.all_to_all(taught, "layer", 0, 0, tiled=True)
-    taught = taught.reshape(layers, xs, 2, strip, block)
+    cut = lambda m, k: m[:, k * block : (k + 1) * block]
+    sent = [jnp.concatenate([cut(table, k), cut(teacher, k)]) for k in range(layers)]
+    sent = lax.all_to_all(jnp.stack(sent), "layer", 0, 0, tiled=True)
+    table = sent[:, :quarter].reshape(width, block)
+    taught = sent[:, quarter:].reshape(layers, xs, 2, strip, block)
 
     own = jnp.zeros((xs, layers * strip, width), bf16)
     pieces = ring_gather(mine.reshape(layers * strip, width), shift_x)
@@ -97,43 +96,40 @@
     own = own.reshape(half, width)
     other = swap_core(own)
 
-    side = lambda c: at(taught, c, 2).swapaxes(0, 1).reshape(half, block).astype(f32)
-    taught_own, taught_other = side(core), side(1 - core)
-    logits_own = jnp.dot(own, table, preferred_element_type=f32)
-    logits_other = jnp.dot(other, table, preferred_element_type=f32)
-    lse = ordered(
-        core,
-        jnp.stack([logsum(logits_own, 1), logsum(taught_own, 1)]),
-        jnp.stack([logsum(logits_other, 1), logsum(taught_other, 1)]),
-    )
-    lse = lse.reshape(2, 2, xs, layers, strip).transpose(3, 2, 0, 1, 4)
-    got = lax.all_to_all(lse.reshape(layers * rows, 2 * strip), ("layer", "row"), 0, 0, tiled=True)
-    lse = logsum(got, 0)
-    got = spread(lse, ("layer", "row", "col"))
-    lse = logsum(got.reshape(layers * rows, cols, 2 * strip), 1)
-    lse = lse.reshape(layers, xs, 2, 2, strip).transpose(2, 3, 1, 0, 4).reshape(2, 2, half)
+    states = jnp.concatenate([own, other])
+    logits = jnp.dot(states, table, preferred_element_type=f32)
+    lse_s = logsum(logits, 1)
+    lse_s = ordered(core, lse_s[:half], lse_s[half:])
+    lse_t = logsum(teacher.astype(f32), 1)
+    got = spread(jnp.concatenate([lse_s.reshape(2 * half), lse_t]), ("layer", "row"))
+    lse_s = logsum(got[:, : 2 * half], 0)
+    lse_t = logsum(got[:, 2 * half :].reshape(layers, rows, -1), 1)
+    got = spread(jnp.concatenate([lse_s, lse_t.reshape(2 * half)]), "col")
+    lse_s, lse_t = jnp.split(logsum(got, 0), 2)
+    lse_s = lse_s.reshape(2, half)
+    lse_t = lse_t.reshape(layers, xs, 2, strip).transpose(2, 1, 0, 3).reshape(2, half)
 
-    def gradient(logits, taught, lse):
-        prob_s = jnp.exp(logits - lse[0][:, None])
-        prob_t = jnp.exp(taught - lse[1][:, None])
+    def gradient(logits, c):
+        taught_c = at(taught, c, 2).swapaxes(0, 1).reshape(half, block).astype(f32)
+        prob_s = jnp.exp(logits - at(lse_s, c)[:, None])
+        prob_t = jnp.exp(taught_c - at(lse_t, c)[:, None])
         return ((prob_s - prob_t) * LOSS_SCALE).astype(bf16)
 
-    grads_other = gradient(logits_other, taught_other, at(lse, 1 - core))
+    grads_other = gradient(logits[half:], 1 - core)
     crossed = swap_core(grads_other)
-    grads_own = gradient(logits_own, taught_own, at(lse, core))
+    grads_own = gradient(logits[:half], core)
     other_table = swap_core(table)
 
     both = jnp.concatenate([grads_own, crossed], axis=1).reshape(xs, layers * strip, 2 * block)
     tables = jnp.concatenate([table, other_table], axis=1)
 
-    def part(k):
-        lines = at(both, (x + k) % xs)
+    def part(*ks):
+        lines = jnp.concatenate([at(both, (x + k) % xs) for k in ks])
         return lax.dot_general(
             lines, tables, (((1,), (1,)), ((), ())), preferred_element_type=f32
         ).astype(bf16)
 
     grads = jnp.concatenate([grads_own, grads_other])
-    states = jnp.concatenate([own, other])
     far = ring_sum_far(part(2), shift_x)
     grad_table = lax.dot_general(
         states, grads, (((0,), (0,)), ((), ())), preferred_element_type=f32
@@ -143,9 +139,8 @@
     grad_table = lax.all_to_all(grad_table, "layer", 0, 0, tiled=True)
     grad_table = jnp.concatenate([grad_table[k].astype(f32) for k in range(layers)], axis=1)
 
-    near = part(1), part(3)
-    both, near = lax.optimization_barrier((both, near))
-    summed = ring_sum(lax.optimization_barrier(part(0)), *near, far, shift_x).astype(bf16)
+    ahead, behind, here = jnp.split(lax.optimization_barrier(part(1, 3, 0)), 3)
+    summed = ring_sum(here, ahead, behind, far, shift_x).astype(bf16)
     summed = summed.reshape(layers, strip, width)
     summed = lax.all_to_all(summed, "layer", 0, 0, tiled=True)
     summed = jnp.sum(summed.astype(f32), axis=0).astype(bf16)

time: 262 us -> 275 us (1.050)
  waiting for transfers between devices: 120 us -> 139 us
  matrix products: 34.3 us -> 24.2 us
  local copies, waits for them, and re-layouts: 19.9 us -> 27.3 us
    all_to_all x3 -> x1, waiting for transfers between devices: 34.6 us -> 45 us  [local(): sent = lax.all_to_all(jnp.stack(sent), 'layer', 0, 0, tiled=True)]
    dot_general x4 -> x2, matrix products: 16.2 us -> 7.97 us  [part(): lax.dot_general(lines, tables, (((1,), (1,)), ((), ())), preferred_elemen...]
    all_to_all x3 -> x1, starting transfers between devices: 12.6 us -> 4.98 us  [local(): sent = lax.all_to_all(jnp.stack(sent), 'layer', 0, 0, tiled=True)]
    ppermute x8, waiting for transfers between devices: 43.1 us -> 48.8 us  [shift_x(): return lax.ppermute(x, 'row', [(i, (i + 2 * s) % n) for i in range(n)])]
    slice x1 -> x5, local copies, waits for them, and re-layouts: 0.04 us -> 4.83 us  [the longest x1 2.65 us: local(): taught = sent[:, quarter:].reshape(layers, xs, 2, strip, block)]
    convert_element_type x2 -> x4, local copies, waits for them, and re-layouts: 6.18 us -> 10.1 us  [gradient(): taught_c = at(taught, c, 2).swapaxes(0, 1).reshape(half, block).astype(f32)]
    all_to_all x1, starting transfers between devices: 3.99 us -> 7.26 us  [local(): summed = lax.all_to_all(summed, 'col', 0, 0, tiled=True)]
    all_to_all x1 -> x2, waiting for transfers between devices: 2.53 us -> 5.72 us  [spread(): lax.all_to_all(jnp.broadcast_to(x[None], (n, *x.shape)), axis, 0, 0, tile...]
  transfers between devices with their start and end apart: 20 -> 19, of which waited for: 15 -> 13; matrix products, arithmetic and copies ran while one was open for 22% -> 19% of each run, Pallas kernels for 0% -> 0%
where the time goes in v2:
time: 275 us; the launch traced here: 271 us
  waiting for transfers between devices  139 us (51%)
  starting transfers between devices  50.2 us (18%)
  local copies, waits for them, and re-layouts  27.3 us (10%)
  matrix products  24.2 us (9%)
  other arithmetic  15.1 us (5%)
  blocking collectives  13.5 us (5%)
    ppermute x8, waiting for transfers between devices, shift_x(): return lax.ppermute(x, 'row', [(i, (i + 2 * s) % n) for i in range(n)])  48.8 us
    all_to_all x1, waiting for transfers between devices, local(): sent = lax.all_to_all(jnp.stack(sent), 'layer', 0, 0, tiled=True)  45 us
    all_to_all x1, waiting for transfers between devices, local(): grad_table = lax.all_to_all(grad_table, 'layer', 0, 0, tiled=True)  25 us
    all_to_all x1, blocking collectives, local(): summed = lax.all_to_all(summed, 'layer', 0, 0, tiled=True)  13.5 us
    all_to_all x2, starting transfers between devices, spread(): lax.all_to_all(jnp.broadcast_to(x[None], (n, *x.shape)), axis, 0, 0, tile...  13.2 us
    ppermute x8, starting transfers between devices, shift_x(): return lax.ppermute(x, 'row', [(i, (i + 2 * s) % n) for i in range(n)])  10.8 us
    convert_element_type x4, local copies, waits for them, and re-layouts, gradient(): taught_c = at(taught, c, 2).swapaxes(0, 1).reshape(half, block).astype(f32)  10.1 us
    dot_general x1, matrix products, local(): lax.dot_general(states, grads, (((0,), (0,)), ((), ())), preferred_elemen...  8.39 us
  transfers between devices with their start and end apart: 19, of which 13 were waited for; matrix products, arithmetic and copies ran while one was open for 19% of the time, Pallas kernels for 0%

profile of v2, /device:TPU:1, one launch (start us, length us, event | category | flops | bytes accessed | tf_op | source)
XLA Modules:
  0.0 270.9 jit_solution(6665341809850264683)
XLA Ops:
  0.6 2.2 collective-permute-start
  2.8 1.5 collective-permute-start.1
  4.4 1.6 collective-permute-start.2
  6.0 1.0 bitcast_dynamic-update-slice_fusion.6
  7.1 0.7 collective-permute-done
  7.8 1.0 collective-permute-done.1
  8.9 6.4 %collective-permute-done.2 = bf16[48,2304]{1,0:T(8,128)(2,1)S(1)} collective-permute-done((bf16[48,2304]{1,0:T(8,128)(2,1)}, bf16[48,2304]{1,0:T(8,128)(2,1)S(1)}, u32[]{:S(2)}, u32[]{:S(2)}) %collective-permute-start.2) | collective-permute-done | bytes 221216 | tf_op jit(solution)/shard_map/ppermute | solution.py:11
  15.3 1.3 collective-permute-start.3
  16.6 1.5 collective-permute-start.4
  18.2 0.2 fusion.34
  18.4 2.1 broadcast_in_dim.22
  20.5 1.0 bitcast_dynamic-update-slice_fusion.2
  21.5 14.5 %collective-permute-done.4 = bf16[192,2304]{1,0:T(8,128)(2,1)S(1)} collective-permute-done((bf16[192,2304]{1,0:T(8,128)(2,1)S(1)}, bf16[192,2304]{1,0:T(8,128)(2,1)S(1)}, u32[]{:S(2)}, u32[]{:S(2)}) %collective-permute-start.4) | collective-permute-done | bytes 884768 | tf_op jit(solution)/shard_map/ppermute | solution.py:16
  36.0 2.8 %collective-permute-start.6 = (bf16[96,2304]{1,0:T(8,128)(2,1)S(1)}, bf16[96,2304]{1,0:T(8,128)(2,1)S(1)}, u32[]{:S(2)}, u32[]{:S(2)}) collective-permute-start(bf16[96,2304]{1,0:T(8,128)(2,1)S(1)} %slice.101), channel_id=1, source_target_pairs={{0,48},{8,56},{16,0},{24,8},{32,16},{40,24},{48,32},{56,40},{1,49}... | collective-permute-start | bytes 1327112 | tf_op jit(solution)/shard_map/ppermute | solution.py:16
  38.9 1.0 bitcast_dynamic-update-slice_fusion.1
  39.9 1.0 bitcast_dynamic-update-slice_fusion
  40.9 4.7 %collective-permute-done.6 = bf16[96,2304]{1,0:T(8,128)(2,1)S(1)} collective-permute-done((bf16[96,2304]{1,0:T(8,128)(2,1)S(1)}, bf16[96,2304]{1,0:T(8,128)(2,1)S(1)}, u32[]{:S(2)}, u32[]{:S(2)}) %collective-permute-start.6) | collective-permute-done | bytes 442400 | tf_op jit(solution)/shard_map/ppermute | solution.py:16
  45.6 3.2 %collective-permute-done.5 = bf16[96,2304]{1,0:T(8,128)(2,1)S(1)} collective-permute-done((bf16[96,2304]{1,0:T(8,128)(2,1)S(1)}, bf16[96,2304]{1,0:T(8,128)(2,1)S(1)}, u32[]{:S(2)}, u32[]{:S(2)}) %collective-permute-start.5) | collective-permute-done | bytes 442400 | tf_op jit(solution)/shard_map/ppermute | solution.py:16
  48.9 1.0 fusion.19
  49.8 3.8 %collective-permute-start.7 = (bf16[768,2304]{1,0:T(8,128)(2,1)}, bf16[768,2304]{1,0:T(8,128)(2,1)}, u32[]{:S(2)}, u32[]{:S(2)}) collective-permute-start(bf16[768,2304]{1,0:T(8,128)(2,1)} %bitcast.9), channel_id=1, source_target_pairs={{0,8},{8,0},{16,24},{24,16},{32,40},{40,32},{48,56},{56,48},{1,9},... | collective-permute-start | bytes 10616840 | tf_op jit(solution)/shard_map/ppermute | solution.py:21
  53.9 2.2 pad_maximum_fusion.6
  56.1 5.0 %all-to-all-start = ((bf16[4,960,512]{2,1,0:T(8,128)(2,1)}), bf16[4,960,512]{2,1,0:T(8,128)(2,1)}, u32[]{:S(2)}, u32[]{:S(2)}) async-start(bf16[4,960,512]{2,1,0:T(8,128)(2,1)} %pad_maximum_fusion.6), calls=%async_computation | async-start | bytes 7864320 | tf_op jit(solution)/shard_map/all_to_all | solution.py:88
  61.1 0.3 reduce_max.51
  61.4 0.7 exponential_reduce_fusion
  62.0 45.0 %all-to-all-done = bf16[4,960,512]{2,1,0:T(8,128)(2,1)} async-done(((bf16[4,960,512]{2,1,0:T(8,128)(2,1)}), bf16[4,960,512]{2,1,0:T(8,128)(2,1)}, u32[]{:S(2)}, u32[]{:S(2)}) %all-to-all-start) | async-done | bytes 3932192 | tf_op jit(solution)/shard_map/all_to_all | solution.py:88
  107.0 1.8 slice.106
  108.9 7.8 %fusion.39 = (f32[1536]{0:T(1024)S(1)}, f32[1536,512]{0,1:T(8,128)S(1)}) fusion(bf16[2304,512]{1,0:T(8,128)(2,1)S(1)} %bitcast.93, bf16[768,2304]{1,0:T(8,128)(2,1)} %collective-permute-done.7, bf16[768,2304]{1,0:T(8,128)(2,1)} %bitcast.9), kind=kOutput, calls=%fused_computation.93 | convolution fusion | flops 3638819328 | bytes 12589056 | tf_op jit(solution)/shard_map/dot_general | solution.py:100
  116.7 0.5 exponential_reduce_fusion.1
  117.3 0.8 broadcast_in_dim.58
  118.1 5.0 %all-to-all-start.1 = ((f32[32,1,1920]{2,1,0:T(1,128)}), f32[32,1,1920]{2,1,0:T(1,128)}, u32[]{:S(2)}, u32[]{:S(2)}) async-start(f32[32,1,1920]{2,1,0:T(1,128)} %broadcast_in_dim.58), calls=%async_computation.1 | async-start | bytes 491520 | tf_op jit(solution)/shard_map/all_to_all | solution.py:56
  123.1 0.5 collective-permute-start.9
  123.6 2.7 slice.112
  126.3 5.7 %all-to-all-done.1 = f32[32,1,1920]{2,1,0:T(1,128)} async-done(((f32[32,1,1920]{2,1,0:T(1,128)}), f32[32,1,1920]{2,1,0:T(1,128)}, u32[]{:S(2)}, u32[]{:S(2)}) %all-to-all-start.1) | async-done | bytes 245792 | tf_op jit(solution)/shard_map/all_to_all | solution.py:56
  132.0 1.0 copy.34
  133.2 0.7 broadcast_in_dim.59
  133.9 8.2 %all-to-all-start.2 = ((f32[8,1,3072]{2,1,0:T(1,128)}), f32[8,1,3072]{2,1,0:T(1,128)S(1)}, u32[]{:S(2)}, u32[]{:S(2)}) async-start(f32[8,1,3072]{2,1,0:T(1,128)} %broadcast_in_dim.59), calls=%async_computation.2 | async-start | bytes 196608 | tf_op jit(solution)/shard_map/all_to_all | solution.py:56
  142.1 2.8 %convert_bitcast_fusion.2 = (f32[4,4,48,512]{3,2,0,1:T(8,128)S(1)}, f32[4,4,48,512]{3,2,0,1:T(8,128)}) fusion(bf16[4,4,2,48,512]{4,3,2,1,0:T(8,128)(2,1)} %bitcast.83, s32[]{:T(128)S(6)} %select_n.125, s32[]{:T(128)S(6)} %select_n.126), kind=kLoop, calls=%fused_computation.27 | loop fusion | flops 786432 | bytes 4718600 | tf_op jit(solution)/shard_map/convert_element_type | solution.py:113
  144.9 1.3 copy.23
  146.2 3.0 %copy.25 = f32[768,512]{0,1:T(8,128)} copy(f32[768,512]{1,0:T(8,128)} %bitcast.84) | data formatting | bytes 3145728 | tf_op jit(solution)/shard_map/convert_element_type | solution.py:113
  149.2 2.7 %copy.26 = f32[4,4,48,512]{3,2,1,0:T(8,128)} copy(f32[4,4,48,512]{3,2,0,1:T(8,128)} %get-tuple-element.26) | data formatting | bytes 3145728 | tf_op jit(solution)/shard_map/convert_element_type | solution.py:113
  151.9 3.0 %copy.27 = f32[768,512]{0,1:T(8,128)} copy(f32[768,512]{1,0:T(8,128)} %bitcast.85) | data formatting | bytes 3145728 | tf_op jit(solution)/shard_map/convert_element_type | solution.py:113
  155.4 2.8 %fusion.10 = (bf16[768,512]{0,1:T(8,128)(2,1)S(1)}, bf16[768,512]{0,1:T(8,128)(2,1)S(1)}) fusion(f32[1536,512]{0,1:T(8,128)S(1)} %get-tuple-element.38, f32[768,512]{0,1:T(8,128)} %copy.25, f32[768]{0:T(1024)S(1)} %get-tuple-element.8, f32[768]{0:T(1024)S(1)} %get-tuple-element.6, f32[768,512]{0,1:T(8,128)} %copy.27, f32[768]{0:T(1024)S(1)} %get-tuple-element.9, ...), kind=kLoop, calls=%fused_computation.21 | loop fusion | flops 3932160 | bytes 7876608 | tf_op jit(solution)/shard_map/convert_element_type | solution.py:116
  158.2 0.7 collective-permute-start.8
  158.9 8.4 %fusion.2 = bf16[2304,512]{1,0:T(8,128)(2,1)} fusion(bf16[768,2304]{1,0:T(8,128)(2,1)} %collective-permute-done.7, bf16[768,2304]{1,0:T(8,128)(2,1)} %bitcast.9, bf16[768,512]{0,1:T(8,128)(2,1)S(1)} %get-tuple-element.11, bf16[768,512]{0,1:T(8,128)(2,1)S(1)} %get-tuple-element.10), kind=kOutput, calls=%fused_computation.6 | convolution fusion | flops 3642359808 | bytes 11010048 | tf_op jit(solution)/shard_map/dot_general | solution.py:134
  167.4 0.8 copy.28
  168.3 1.5 copy-done.3
  169.8 3.4 %convolution_convert_fusion.1 = bf16[192,2304]{1,0:T(8,128)(2,1)S(1)} fusion(bf16[2304,512]{1,0:T(8,128)(2,1)} %collective-permute-done.9, bf16[2304,512]{1,0:T(8,128)(2,1)S(1)} %bitcast.95, bf16[4,192,1024]{2,1,0:T(8,128)(2,1)S(1)} %bitcast.87, s32[]{:T(128)S(6)} %select_n.120), kind=kOutput, calls=%fused_computation.8 | convolution fusion | flops 915849216 | bytes 5996548 | tf_op jit(solution)/shard_map/dot_general | solution.py:128
  173.3 0.4 collective-permute-start.10
  173.6 2.4 collective-permute-start.12
  176.0 4.6 %convolution_convert_fusion = bf16[576,2304]{1,0:T(8,128)(2,1)S(1)} fusion(bf16[2304,512]{1,0:T(8,128)(2,1)} %collective-permute-done.9, bf16[2304,512]{1,0:T(8,128)(2,1)S(1)} %bitcast.96, bf16[192,1024]{1,0:T(8,128)(2,1)S(1)} %get-tuple-element.23, bf16[192,1024]{1,0:T(8,128)(2,1)S(1)} %get-tuple-element.24, bf16[192,1024]{1,0:T(8,128)(2,1)S(1)} %get-tuple-element.22), kind=kOutput, calls=%fused_computation.3 | convolution fusion | flops 2732212224 | bytes 8552448 | tf_op jit(solution)/shard_map/dot_general | solution.py:128
  180.6 5.5 %collective-permute-done.10 = bf16[96,2304]{1,0:T(8,128)(2,1)S(1)} collective-permute-done((bf16[96,2304]{1,0:T(8,128)(2,1)S(1)}, bf16[96,2304]{1,0:T(8,128)(2,1)S(1)}, u32[]{:S(2)}, u32[]{:S(2)}) %collective-permute-start.10) | collective-permute-done | bytes 442400 | tf_op jit(solution)/shard_map/ppermute | solution.py:16
  186.2 0.2 slice_add_fusion.1
  186.4 2.5 collective-permute-start.13
  188.9 17.9 %collective-permute-done.13 = bf16[192,2304]{1,0:T(8,128)(2,1)S(1)} collective-permute-done((bf16[192,2304]{1,0:T(8,128)(2,1)S(1)}, bf16[192,2304]{1,0:T(8,128)(2,1)S(1)}, u32[]{:S(2)}, u32[]{:S(2)}) %collective-permute-start.13) | collective-permute-done | bytes 884768 | tf_op jit(solution)/shard_map/ppermute | solution.py:16
  206.7 3.0 %collective-permute-done.11 = bf16[192,2304]{1,0:T(8,128)(2,1)S(1)} collective-permute-done((bf16[192,2304]{1,0:T(8,128)(2,1)S(1)}, bf16[192,2304]{1,0:T(8,128)(2,1)S(1)}, u32[]{:S(2)}, u32[]{:S(2)}) %collective-permute-start.11) | collective-permute-done | bytes 884768 | tf_op jit(solution)/shard_map/ppermute | solution.py:16
  209.8 0.3 add_convert_fusion
  210.1 13.5 %all_to_all.38 = bf16[4,48,2304]{2,1,0:T(8,128)(2,1)S(1)} all-to-all(bf16[4,48,2304]{2,1,0:T(8,128)(2,1)S(1)} %bitcast.88), channel_id=1, replica_groups=mesh['layer'=4,'row'=8,'col'=8] {'layer'}, dimensions={0} | all-to-all | bytes 1769472 | tf_op jit(solution)/shard_map/all_to_all | solution.py:145
  223.6 3.6 %all-to-all-start.3 = ((bf16[4,576,512]{2,1,0:T(8,128)(2,1)}), bf16[4,576,512]{2,1,0:T(8,128)(2,1)S(1)}, u32[]{:S(2)}, u32[]{:S(2)}) async-start(bf16[4,576,512]{2,1,0:T(8,128)(2,1)} %bitcast.97), calls=%async_computation.3 | async-start | bytes 4718592 | tf_op jit(solution)/shard_map/all_to_all | solution.py:139
  227.4 0.8 reshape.112
  228.2 25.0 %all-to-all-done.3 = bf16[4,576,512]{2,1,0:T(8,128)(2,1)S(1)} async-done(((bf16[4,576,512]{2,1,0:T(8,128)(2,1)}), bf16[4,576,512]{2,1,0:T(8,128)(2,1)S(1)}, u32[]{:S(2)}, u32[]{:S(2)}) %all-to-all-start.3) | async-done | bytes 2359328 | tf_op jit(solution)/shard_map/all_to_all | solution.py:139
  253.2 7.3 %all-to-all-start.5 = ((bf16[8,6,2304]{2,1,0:T(8,128)(2,1)}), bf16[8,6,2304]{2,1,0:T(8,128)(2,1)S(1)}, u32[]{:S(2)}, u32[]{:S(2)}) async-start(bf16[8,6,2304]{2,1,0:T(8,128)(2,1)} %reshape.112), calls=%async_computation.5 | async-start | bytes 589824 | tf_op jit(solution)/shard_map/all_to_all | solution.py:148
  260.6 2.8 %convert_bitcast_fusion = f32[2048,576]{0,1:T(8,128)} fusion(bf16[576,512]{1,0:T(8,128)(2,1)S(1)} %get-tuple-element.15, bf16[576,512]{1,0:T(8,128)(2,1)S(1)} %get-tuple-element.16, bf16[576,512]{1,0:T(8,128)(2,1)S(1)} %get-tuple-element.17, bf16[576,512]{1,0:T(8,128)(2,1)S(1)} %get-tuple-element.14), kind=kLoop, calls=%fused_computation.2 | loop fusion | flops 9437184 | bytes 7077888 | tf_op jit(solution)/shard_map/transpose | solution.py:150
  263.4 6.7 %all-to-all-done.5 = bf16[8,6,2304]{2,1,0:T(8,128)(2,1)S(1)} async-done(((bf16[8,6,2304]{2,1,0:T(8,128)(2,1)}), bf16[8,6,2304]{2,1,0:T(8,128)(2,1)S(1)}, u32[]{:S(2)}, u32[]{:S(2)}) %all-to-all-start.5) | async-done | bytes 221216 | tf_op jit(solution)/shard_map/all_to_all | solution.py:148
  270.2 0.7 convert_reduce_fusion
  (56 shorter events, 1.9 us)
Async XLA Ops:
  0.6 17.4 %copy-start = (bf16[384,2048]{1,0:T(8,128)(2,1)S(1)}, bf16[384,2048]{1,0:T(8,128)(2,1)}, u32[]{:S(2)}) copy-start(bf16[384,2048]{1,0:T(8,128)(2,1)} %param.5) | copy-start | bytes 4718596
  0.6 7.2 %collective-permute-start = (bf16[48,2304]{1,0:T(8,128)(2,1)}, bf16[48,2304]{1,0:T(8,128)(2,1)S(1)}, u32[]{:S(2)}, u32[]{:S(2)}) collective-permute-start(bf16[48,2304]{1,0:T(8,128)(2,1)} %param.3), channel_id=1, source_target_pairs={{0,64},{64,128},{128,192},{192,0},{1,65},{65,129},{129,193},{193,1... | collective-permute-start | bytes 663560 | tf_op jit(solution)/shard_map/ppermute | solution.py:11
  2.8 6.0 %collective-permute-start.1 = (bf16[48,2304]{1,0:T(8,128)(2,1)}, bf16[48,2304]{1,0:T(8,128)(2,1)S(1)}, u32[]{:S(2)}, u32[]{:S(2)}) collective-permute-start(bf16[48,2304]{1,0:T(8,128)(2,1)} %param.3), channel_id=1, source_target_pairs={{0,192},{64,0},{128,64},{192,128},{1,193},{65,1},{129,65},{193,129... | collective-permute-start | bytes 663560 | tf_op jit(solution)/shard_map/ppermute | solution.py:11
  4.4 10.9 %collective-permute-start.2 = (bf16[48,2304]{1,0:T(8,128)(2,1)}, bf16[48,2304]{1,0:T(8,128)(2,1)S(1)}, u32[]{:S(2)}, u32[]{:S(2)}) collective-permute-start(bf16[48,2304]{1,0:T(8,128)(2,1)} %param.3), channel_id=1, source_target_pairs={{0,128},{64,192},{128,0},{192,64},{1,129},{65,193},{129,1},{193,65... | collective-permute-start | bytes 663560 | tf_op jit(solution)/shard_map/ppermute | solution.py:11
  7.1 11.1 %copy-start.1 = (bf16[2048,576]{0,1:T(8,128)(2,1)S(1)}, bf16[2048,576]{0,1:T(8,128)(2,1)}, u32[]{:S(2)}) copy-start(bf16[2048,576]{0,1:T(8,128)(2,1)} %param.4) | copy-start | bytes 7077892
  15.3 23.5 %collective-permute-start.3 = (bf16[192,2304]{1,0:T(8,128)(2,1)S(1)}, bf16[192,2304]{1,0:T(8,128)(2,1)S(1)}, u32[]{:S(2)}, u32[]{:S(2)}) collective-permute-start(bf16[192,2304]{1,0:T(8,128)(2,1)S(1)} %bitcast.89), channel_id=1, source_target_pairs={{0,16},{8,24},{16,32},{24,40},{32,48},{40,56},{48,0},{56,8},{1,17}... | collective-permute-start | bytes 2654216 | tf_op jit(solution)/shard_map/ppermute | solution.py:16
  16.6 19.4 %collective-permute-start.4 = (bf16[192,2304]{1,0:T(8,128)(2,1)S(1)}, bf16[192,2304]{1,0:T(8,128)(2,1)S(1)}, u32[]{:S(2)}, u32[]{:S(2)}) collective-permute-start(bf16[192,2304]{1,0:T(8,128)(2,1)S(1)} %bitcast.90), channel_id=1, source_target_pairs={{0,48},{8,56},{16,0},{24,8},{32,16},{40,24},{48,32},{56,40},{1,49}... | collective-permute-start | bytes 2654216 | tf_op jit(solution)/shard_map/ppermute | solution.py:16
  36.0 9.6 %collective-permute-start.6 = (bf16[96,2304]{1,0:T(8,128)(2,1)S(1)}, bf16[96,2304]{1,0:T(8,128)(2,1)S(1)}, u32[]{:S(2)}, u32[]{:S(2)}) collective-permute-start(bf16[96,2304]{1,0:T(8,128)(2,1)S(1)} %slice.101), channel_id=1, source_target_pairs={{0,48},{8,56},{16,0},{24,8},{32,16},{40,24},{48,32},{56,40},{1,49}... | collective-permute-start | bytes 1327112 | tf_op jit(solution)/shard_map/ppermute | solution.py:16
  38.8 10.1 %collective-permute-start.5 = (bf16[96,2304]{1,0:T(8,128)(2,1)S(1)}, bf16[96,2304]{1,0:T(8,128)(2,1)S(1)}, u32[]{:S(2)}, u32[]{:S(2)}) collective-permute-start(bf16[96,2304]{1,0:T(8,128)(2,1)S(1)} %slice.100), channel_id=1, source_target_pairs={{0,16},{8,24},{16,32},{24,40},{32,48},{40,56},{48,0},{56,8},{1,17}... | collective-permute-start | bytes 1327112 | tf_op jit(solution)/shard_map/ppermute | solution.py:16
  49.8 59.0 %collective-permute-start.7 = (bf16[768,2304]{1,0:T(8,128)(2,1)}, bf16[768,2304]{1,0:T(8,128)(2,1)}, u32[]{:S(2)}, u32[]{:S(2)}) collective-permute-start(bf16[768,2304]{1,0:T(8,128)(2,1)} %bitcast.9), channel_id=1, source_target_pairs={{0,8},{8,0},{16,24},{24,16},{32,40},{40,32},{48,56},{56,48},{1,9},... | collective-permute-start | bytes 10616840 | tf_op jit(solution)/shard_map/ppermute | solution.py:21
  56.1 50.9 %all-to-all-start = ((bf16[4,960,512]{2,1,0:T(8,128)(2,1)}), bf16[4,960,512]{2,1,0:T(8,128)(2,1)}, u32[]{:S(2)}, u32[]{:S(2)}) async-start(bf16[4,960,512]{2,1,0:T(8,128)(2,1)} %pad_maximum_fusion.6), calls=%async_computation | async-start | bytes 7864320 | tf_op jit(solution)/shard_map/all_to_all | solution.py:88
  108.8 7.9 %copy-start.2 = (bf16[4,576,512]{2,1,0:T(8,128)(2,1)}, bf16[4,576,512]{2,1,0:T(8,128)(2,1)S(1)}, u32[]{:S(2)}) copy-start(bf16[4,576,512]{2,1,0:T(8,128)(2,1)S(1)} %slice.106) | copy-start | bytes 7077892
  118.1 13.9 %all-to-all-start.1 = ((f32[32,1,1920]{2,1,0:T(1,128)}), f32[32,1,1920]{2,1,0:T(1,128)}, u32[]{:S(2)}, u32[]{:S(2)}) async-start(f32[32,1,1920]{2,1,0:T(1,128)} %broadcast_in_dim.58), calls=%async_computation.1 | async-start | bytes 491520 | tf_op jit(solution)/shard_map/all_to_all | solution.py:56
  123.1 45.1 %collective-permute-start.9 = (bf16[2304,512]{1,0:T(8,128)(2,1)}, bf16[2304,512]{1,0:T(8,128)(2,1)}, u32[]{:S(2)}, u32[]{:S(2)}) collective-permute-start(bf16[2304,512]{1,0:T(8,128)(2,1)} %bitcast.94), channel_id=1, source_target_pairs={{0,8},{8,0},{16,24},{24,16},{32,40},{40,32},{48,56},{56,48},{1,9},... | collective-permute-start | bytes 7077896 | tf_op jit(solution)/shard_map/ppermute | solution.py:21
  133.9 21.1 %all-to-all-start.2 = ((f32[8,1,3072]{2,1,0:T(1,128)}), f32[8,1,3072]{2,1,0:T(1,128)S(1)}, u32[]{:S(2)}, u32[]{:S(2)}) async-start(f32[8,1,3072]{2,1,0:T(1,128)} %broadcast_in_dim.59), calls=%async_computation.2 | async-start | bytes 196608 | tf_op jit(solution)/shard_map/all_to_all | solution.py:56
  158.2 9.1 %collective-permute-start.8 = (bf16[768,512]{0,1:T(8,128)(2,1)S(1)}, bf16[768,512]{0,1:T(8,128)(2,1)S(1)}, u32[]{:S(2)}, u32[]{:S(2)}) collective-permute-start(bf16[768,512]{0,1:T(8,128)(2,1)S(1)} %get-tuple-element.11), channel_id=1, source_target_pairs={{0,8},{8,0},{16,24},{24,16},{32,40},{40,32},{48,56},{56,48},{1,9},... | collective-permute-start | bytes 2359304 | tf_op jit(solution)/shard_map/ppermute | solution.py:21
  168.2 1.7 copy-start.3
  173.3 12.9 %collective-permute-start.10 = (bf16[96,2304]{1,0:T(8,128)(2,1)S(1)}, bf16[96,2304]{1,0:T(8,128)(2,1)S(1)}, u32[]{:S(2)}, u32[]{:S(2)}) collective-permute-start(bf16[96,2304]{1,0:T(8,128)(2,1)S(1)} %get-tuple-element.31), channel_id=1, source_target_pairs={{0,16},{8,24},{16,32},{24,40},{32,48},{40,56},{48,0},{56,8},{1,17}... | collective-permute-start | bytes 1327112 | tf_op jit(solution)/shard_map/ppermute | solution.py:16
  173.6 12.5 %collective-permute-start.12 = (bf16[96,2304]{1,0:T(8,128)(2,1)S(1)}, bf16[96,2304]{1,0:T(8,128)(2,1)S(1)}, u32[]{:S(2)}, u32[]{:S(2)}) collective-permute-start(bf16[96,2304]{1,0:T(8,128)(2,1)S(1)} %get-tuple-element.32), channel_id=1, source_target_pairs={{0,48},{8,56},{16,0},{24,8},{32,16},{40,24},{48,32},{56,40},{1,49}... | collective-permute-start | bytes 1327112 | tf_op jit(solution)/shard_map/ppermute | solution.py:16
  186.4 20.3 %collective-permute-start.13 = (bf16[192,2304]{1,0:T(8,128)(2,1)S(1)}, bf16[192,2304]{1,0:T(8,128)(2,1)S(1)}, u32[]{:S(2)}, u32[]{:S(2)}) collective-permute-start(bf16[192,2304]{1,0:T(8,128)(2,1)S(1)} %get-tuple-element.13), channel_id=1, source_target_pairs={{0,48},{8,56},{16,0},{24,8},{32,16},{40,24},{48,32},{56,40},{1,49}... | collective-permute-start | bytes 2654216 | tf_op jit(solution)/shard_map/ppermute | solution.py:16
  188.9 20.9 %collective-permute-start.11 = (bf16[192,2304]{1,0:T(8,128)(2,1)S(1)}, bf16[192,2304]{1,0:T(8,128)(2,1)S(1)}, u32[]{:S(2)}, u32[]{:S(2)}) collective-permute-start(bf16[192,2304]{1,0:T(8,128)(2,1)S(1)} %get-tuple-element.12), channel_id=1, source_target_pairs={{0,16},{8,24},{16,32},{24,40},{32,48},{40,56},{48,0},{56,8},{1,17}... | collective-permute-start | bytes 2654216 | tf_op jit(solution)/shard_map/ppermute | solution.py:16
  223.6 29.6 %all-to-all-start.3 = ((bf16[4,576,512]{2,1,0:T(8,128)(2,1)}), bf16[4,576,512]{2,1,0:T(8,128)(2,1)S(1)}, u32[]{:S(2)}, u32[]{:S(2)}) async-start(bf16[4,576,512]{2,1,0:T(8,128)(2,1)} %bitcast.97), calls=%async_computation.3 | async-start | bytes 4718592 | tf_op jit(solution)/shard_map/all_to_all | solution.py:139
  253.2 17.0 %all-to-all-start.5 = ((bf16[8,6,2304]{2,1,0:T(8,128)(2,1)}), bf16[8,6,2304]{2,1,0:T(8,128)(2,1)S(1)}, u32[]{:S(2)}, u32[]{:S(2)}) async-start(bf16[8,6,2304]{2,1,0:T(8,128)(2,1)} %reshape.112), calls=%async_computation.5 | async-start | bytes 589824 | tf_op jit(solution)/shard_map/all_to_all | solution.py:148

commit v3 on v2

--- a/solution.py
+++ b/solution.py
@@ -1,6 +1,7 @@
 import jax
 import jax.numpy as jnp
 from jax import lax
+from jax.experimental import pallas as pl
 from jax.sharding import PartitionSpec as P
 
 LOSS_SCALE = 256
@@ -59,6 +60,90 @@
 def logsum(values, dim):
     top = jnp.max(values, axis=dim)
     return top + jnp.log(jnp.sum(jnp.exp(values - jnp.expand_dims(top, dim)), axis=dim))
+
+
+def whole(x):
+    return pl.BlockSpec(x.shape, lambda i: (0,) * x.ndim)
+
+
+def cost(rows, depth, cols, moved):
+    return pl.CostEstimate(flops=2 * rows * depth * cols, bytes_accessed=moved, transcendentals=0)
+
+
+def scores_kernel(state_ref, table_ref, out_ref, sum_ref):
+    out = jnp.dot(state_ref[...], table_ref[...], preferred_element_type=jnp.float32)
+    out_ref[...] = out
+    top = jnp.max(out, axis=1, keepdims=True)
+    total = top + jnp.log(jnp.sum(jnp.exp(out - top), axis=1, keepdims=True))
+    total = jnp.broadcast_to(total, (out.shape[0], 128)).T
+    sum_ref[...] = total[: sum_ref.shape[0]]
+
+
+def scores(states, table):
+    tokens, width = states.shape
+    block = table.shape[1]
+    tile = 256 if tokens % 256 == 0 else tokens
+    logits, sums = pl.pallas_call(
+        scores_kernel,
+        grid=(tokens // tile,),
+        in_specs=[pl.BlockSpec((tile, width), lambda i: (i, 0)), whole(table)],
+        out_specs=[
+            pl.BlockSpec((tile, block), lambda i: (i, 0)),
+            pl.BlockSpec((8, tile), lambda i: (0, i)),
+        ],
+        out_shape=[
+            jax.ShapeDtypeStruct((tokens, block), jnp.float32),
+            jax.ShapeDtypeStruct((8, tokens), jnp.float32),
+        ],
+        cost_estimate=cost(tokens, width, block, 2 * tokens * width + 4 * tokens * block),
+    )(states, table)
+    return logits, sums[0]
+
+
+def part_kernel(mine_ref, other_ref, table_ref, far_ref, out_ref):
+    over = (((1,), (1,)), ((), ()))
+    f32 = jnp.float32
+    total = lax.dot_general(mine_ref[...], table_ref[...], over, preferred_element_type=f32)
+    total += lax.dot_general(other_ref[...], far_ref[...], over, preferred_element_type=f32)
+    out_ref[...] = total.astype(out_ref.dtype)
+
+
+def part_of(mine, other, table, far):
+    tokens, block = mine.shape
+    width = table.shape[0]
+    tile = 384 if width % 384 == 0 else width
+    band = pl.BlockSpec((tile, block), lambda i: (i, 0))
+    return pl.pallas_call(
+        part_kernel,
+        grid=(width // tile,),
+        in_specs=[whole(mine), whole(other), band, band],
+        out_specs=pl.BlockSpec((tokens, tile), lambda i: (0, i)),
+        out_shape=jax.ShapeDtypeStruct((tokens, width), jnp.bfloat16),
+        cost_estimate=cost(tokens, 2 * block, width, 4 * width * block),
+    )(mine, other, table, far)
+
+
+def table_kernel(own_ref, other_ref, own_grad_ref, other_grad_ref, out_ref):
+    over = (((0,), (0,)), ((), ()))
+    f32 = jnp.float32
+    total = lax.dot_general(own_ref[...], own_grad_ref[...], over, preferred_element_type=f32)
+    total += lax.dot_general(other_ref[...], other_grad_ref[...], over, preferred_element_type=f32)
+    out_ref[...] = total.astype(out_ref.dtype)
+
+
+def table_gradient(own, other, own_grads, other_grads):
+    tokens, width = own.shape
+    block = own_grads.shape[1]
+    tile = 256 if width % 256 == 0 else width
+    band = pl.BlockSpec((tokens, tile), lambda i: (0, i))
+    return pl.pallas_call(
+        table_kernel,
+        grid=(width // tile,),
+        in_specs=[band, band, whole(own_grads), whole(other_grads)],
+        out_specs=pl.BlockSpec((tile, block), lambda i: (i, 0)),
+        out_shape=jax.ShapeDtypeStruct((width, block), jnp.bfloat16),
+        cost_estimate=cost(2 * tokens, width, block, 4 * tokens * width),
+    )(own, other, own_grads, other_grads)
 
 
 def ordered(core, own, other):
@@ -89,17 +174,16 @@
     table = sent[:, :quarter].reshape(width, block)
     taught = sent[:, quarter:].reshape(layers, xs, 2, strip, block)
 
-    own = jnp.zeros((xs, layers * strip, width), bf16)
+    own = jnp.zeros((layers, xs, strip, width), bf16)
     pieces = ring_gather(mine.reshape(layers * strip, width), shift_x)
     for k, p in pieces:
-        own = put(own, p, (x + k) % xs)
+        own = put(own, p.reshape(layers, strip, width), (x + k) % xs, 1)
     own = own.reshape(half, width)
     other = swap_core(own)
 
-    states = jnp.concatenate([own, other])
-    logits = jnp.dot(states, table, preferred_element_type=f32)
-    lse_s = logsum(logits, 1)
-    lse_s = ordered(core, lse_s[:half], lse_s[half:])
+    logits_own, sum_own = scores(own, table)
+    logits_other, sum_other = scores(other, table)
+    lse_s = ordered(core, sum_own, sum_other)
     lse_t = logsum(teacher.astype(f32), 1)
     got = spread(jnp.concatenate([lse_s.reshape(2 * half), lse_t]), ("layer", "row"))
     lse_s = logsum(got[:, : 2 * half], 0)
@@ -107,39 +191,37 @@
     got = spread(jnp.concatenate([lse_s, lse_t.reshape(2 * half)]), "col")
     lse_s, lse_t = jnp.split(logsum(got, 0), 2)
     lse_s = lse_s.reshape(2, half)
-    lse_t = lse_t.reshape(layers, xs, 2, strip).transpose(2, 1, 0, 3).reshape(2, half)
+    lse_t = lse_t.reshape(layers * xs, 2, strip).swapaxes(0, 1).reshape(2, half)
 
     def gradient(logits, c):
-        taught_c = at(taught, c, 2).swapaxes(0, 1).reshape(half, block).astype(f32)
+        taught_c = at(taught, c, 2).reshape(half, block).astype(f32)
         prob_s = jnp.exp(logits - at(lse_s, c)[:, None])
         prob_t = jnp.exp(taught_c - at(lse_t, c)[:, None])
         return ((prob_s - prob_t) * LOSS_SCALE).astype(bf16)
 
-    grads_other = gradient(logits[half:], 1 - core)
+    grads_other = gradient(logits_other, 1 - core)
     crossed = swap_core(grads_other)
-    grads_own = gradient(logits[:half], core)
+    grads_own = gradient(logits_own, core)
     other_table = swap_core(table)
 
-    both = jnp.concatenate([grads_own, crossed], axis=1).reshape(xs, layers * strip, 2 * block)
-    tables = jnp.concatenate([table, other_table], axis=1)
 
     def part(*ks):
-        lines = jnp.concatenate([at(both, (x + k) % xs) for k in ks])
-        return lax.dot_general(
-            lines, tables, (((1,), (1,)), ((), ())), preferred_element_type=f32
-        ).astype(bf16)
-
-    grads = jnp.concatenate([grads_own, grads_other])
+        def lines(grads):
+            grads = grads.reshape(layers, xs, strip, block)
+            picked = [at(grads, (x + k) % xs, 1).reshape(layers * strip, block) for k in ks]
+            return jnp.concatenate(picked)
+
+        return part_of(lines(grads_own), lines(crossed), table, other_table)
+
     far = ring_sum_far(part(2), shift_x)
-    grad_table = lax.dot_general(
-        states, grads, (((0,), (0,)), ((), ())), preferred_element_type=f32
-    ).astype(bf16)
-    both, grad_table = lax.optimization_barrier((both, grad_table))
+
+    grad_table = table_gradient(own, other, grads_own, grads_other)
+    crossed, grad_table = lax.optimization_barrier((crossed, grad_table))
     grad_table = grad_table.reshape(layers, quarter, block)
     grad_table = lax.all_to_all(grad_table, "layer", 0, 0, tiled=True)
     grad_table = jnp.concatenate([grad_table[k].astype(f32) for k in range(layers)], axis=1)
 
-    ahead, behind, here = jnp.split(lax.optimization_barrier(part(1, 3, 0)), 3)
+    ahead, behind, here = jnp.split(part(1, 3, 0), 3)
     summed = ring_sum(here, ahead, behind, far, shift_x).astype(bf16)
     summed = summed.reshape(layers, strip, width)
     summed = lax.all_to_all(summed, "layer", 0, 0, tiled=True)

time: 275 us -> 288 us (1.047)
  Pallas kernels: 0 us -> 36.8 us
  matrix products: 24.2 us -> 0 us
  local copies, waits for them, and re-layouts: 27.3 us -> 37.4 us
  waiting for transfers between devices: 139 us -> 129 us
  other arithmetic: 15.1 us -> 19.2 us
  starting transfers between devices: 50.2 us -> 46.8 us
    pallas_call x0 -> x5, Pallas kernels: none -> 36.8 us  [the longest x2 14.4 us: part_of(): pl.pallas_call(part_kernel, grid=(width // tile,), in_specs=[whole(mine),...]
    dot_general x4 -> x0, matrix products: 24.2 us -> none  [the longest x1 8.39 us: local(): lax.dot_general(states, grads, (((0,), (0,)), ((), ())), preferred_elemen...]
    ppermute x8, waiting for transfers between devices: 48.8 us -> 38.1 us  [shift_x(): return lax.ppermute(x, 'row', [(i, (i + 2 * s) % n) for i in range(n)])]
    convert_element_type x4 -> x0, local copies, waits for them, and re-layouts: 10.1 us -> none  [gradient(): taught_c = at(taught, c, 2).swapaxes(0, 1).reshape(half, block).astype(f32)]
    dynamic_update_slice x7 -> x8, local copies, waits for them, and re-layouts: 4.04 us -> 13.1 us  [put(): return lax.dynamic_update_slice_in_dim(buf, jnp.expand_dims(x, dim), k, dim)]
    ppermute x3, waiting for transfers between devices: 8.11 us -> 0.32 us  [shift_y(): return lax.ppermute(x, 'layer', [(i, (i + s) % n) for i in range(n)])]
    all_to_all x2, waiting for transfers between devices: 5.72 us -> 13.4 us  [spread(): lax.all_to_all(jnp.broadcast_to(x[None], (n, *x.shape)), axis, 0, 0, tile...]
    dynamic_slice x2 -> x5, local copies, waits for them, and re-layouts: 0.06 us -> 4.76 us  [at(): return lax.dynamic_index_in_dim(x, k, dim, keepdims=False)]
  transfers between devices with their start and end apart: 19 -> 19, of which waited for: 13 -> 12; matrix products, arithmetic and copies ran while one was open for 19% -> 17% of each run, Pallas kernels for 0% -> 9%
where the time goes in v3:
time: 288 us; the launch traced here: 284 us
  waiting for transfers between devices  129 us (45%)
  starting transfers between devices  46.8 us (16%)
  local copies, waits for them, and re-layouts  37.4 us (13%)
  Pallas kernels  36.8 us (13%)
  other arithmetic  19.2 us (7%)
  blocking collectives  13.5 us (5%)
    all_to_all x1, waiting for transfers between devices, local(): sent = lax.all_to_all(jnp.stack(sent), 'layer', 0, 0, tiled=True)  45.2 us
    ppermute x8, waiting for transfers between devices, shift_x(): return lax.ppermute(x, 'row', [(i, (i + 2 * s) % n) for i in range(n)])  38.1 us
    all_to_all x1, waiting for transfers between devices, local(): grad_table = lax.all_to_all(grad_table, 'layer', 0, 0, tiled=True)  25.1 us
    pallas_call x2, Pallas kernels, part_of(): pl.pallas_call(part_kernel, grid=(width // tile,), in_specs=[whole(mine),...  14.4 us
    all_to_all x1, blocking collectives, local(): summed = lax.all_to_all(summed, 'layer', 0, 0, tiled=True)  13.5 us
    all_to_all x2, waiting for transfers between devices, spread(): lax.all_to_all(jnp.broadcast_to(x[None], (n, *x.shape)), axis, 0, 0, tile...  13.4 us
    dynamic_update_slice x8, local copies, waits for them, and re-layouts, put(): return lax.dynamic_update_slice_in_dim(buf, jnp.expand_dims(x, dim), k, dim)  13.1 us
    all_to_all x2, starting transfers between devices, spread(): lax.all_to_all(jnp.broadcast_to(x[None], (n, *x.shape)), axis, 0, 0, tile...  12.9 us
  transfers between devices with their start and end apart: 19, of which 12 were waited for; matrix products, arithmetic and copies ran while one was open for 17% of the time, Pallas kernels for 9%

profile of v3, /device:TPU:1, one launch (start us, length us, event | category | flops | bytes accessed | tf_op | source)
XLA Modules:
  0.0 283.5 jit_solution(16322378415616591004)
XLA Ops:
  0.6 2.2 collective-permute-start
  2.8 1.5 collective-permute-start.1
  4.4 1.6 collective-permute-start.2
  5.9 3.0 %fusion.15 = (bf16[576,512]{1,0:T(8,128)(2,1)}, bf16[576,512]{1,0:T(8,128)(2,1)S(1)}, bf16[576,512]{1,0:T(8,128)(2,1)}, bf16[576,512]{1,0:T(8,128)(2,1)}) fusion(bf16[576,2048]{1,0:T(8,128)(2,1)} %bitcast.100), kind=kLoop, calls=%fused_computation.70 | loop fusion | bytes 4718592 | tf_op jit(solution)/shard_map/slice | solution.py:171
  8.9 1.0 broadcast_in_dim.17
  10.6 1.1 fusion.16
  11.7 1.7 bitcast_dynamic-update-slice_fusion.3
  13.4 1.6 bitcast_dynamic-update-slice_fusion.2
  15.3 1.6 bitcast_dynamic-update-slice_fusion.1
  17.0 1.2 collective-permute-start.3
  18.2 1.5 collective-permute-start.4
  19.7 1.1 maximum_bitcast_fusion.2
  20.9 1.3 maximum_bitcast_fusion.1
  22.1 2.1 broadcast_in_dim.16
  24.3 2.2 bitcast_dynamic-update-slice_fusion
  26.4 11.5 %collective-permute-done.4 = bf16[192,2304]{1,0:T(8,128)(2,1)} collective-permute-done((bf16[192,2304]{1,0:T(8,128)(2,1)}, bf16[192,2304]{1,0:T(8,128)(2,1)}, u32[]{:S(2)}, u32[]{:S(2)}) %collective-permute-start.4) | collective-permute-done | bytes 884768 | tf_op jit(solution)/shard_map/ppermute | solution.py:17
  37.9 1.0 slice.93
  39.0 2.4 collective-permute-start.6
  41.4 1.0 slice.92
  42.5 2.2 constant_dynamic-update-slice_fusion.2
  44.7 2.1 constant_dynamic-update-slice_fusion.1
  46.8 1.3 collective-permute-done.6
  48.1 4.1 %collective-permute-done.5 = bf16[96,2304]{1,0:T(8,128)(2,1)S(1)} collective-permute-done((bf16[96,2304]{1,0:T(8,128)(2,1)S(1)}, bf16[96,2304]{1,0:T(8,128)(2,1)S(1)}, u32[]{:S(2)}, u32[]{:S(2)}) %collective-permute-start.5) | collective-permute-done | bytes 442400 | tf_op jit(solution)/shard_map/ppermute | solution.py:17
  52.2 1.0 constant_dynamic-update-slice_fusion
  53.2 4.1 %collective-permute-start.7 = (bf16[768,2304]{1,0:T(8,128)(2,1)}, bf16[768,2304]{1,0:T(8,128)(2,1)}, u32[]{:S(2)}, u32[]{:S(2)}) collective-permute-start(bf16[768,2304]{1,0:T(8,128)(2,1)} %bitcast.9.state_ref.own_ref), channel_id=1, source_target_pairs={{0,8},{8,0},{16,24},{24,16},{32,40},{40,32},{48,56},{56,48},{1,9},... | collective-permute-start | bytes 10616840 | tf_op jit(solution)/shard_map/ppermute | solution.py:22
  57.4 2.2 pad_maximum_fusion
  59.6 4.8 %all-to-all-start = ((bf16[4,960,512]{2,1,0:T(8,128)(2,1)}), bf16[4,960,512]{2,1,0:T(8,128)(2,1)}, u32[]{:S(2)}, u32[]{:S(2)}) async-start(bf16[4,960,512]{2,1,0:T(8,128)(2,1)} %pad_maximum_fusion), calls=%async_computation | async-start | bytes 7864320 | tf_op jit(solution)/shard_map/all_to_all | solution.py:173
  65.4 45.2 %all-to-all-done = bf16[4,960,512]{2,1,0:T(8,128)(2,1)} async-done(((bf16[4,960,512]{2,1,0:T(8,128)(2,1)}), bf16[4,960,512]{2,1,0:T(8,128)(2,1)}, u32[]{:S(2)}, u32[]{:S(2)}) %all-to-all-start) | async-done | bytes 3932192 | tf_op jit(solution)/shard_map/all_to_all | solution.py:173
  110.5 3.3 %slice.98 = bf16[4,576,512]{2,1,0:T(8,128)(2,1)} slice(bf16[4,960,512]{2,1,0:T(8,128)(2,1)} %all-to-all-done), slice={[0:4], [0:576], [0:512]} | slice | bytes 4718592 | tf_op jit(solution)/shard_map/slice | solution.py:174
  113.9 5.9 %shard_map.51 = (f32[768,512]{1,0:T(8,128)}, f32[8,768]{1,0:T(8,128)}) custom-call(bf16[768,2304]{1,0:T(8,128)(2,1)} %bitcast.9.state_ref.own_ref, bf16[2304,512]{1,0:T(8,128)(2,1)} %bitcast.91), custom_call_target="tpu_custom_call" | custom-call | flops 1811939328 | bytes 5111808 | tf_op jit(solution)/shard_map/pallas_call | solution.py:86
  119.8 0.7 slice.81
  120.5 6.0 %shard_map.50 = (f32[768,512]{1,0:T(8,128)}, f32[8,768]{1,0:T(8,128)}) custom-call(bf16[768,2304]{1,0:T(8,128)(2,1)} %collective-permute-done.7.state_ref.other_ref, bf16[2304,512]{1,0:T(8,128)(2,1)} %bitcast.92), custom_call_target="tpu_custom_call" | custom-call | flops 1811939328 | bytes 5111808 | tf_op jit(solution)/shard_map/pallas_call | solution.py:86
  126.6 0.7 slice.82
  127.4 0.8 broadcast_in_dim.22
  128.2 4.4 %all-to-all-start.1 = ((f32[32,1,1920]{2,1,0:T(1,128)}), f32[32,1,1920]{2,1,0:T(1,128)S(1)}, u32[]{:S(2)}, u32[]{:S(2)}) async-start(f32[32,1,1920]{2,1,0:T(1,128)} %broadcast_in_dim.22), calls=%async_computation.1 | async-start | bytes 491520 | tf_op jit(solution)/shard_map/all_to_all | solution.py:57
  133.0 8.4 %all-to-all-done.1 = f32[32,1,1920]{2,1,0:T(1,128)S(1)} async-done(((f32[32,1,1920]{2,1,0:T(1,128)}), f32[32,1,1920]{2,1,0:T(1,128)S(1)}, u32[]{:S(2)}, u32[]{:S(2)}) %all-to-all-start.1) | async-done | bytes 245792 | tf_op jit(solution)/shard_map/all_to_all | solution.py:57
  142.3 8.5 %all-to-all-start.2 = ((f32[8,1,3072]{2,1,0:T(1,128)}), f32[8,1,3072]{2,1,0:T(1,128)S(1)}, u32[]{:S(2)}, u32[]{:S(2)}) async-start(f32[8,1,3072]{2,1,0:T(1,128)} %broadcast_in_dim.46), calls=%async_computation.2 | async-start | bytes 196608 | tf_op jit(solution)/shard_map/all_to_all | solution.py:57
  150.8 1.5 slice.101
  152.3 1.0 constant_dynamic-slice_fusion.9
  153.3 5.0 %all-to-all-done.2 = f32[8,1,3072]{2,1,0:T(1,128)S(1)} async-done(((f32[8,1,3072]{2,1,0:T(1,128)}), f32[8,1,3072]{2,1,0:T(1,128)S(1)}, u32[]{:S(2)}, u32[]{:S(2)}) %all-to-all-start.2) | async-done | bytes 98336 | tf_op jit(solution)/shard_map/all_to_all | solution.py:57
  158.8 3.1 %fusion.7.other_grad_ref = bf16[768,512]{1,0:T(8,128)(2,1)} fusion(f32[768,512]{1,0:T(8,128)} %get-tuple-element.8, bf16[4,4,1,48,512]{4,3,2,1,0:T(8,128)(2,1)} %get-tuple-element.29, f32[768]{0:T(1024)S(1)} %get-tuple-element.17, f32[768]{0:T(1024)S(1)} %get-tuple-element.15), kind=kLoop, calls=%fused_computation.13 | loop fusion | flops 2359296 | bytes 3151872 | tf_op jit(solution)/shard_map/convert_element_type | solution.py:200
  161.9 1.8 collective-permute-start.8
  163.7 1.5 fusion.3.own_grad_ref
  165.2 10.4 %shard_map.52 = bf16[2304,512]{1,0:T(8,128)(2,1)} custom-call(bf16[768,2304]{1,0:T(8,128)(2,1)} %bitcast.9.state_ref.own_ref, bf16[768,2304]{1,0:T(8,128)(2,1)} %collective-permute-done.7.state_ref.other_ref, bf16[768,512]{1,0:T(8,128)(2,1)} %fusion.3.own_grad_ref, bf16[768,512]{1,0:T(8,128)(2,1)} %fusion.7.other_grad_ref), custom_call_target="tpu_custom_call" | custom-call | flops 3623878656 | bytes 7077888 | tf_op jit(solution)/shard_map/pallas_call | solution.py:139
  175.6 1.6 constant_dynamic-slice_fusion
  177.2 2.1 constant_dynamic-slice_fusion.1
  179.3 6.3 %shard_map.54 = bf16[192,2304]{1,0:T(8,128)(2,1)} custom-call(bf16[192,512]{1,0:T(8,128)(2,1)} %bitcast.106, bf16[192,512]{1,0:T(8,128)(2,1)} %bitcast.107, bf16[2304,512]{1,0:T(8,128)(2,1)} %bitcast.93, bf16[2304,512]{1,0:T(8,128)(2,1)} %collective-permute-done.9.far_ref), custom_call_target="tpu_custom_call" | custom-call | flops 905969664 | bytes 4718592 | tf_op jit(solution)/shard_map/pallas_call | solution.py:116
  185.6 1.2 fusion.17
  187.4 2.2 collective-permute-start.12
  189.6 0.9 pad_maximum_fusion.2.mine_ref
  190.5 0.9 pad_maximum_fusion.3.other_ref
  191.3 8.2 %shard_map.53 = bf16[576,2304]{1,0:T(8,128)(2,1)} custom-call(bf16[576,512]{1,0:T(8,128)(2,1)} %pad_maximum_fusion.2.mine_ref, bf16[576,512]{1,0:T(8,128)(2,1)} %pad_maximum_fusion.3.other_ref, bf16[2304,512]{1,0:T(8,128)(2,1)} %bitcast.94, bf16[2304,512]{1,0:T(8,128)(2,1)} %collective-permute-done.9.far_ref), custom_call_target="tpu_custom_call" | custom-call | flops 2717908992 | bytes 4718592 | tf_op jit(solution)/shard_map/pallas_call | solution.py:116
  199.9 1.6 slice_add_fusion.1
  201.5 2.5 collective-permute-start.13
  204.0 18.0 %collective-permute-done.13 = bf16[192,2304]{1,0:T(8,128)(2,1)S(1)} collective-permute-done((bf16[192,2304]{1,0:T(8,128)(2,1)S(1)}, bf16[192,2304]{1,0:T(8,128)(2,1)S(1)}, u32[]{:S(2)}, u32[]{:S(2)}) %collective-permute-start.13) | collective-permute-done | bytes 884768 | tf_op jit(solution)/shard_map/ppermute | solution.py:17
  221.9 3.0 %collective-permute-done.11 = bf16[192,2304]{1,0:T(8,128)(2,1)S(1)} collective-permute-done((bf16[192,2304]{1,0:T(8,128)(2,1)S(1)}, bf16[192,2304]{1,0:T(8,128)(2,1)S(1)}, u32[]{:S(2)}, u32[]{:S(2)}) %collective-permute-start.11) | collective-permute-done | bytes 884768 | tf_op jit(solution)/shard_map/ppermute | solution.py:17
  225.0 1.5 add_convert_fusion
  226.5 13.5 %all_to_all.38 = bf16[4,48,2304]{2,1,0:T(8,128)(2,1)S(1)} all-to-all(bf16[4,48,2304]{2,1,0:T(8,128)(2,1)S(1)} %bitcast.97), channel_id=1, replica_groups=mesh['layer'=4,'row'=8,'col'=8] {'layer'}, dimensions={0} | all-to-all | bytes 1769472 | tf_op jit(solution)/shard_map/all_to_all | solution.py:227
  240.0 3.6 %all-to-all-start.3 = ((bf16[4,576,512]{2,1,0:T(8,128)(2,1)}), bf16[4,576,512]{2,1,0:T(8,128)(2,1)S(1)}, u32[]{:S(2)}, u32[]{:S(2)}) async-start(bf16[4,576,512]{2,1,0:T(8,128)(2,1)} %bitcast.101), calls=%async_computation.3 | async-start | bytes 4718592 | tf_op jit(solution)/shard_map/all_to_all | solution.py:221
  243.8 0.8 reshape.158
  244.6 25.1 %all-to-all-done.3 = bf16[4,576,512]{2,1,0:T(8,128)(2,1)S(1)} async-done(((bf16[4,576,512]{2,1,0:T(8,128)(2,1)}), bf16[4,576,512]{2,1,0:T(8,128)(2,1)S(1)}, u32[]{:S(2)}, u32[]{:S(2)}) %all-to-all-start.3) | async-done | bytes 2359328 | tf_op jit(solution)/shard_map/all_to_all | solution.py:221
  269.7 3.4 %all-to-all-start.5 = ((bf16[8,6,2304]{2,1,0:T(8,128)(2,1)}), bf16[8,6,2304]{2,1,0:T(8,128)(2,1)S(1)}, u32[]{:S(2)}, u32[]{:S(2)}) async-start(bf16[8,6,2304]{2,1,0:T(8,128)(2,1)} %reshape.158), calls=%async_computation.5 | async-start | bytes 589824 | tf_op jit(solution)/shard_map/all_to_all | solution.py:230
  273.3 2.8 convert_bitcast_fusion
  276.1 6.7 %all-to-all-done.5 = bf16[8,6,2304]{2,1,0:T(8,128)(2,1)S(1)} async-done(((bf16[8,6,2304]{2,1,0:T(8,128)(2,1)}), bf16[8,6,2304]{2,1,0:T(8,128)(2,1)S(1)}, u32[]{:S(2)}, u32[]{:S(2)}) %all-to-all-start.5) | async-done | bytes 221216 | tf_op jit(solution)/shard_map/all_to_all | solution.py:230
  (71 shorter events, 5.9 us)
Async XLA Ops:
  0.6 11.1 %collective-permute-start = (bf16[48,2304]{1,0:T(8,128)(2,1)}, bf16[48,2304]{1,0:T(8,128)(2,1)}, u32[]{:S(2)}, u32[]{:S(2)}) collective-permute-start(bf16[48,2304]{1,0:T(8,128)(2,1)} %param.3), channel_id=1, source_target_pairs={{0,64},{64,128},{128,192},{192,0},{1,65},{65,129},{129,193},{193,1... | collective-permute-start | bytes 663560 | tf_op jit(solution)/shard_map/ppermute | solution.py:12
  2.8 10.6 %collective-permute-start.1 = (bf16[48,2304]{1,0:T(8,128)(2,1)}, bf16[48,2304]{1,0:T(8,128)(2,1)}, u32[]{:S(2)}, u32[]{:S(2)}) collective-permute-start(bf16[48,2304]{1,0:T(8,128)(2,1)} %param.3), channel_id=1, source_target_pairs={{0,192},{64,0},{128,64},{192,128},{1,193},{65,1},{129,65},{193,129... | collective-permute-start | bytes 663560 | tf_op jit(solution)/shard_map/ppermute | solution.py:12
  4.4 11.0 %collective-permute-start.2 = (bf16[48,2304]{1,0:T(8,128)(2,1)}, bf16[48,2304]{1,0:T(8,128)(2,1)}, u32[]{:S(2)}, u32[]{:S(2)}) collective-permute-start(bf16[48,2304]{1,0:T(8,128)(2,1)} %param.3), channel_id=1, source_target_pairs={{0,128},{64,192},{128,0},{192,64},{1,129},{65,193},{129,1},{193,65... | collective-permute-start | bytes 663560 | tf_op jit(solution)/shard_map/ppermute | solution.py:12
  5.9 4.0 %copy-start.11 = (bf16[48,2304]{1,0:T(8,128)(2,1)S(1)}, bf16[48,2304]{1,0:T(8,128)(2,1)}, u32[]{:S(2)}) copy-start(bf16[48,2304]{1,0:T(8,128)(2,1)} %param.3) | copy-start | bytes 663556
  5.9 4.7 %copy-start = (bf16[384,2048]{1,0:T(8,128)(2,1)S(1)}, bf16[384,2048]{1,0:T(8,128)(2,1)}, u32[]{:S(2)}) copy-start(bf16[384,2048]{1,0:T(8,128)(2,1)} %param.5) | copy-start | bytes 4718596
  11.6 8.0 %copy-start.6 = (bf16[384,512]{1,0:T(8,128)(2,1)S(1)}, bf16[384,512]{1,0:T(8,128)(2,1)}, u32[]{:S(2)}) copy-start(bf16[384,512]{1,0:T(8,128)(2,1)} %get-tuple-element.32) | copy-start | bytes 1179652
  17.0 24.4 %collective-permute-start.3 = (bf16[192,2304]{1,0:T(8,128)(2,1)}, bf16[192,2304]{1,0:T(8,128)(2,1)}, u32[]{:S(2)}, u32[]{:S(2)}) collective-permute-start(bf16[192,2304]{1,0:T(8,128)(2,1)} %bitcast.5), channel_id=1, source_target_pairs={{0,16},{8,24},{16,32},{24,40},{32,48},{40,56},{48,0},{56,8},{1,17}... | collective-permute-start | bytes 2654216 | tf_op jit(solution)/shard_map/ppermute | solution.py:17
  18.2 19.7 %collective-permute-start.4 = (bf16[192,2304]{1,0:T(8,128)(2,1)}, bf16[192,2304]{1,0:T(8,128)(2,1)}, u32[]{:S(2)}, u32[]{:S(2)}) collective-permute-start(bf16[192,2304]{1,0:T(8,128)(2,1)} %bitcast.5), channel_id=1, source_target_pairs={{0,48},{8,56},{16,0},{24,8},{32,16},{40,24},{48,32},{56,40},{1,49}... | collective-permute-start | bytes 2654216 | tf_op jit(solution)/shard_map/ppermute | solution.py:17
  39.0 9.1 %collective-permute-start.6 = (bf16[96,2304]{1,0:T(8,128)(2,1)S(1)}, bf16[96,2304]{1,0:T(8,128)(2,1)S(1)}, u32[]{:S(2)}, u32[]{:S(2)}) collective-permute-start(bf16[96,2304]{1,0:T(8,128)(2,1)S(1)} %slice.93), channel_id=1, source_target_pairs={{0,48},{8,56},{16,0},{24,8},{32,16},{40,24},{48,32},{56,40},{1,49}... | collective-permute-start | bytes 1327112 | tf_op jit(solution)/shard_map/ppermute | solution.py:17
  42.4 9.7 %collective-permute-start.5 = (bf16[96,2304]{1,0:T(8,128)(2,1)S(1)}, bf16[96,2304]{1,0:T(8,128)(2,1)S(1)}, u32[]{:S(2)}, u32[]{:S(2)}) collective-permute-start(bf16[96,2304]{1,0:T(8,128)(2,1)S(1)} %slice.92), channel_id=1, source_target_pairs={{0,16},{8,24},{16,32},{24,40},{32,48},{40,56},{48,0},{56,8},{1,17}... | collective-permute-start | bytes 1327112 | tf_op jit(solution)/shard_map/ppermute | solution.py:17
  46.8 10.5 %copy-start.3 = (bf16[576,512]{1,0:T(8,128)(2,1)S(1)}, bf16[576,512]{1,0:T(8,128)(2,1)}, u32[]{:S(2)}) copy-start(bf16[576,512]{1,0:T(8,128)(2,1)} %get-tuple-element.24) | copy-start | bytes 1769476
  46.8 10.5 %copy-start.5 = (bf16[384,512]{1,0:T(8,128)(2,1)S(1)}, bf16[384,512]{1,0:T(8,128)(2,1)}, u32[]{:S(2)}) copy-start(bf16[384,512]{1,0:T(8,128)(2,1)} %get-tuple-element.30) | copy-start | bytes 1179652
  53.2 67.3 %collective-permute-start.7 = (bf16[768,2304]{1,0:T(8,128)(2,1)}, bf16[768,2304]{1,0:T(8,128)(2,1)}, u32[]{:S(2)}, u32[]{:S(2)}) collective-permute-start(bf16[768,2304]{1,0:T(8,128)(2,1)} %bitcast.9.state_ref.own_ref), channel_id=1, source_target_pairs={{0,8},{8,0},{16,24},{24,16},{32,40},{40,32},{48,56},{56,48},{1,9},... | collective-permute-start | bytes 10616840 | tf_op jit(solution)/shard_map/ppermute | solution.py:22
  59.6 50.9 %all-to-all-start = ((bf16[4,960,512]{2,1,0:T(8,128)(2,1)}), bf16[4,960,512]{2,1,0:T(8,128)(2,1)}, u32[]{:S(2)}, u32[]{:S(2)}) async-start(bf16[4,960,512]{2,1,0:T(8,128)(2,1)} %pad_maximum_fusion), calls=%async_computation | async-start | bytes 7864320 | tf_op jit(solution)/shard_map/all_to_all | solution.py:173
  120.5 12.1 %copy-start.1 = (bf16[4,576,512]{2,1,0:T(8,128)(2,1)S(1)}, bf16[4,576,512]{2,1,0:T(8,128)(2,1)}, u32[]{:S(2)}) copy-start(bf16[4,576,512]{2,1,0:T(8,128)(2,1)} %slice.98) | copy-start | bytes 7077892
  128.2 13.2 %all-to-all-start.1 = ((f32[32,1,1920]{2,1,0:T(1,128)}), f32[32,1,1920]{2,1,0:T(1,128)S(1)}, u32[]{:S(2)}, u32[]{:S(2)}) async-start(f32[32,1,1920]{2,1,0:T(1,128)} %broadcast_in_dim.22), calls=%async_computation.1 | async-start | bytes 491520 | tf_op jit(solution)/shard_map/all_to_all | solution.py:57
  132.6 46.7 %collective-permute-start.9 = (bf16[2304,512]{1,0:T(8,128)(2,1)S(1)}, bf16[2304,512]{1,0:T(8,128)(2,1)}, u32[]{:S(2)}, u32[]{:S(2)}) collective-permute-start(bf16[2304,512]{1,0:T(8,128)(2,1)S(1)} %bitcast.95), channel_id=1, source_target_pairs={{0,8},{8,0},{16,24},{24,16},{32,40},{40,32},{48,56},{56,48},{1,9},... | collective-permute-start | bytes 7077896 | tf_op jit(solution)/shard_map/ppermute | solution.py:22
  142.3 16.1 %all-to-all-start.2 = ((f32[8,1,3072]{2,1,0:T(1,128)}), f32[8,1,3072]{2,1,0:T(1,128)S(1)}, u32[]{:S(2)}, u32[]{:S(2)}) async-start(f32[8,1,3072]{2,1,0:T(1,128)} %broadcast_in_dim.46), calls=%async_computation.2 | async-start | bytes 196608 | tf_op jit(solution)/shard_map/all_to_all | solution.py:57
  158.7 5.0 %copy-start.4 = (f32[768,512]{1,0:T(8,128)S(1)}, f32[768,512]{1,0:T(8,128)}, u32[]{:S(2)}) copy-start(f32[768,512]{1,0:T(8,128)} %get-tuple-element.11) | copy-start | bytes 4718596
  161.9 13.7 %collective-permute-start.8 = (bf16[768,512]{1,0:T(8,128)(2,1)}, bf16[768,512]{1,0:T(8,128)(2,1)}, u32[]{:S(2)}, u32[]{:S(2)}) collective-permute-start(bf16[768,512]{1,0:T(8,128)(2,1)} %fusion.7.other_grad_ref), channel_id=1, source_target_pairs={{0,8},{8,0},{16,24},{24,16},{32,40},{40,32},{48,56},{56,48},{1,9},... | collective-permute-start | bytes 2359304 | tf_op jit(solution)/shard_map/ppermute | solution.py:22
  165.2 12.0 %copy-start.2 = (bf16[768,512]{1,0:T(8,128)(2,1)S(1)}, bf16[768,512]{1,0:T(8,128)(2,1)}, u32[]{:S(2)}) copy-start(bf16[768,512]{1,0:T(8,128)(2,1)} %fusion.3.own_grad_ref) | copy-start | bytes 2359300
  179.3 10.3 %copy-start.8 = (bf16[4,1,48,512]{3,2,1,0:T(8,128)(2,1)S(1)}, bf16[4,1,48,512]{3,2,1,0:T(8,128)(2,1)}, u32[]{:S(2)}) copy-start(bf16[4,1,48,512]{3,2,1,0:T(8,128)(2,1)} %get-tuple-element.37) | copy-start | bytes 589828
  179.3 10.3 %copy-start.9 = (bf16[4,1,48,512]{3,2,1,0:T(8,128)(2,1)S(1)}, bf16[4,1,48,512]{3,2,1,0:T(8,128)(2,1)}, u32[]{:S(2)}) copy-start(bf16[4,1,48,512]{3,2,1,0:T(8,128)(2,1)} %get-tuple-element.38) | copy-start | bytes 589828
  179.3 10.3 %copy-start.10 = (bf16[4,1,48,512]{3,2,1,0:T(8,128)(2,1)S(1)}, bf16[4,1,48,512]{3,2,1,0:T(8,128)(2,1)}, u32[]{:S(2)}) copy-start(bf16[4,1,48,512]{3,2,1,0:T(8,128)(2,1)} %get-tuple-element.39) | copy-start | bytes 589828
  185.6 4.9 %copy-start.7 = (bf16[4,1,48,512]{3,2,1,0:T(8,128)(2,1)S(1)}, bf16[4,1,48,512]{3,2,1,0:T(8,128)(2,1)}, u32[]{:S(2)}) copy-start(bf16[4,1,48,512]{3,2,1,0:T(8,128)(2,1)} %get-tuple-element.47) | copy-start | bytes 589828
  186.9 13.0 %collective-permute-start.10 = (bf16[96,2304]{1,0:T(8,128)(2,1)S(1)}, bf16[96,2304]{1,0:T(8,128)(2,1)S(1)}, u32[]{:S(2)}, u32[]{:S(2)}) collective-permute-start(bf16[96,2304]{1,0:T(8,128)(2,1)S(1)} %get-tuple-element.34), channel_id=1, source_target_pairs={{0,16},{8,24},{16,32},{24,40},{32,48},{40,56},{48,0},{56,8},{1,17}... | collective-permute-start | bytes 1327112 | tf_op jit(solution)/shard_map/ppermute | solution.py:17
  187.4 12.5 %collective-permute-start.12 = (bf16[96,2304]{1,0:T(8,128)(2,1)S(1)}, bf16[96,2304]{1,0:T(8,128)(2,1)S(1)}, u32[]{:S(2)}, u32[]{:S(2)}) collective-permute-start(bf16[96,2304]{1,0:T(8,128)(2,1)S(1)} %get-tuple-element.35), channel_id=1, source_target_pairs={{0,48},{8,56},{16,0},{24,8},{32,16},{40,24},{48,32},{56,40},{1,49}... | collective-permute-start | bytes 1327112 | tf_op jit(solution)/shard_map/ppermute | solution.py:17
  201.5 20.4 %collective-permute-start.13 = (bf16[192,2304]{1,0:T(8,128)(2,1)S(1)}, bf16[192,2304]{1,0:T(8,128)(2,1)S(1)}, u32[]{:S(2)}, u32[]{:S(2)}) collective-permute-start(bf16[192,2304]{1,0:T(8,128)(2,1)S(1)} %get-tuple-element.19), channel_id=1, source_target_pairs={{0,48},{8,56},{16,0},{24,8},{32,16},{40,24},{48,32},{56,40},{1,49}... | collective-permute-start | bytes 2654216 | tf_op jit(solution)/shard_map/ppermute | solution.py:17
  204.0 21.0 %collective-permute-start.11 = (bf16[192,2304]{1,0:T(8,128)(2,1)S(1)}, bf16[192,2304]{1,0:T(8,128)(2,1)S(1)}, u32[]{:S(2)}, u32[]{:S(2)}) collective-permute-start(bf16[192,2304]{1,0:T(8,128)(2,1)S(1)} %get-tuple-element.18), channel_id=1, source_target_pairs={{0,16},{8,24},{16,32},{24,40},{32,48},{40,56},{48,0},{56,8},{1,17}... | collective-permute-start | bytes 2654216 | tf_op jit(solution)/shard_map/ppermute | solution.py:17
  240.0 29.7 %all-to-all-start.3 = ((bf16[4,576,512]{2,1,0:T(8,128)(2,1)}), bf16[4,576,512]{2,1,0:T(8,128)(2,1)S(1)}, u32[]{:S(2)}, u32[]{:S(2)}) async-start(bf16[4,576,512]{2,1,0:T(8,128)(2,1)} %bitcast.101), calls=%async_computation.3 | async-start | bytes 4718592 | tf_op jit(solution)/shard_map/all_to_all | solution.py:221
  269.7 13.1 %all-to-all-start.5 = ((bf16[8,6,2304]{2,1,0:T(8,128)(2,1)}), bf16[8,6,2304]{2,1,0:T(8,128)(2,1)S(1)}, u32[]{:S(2)}, u32[]{:S(2)}) async-start(bf16[8,6,2304]{2,1,0:T(8,128)(2,1)} %reshape.158), calls=%async_computation.5 | async-start | bytes 589824 | tf_op jit(solution)/shard_map/all_to_all | solution.py:230

commit v4 on v2

--- a/solution.py
+++ b/solution.py
@@ -1,6 +1,7 @@
 import jax
 import jax.numpy as jnp
 from jax import lax
+from jax.experimental.layout import Layout, with_layout_constraint
 from jax.sharding import PartitionSpec as P
 
 LOSS_SCALE = 256
@@ -88,16 +89,18 @@
     sent = lax.all_to_all(jnp.stack(sent), "layer", 0, 0, tiled=True)
     table = sent[:, :quarter].reshape(width, block)
     taught = sent[:, quarter:].reshape(layers, xs, 2, strip, block)
+    taught = [at(taught, c, 2).reshape(half, block) for c in (core, 1 - core)]
 
-    own = jnp.zeros((xs, layers * strip, width), bf16)
+    own = jnp.zeros((layers, xs, strip, width), bf16)
     pieces = ring_gather(mine.reshape(layers * strip, width), shift_x)
     for k, p in pieces:
-        own = put(own, p, (x + k) % xs)
+        own = put(own, p.reshape(layers, strip, width), (x + k) % xs, 1)
     own = own.reshape(half, width)
     other = swap_core(own)
 
     states = jnp.concatenate([own, other])
     logits = jnp.dot(states, table, preferred_element_type=f32)
+    logits = with_layout_constraint(logits, Layout((0, 1)))
     lse_s = logsum(logits, 1)
     lse_s = ordered(core, lse_s[:half], lse_s[half:])
     lse_t = logsum(teacher.astype(f32), 1)
@@ -107,30 +110,33 @@
     got = spread(jnp.concatenate([lse_s, lse_t.reshape(2 * half)]), "col")
     lse_s, lse_t = jnp.split(logsum(got, 0), 2)
     lse_s = lse_s.reshape(2, half)
-    lse_t = lse_t.reshape(layers, xs, 2, strip).transpose(2, 1, 0, 3).reshape(2, half)
+    lse_t = lse_t.reshape(layers * xs, 2, strip).swapaxes(0, 1).reshape(2, half)
 
-    def gradient(logits, c):
-        taught_c = at(taught, c, 2).swapaxes(0, 1).reshape(half, block).astype(f32)
+    def gradient(logits, taught_c, c):
+        taught_c = taught_c.astype(f32)
         prob_s = jnp.exp(logits - at(lse_s, c)[:, None])
         prob_t = jnp.exp(taught_c - at(lse_t, c)[:, None])
         return ((prob_s - prob_t) * LOSS_SCALE).astype(bf16)
 
-    grads_other = gradient(logits[half:], 1 - core)
+    grads_other = gradient(logits[half:], taught[1], 1 - core)
     crossed = swap_core(grads_other)
-    grads_own = gradient(logits[:half], core)
+    grads_own = gradient(logits[:half], taught[0], core)
     other_table = swap_core(table)
 
-    both = jnp.concatenate([grads_own, crossed], axis=1).reshape(xs, layers * strip, 2 * block)
+
+    both = jnp.concatenate([grads_own, crossed], axis=1)
+    both = both.reshape(layers, xs, strip, 2 * block)
     tables = jnp.concatenate([table, other_table], axis=1)
 
     def part(*ks):
-        lines = jnp.concatenate([at(both, (x + k) % xs) for k in ks])
+        picked = [at(both, (x + k) % xs, 1).reshape(layers * strip, 2 * block) for k in ks]
         return lax.dot_general(
-            lines, tables, (((1,), (1,)), ((), ())), preferred_element_type=f32
+            jnp.concatenate(picked), tables, (((1,), (1,)), ((), ())), preferred_element_type=f32
         ).astype(bf16)
 
+    far = ring_sum_far(part(2), shift_x)
+
     grads = jnp.concatenate([grads_own, grads_other])
-    far = ring_sum_far(part(2), shift_x)
     grad_table = lax.dot_general(
         states, grads, (((0,), (0,)), ((), ())), preferred_element_type=f32
     ).astype(bf16)
@@ -141,11 +147,8 @@
 
     ahead, behind, here = jnp.split(lax.optimization_barrier(part(1, 3, 0)), 3)
     summed = ring_sum(here, ahead, behind, far, shift_x).astype(bf16)
-    summed = summed.reshape(layers, strip, width)
-    summed = lax.all_to_all(summed, "layer", 0, 0, tiled=True)
-    summed = jnp.sum(summed.astype(f32), axis=0).astype(bf16)
-    summed = summed.reshape(cols, strip // cols, width)
-    summed = lax.all_to_all(summed, "col", 0, 0, tiled=True)
+    summed = summed.reshape(layers * cols, strip // cols, width)
+    summed = lax.all_to_all(summed, ("layer", "col"), 0, 0, tiled=True)
     grad_hidden = jnp.sum(summed.astype(f32), axis=0)
     return grad_table.T, grad_hidden
 

time: 275 us -> 246 us (0.89)
  the two profiles are of different devices: /device:TPU:1 before, /device:TPU:32 now
where the time goes in v4:
time: 246 us; the launch traced here: 245 us
  waiting for transfers between devices  135 us (55%)
  starting transfers between devices  41.2 us (17%)
  matrix products  24.2 us (10%)
  local copies, waits for them, and re-layouts  19.1 us (8%)
  other arithmetic  12.5 us (5%)
  blocking collectives  11.6 us (5%)
    ppermute x8, waiting for transfers between devices, shift_x(): return lax.ppermute(x, 'row', [(i, (i + 2 * s) % n) for i in range(n)])  51.8 us
    all_to_all x1, waiting for transfers between devices, local(): sent = lax.all_to_all(jnp.stack(sent), 'layer', 0, 0, tiled=True)  45.8 us
    all_to_all x1, waiting for transfers between devices, local(): summed = lax.all_to_all(summed, ('layer', 'col'), 0, 0, tiled=True)  26.8 us
    ppermute x8, starting transfers between devices, shift_x(): return lax.ppermute(x, 'row', [(i, (i + 2 * s) % n) for i in range(n)])  12.8 us
    all_to_all x1, blocking collectives, spread(): lax.all_to_all(jnp.broadcast_to(x[None], (n, *x.shape)), axis, 0, 0, tile...  11.6 us
    all_to_all x1, starting transfers between devices, spread(): lax.all_to_all(jnp.broadcast_to(x[None], (n, *x.shape)), axis, 0, 0, tile...  8.57 us
    dot_general x1, matrix products, local(): lax.dot_general(states, grads, (((0,), (0,)), ((), ())), preferred_elemen...  8.36 us
    dot_general x2, matrix products, part(): lax.dot_general(jnp.concatenate(picked), tables, (((1,), (1,)), ((), ()))...  7.97 us
  transfers between devices with their start and end apart: 18, of which 12 were waited for; matrix products, arithmetic and copies ran while one was open for 18% of the time, Pallas kernels for 0%

profile of v4, /device:TPU:32, one launch (start us, length us, event | category | flops | bytes accessed | tf_op | source)
XLA Modules:
  0.0 245.0 jit_solution(7817638931104516696)
XLA Ops:
  0.6 1.7 collective-permute-start
  2.3 1.7 collective-permute-start.1
  3.9 2.0 collective-permute-start.2
  6.0 1.0 bitcast_dynamic-update-slice_fusion.4
  7.0 1.9 fusion.32
  8.9 0.5 collective-permute-done
  9.4 4.2 %collective-permute-done.1 = bf16[48,2304]{1,0:T(8,128)(2,1)S(1)} collective-permute-done((bf16[48,2304]{1,0:T(8,128)(2,1)}, bf16[48,2304]{1,0:T(8,128)(2,1)S(1)}, u32[]{:S(2)}, u32[]{:S(2)}) %collective-permute-start.1) | collective-permute-done | bytes 221216 | tf_op jit(solution)/shard_map/ppermute | solution.py:12
  13.6 1.7 collective-permute-done.2
  15.3 1.6 collective-permute-start.3
  16.9 1.7 collective-permute-start.4
  18.6 0.1 fusion.33
  18.8 2.1 broadcast_in_dim.16
  20.9 1.0 bitcast_dynamic-update-slice_fusion
  21.9 15.2 %collective-permute-done.4 = bf16[192,2304]{1,0:T(8,128)(2,1)S(1)} collective-permute-done((bf16[192,2304]{1,0:T(8,128)(2,1)S(1)}, bf16[192,2304]{1,0:T(8,128)(2,1)S(1)}, u32[]{:S(2)}, u32[]{:S(2)}) %collective-permute-start.4) | collective-permute-done | bytes 884768 | tf_op jit(solution)/shard_map/ppermute | solution.py:17
  37.2 3.0 %collective-permute-start.6 = (bf16[96,2304]{1,0:T(8,128)(2,1)S(1)}, bf16[96,2304]{1,0:T(8,128)(2,1)S(1)}, u32[]{:S(2)}, u32[]{:S(2)}) collective-permute-start(bf16[96,2304]{1,0:T(8,128)(2,1)S(1)} %slice.101), channel_id=1, source_target_pairs={{0,48},{8,56},{16,0},{24,8},{32,16},{40,24},{48,32},{56,40},{1,49}... | collective-permute-start | bytes 1327112 | tf_op jit(solution)/shard_map/ppermute | solution.py:17
  40.2 0.1 collective-permute-start.5
  40.3 1.0 constant_dynamic-update-slice_fusion.2
  41.4 1.0 constant_dynamic-update-slice_fusion.1
  42.3 5.3 %collective-permute-done.6 = bf16[96,2304]{1,0:T(8,128)(2,1)S(1)} collective-permute-done((bf16[96,2304]{1,0:T(8,128)(2,1)S(1)}, bf16[96,2304]{1,0:T(8,128)(2,1)S(1)}, u32[]{:S(2)}, u32[]{:S(2)}) %collective-permute-start.6) | collective-permute-done | bytes 442400 | tf_op jit(solution)/shard_map/ppermute | solution.py:17
  47.6 3.5 %collective-permute-done.5 = bf16[96,2304]{1,0:T(8,128)(2,1)S(1)} collective-permute-done((bf16[96,2304]{1,0:T(8,128)(2,1)S(1)}, bf16[96,2304]{1,0:T(8,128)(2,1)S(1)}, u32[]{:S(2)}, u32[]{:S(2)}) %collective-permute-start.5) | collective-permute-done | bytes 442400 | tf_op jit(solution)/shard_map/ppermute | solution.py:17
  51.2 1.0 constant_dynamic-update-slice_fusion
  52.2 0.1 maximum_bitcast_fusion.2
  52.4 0.1 maximum_bitcast_fusion
  52.5 2.2 pad_maximum_fusion.6
  54.7 5.0 %all-to-all-start = ((bf16[4,960,512]{2,1,0:T(8,128)(2,1)}), bf16[4,960,512]{2,1,0:T(8,128)(2,1)}, u32[]{:S(2)}, u32[]{:S(2)}) async-start(bf16[4,960,512]{2,1,0:T(8,128)(2,1)} %pad_maximum_fusion.6), calls=%async_computation | async-start | bytes 7864320 | tf_op jit(solution)/shard_map/all_to_all | solution.py:89
  59.7 0.3 reduce_max.51
  60.0 0.7 exponential_reduce_fusion
  60.6 45.8 %all-to-all-done = bf16[4,960,512]{2,1,0:T(8,128)(2,1)} async-done(((bf16[4,960,512]{2,1,0:T(8,128)(2,1)}), bf16[4,960,512]{2,1,0:T(8,128)(2,1)}, u32[]{:S(2)}, u32[]{:S(2)}) %all-to-all-start) | async-done | bytes 3932192 | tf_op jit(solution)/shard_map/all_to_all | solution.py:89
  106.5 1.8 slice.106
  108.3 7.8 %fusion.37 = (f32[1536]{0:T(1024)S(1)}, f32[1536,512]{1,0:T(8,128)S(1)}) fusion(bf16[2304,512]{1,0:T(8,128)(2,1)S(1)} %bitcast.77, bf16[768,2304]{1,0:T(8,128)(2,1)} %collective-permute-done.7, bf16[768,2304]{1,0:T(8,128)(2,1)} %bitcast.9), kind=kOutput, calls=%fused_computation.95 | convolution fusion | flops 3638819328 | bytes 12589056 | tf_op jit(solution)/shard_map/dot_general | solution.py:102
  116.2 0.8 exponential_reduce_fusion.1
  117.1 0.1 broadcast_in_dim.22
  117.3 11.6 %all_to_all.33 = f32[32,1,1920]{2,1,0:T(1,128)S(1)} all-to-all(f32[32,1,1920]{2,1,0:T(1,128)S(1)} %broadcast_in_dim.22), channel_id=1, replica_groups=mesh['layer'=4,'row'=8,'col'=8] {'layer','row'}, dimensions={0} | all-to-all | bytes 491520 | tf_op jit(solution)/shard_map/all_to_all | solution.py:57
  129.1 0.7 broadcast_in_dim.23
  129.8 8.6 %all-to-all-start.2 = ((f32[8,1,3072]{2,1,0:T(1,128)}), f32[8,1,3072]{2,1,0:T(1,128)S(1)}, u32[]{:S(2)}, u32[]{:S(2)}) async-start(f32[8,1,3072]{2,1,0:T(1,128)} %broadcast_in_dim.23), calls=%async_computation.2 | async-start | bytes 196608 | tf_op jit(solution)/shard_map/all_to_all | solution.py:57
  138.3 1.5 slice.112
  139.9 1.2 constant_dynamic-slice_fusion.8
  141.1 4.7 %all-to-all-done.2 = f32[8,1,3072]{2,1,0:T(1,128)S(1)} async-done(((f32[8,1,3072]{2,1,0:T(1,128)}), f32[8,1,3072]{2,1,0:T(1,128)S(1)}, u32[]{:S(2)}, u32[]{:S(2)}) %all-to-all-start.2) | async-done | bytes 98336 | tf_op jit(solution)/shard_map/all_to_all | solution.py:57
  145.8 0.1 reduce_max.55
  146.0 0.1 split.22
  146.1 0.1 reshape.119
  146.2 2.3 fusion.10
  148.5 0.1 collective-permute-start.8
  148.6 8.4 %fusion.2 = bf16[2304,512]{1,0:T(8,128)(2,1)} fusion(bf16[768,2304]{1,0:T(8,128)(2,1)} %collective-permute-done.7, bf16[768,2304]{1,0:T(8,128)(2,1)} %bitcast.9, bf16[768,512]{1,0:T(8,128)(2,1)S(1)} %get-tuple-element.11, bf16[768,512]{1,0:T(8,128)(2,1)S(1)} %get-tuple-element.10), kind=kOutput, calls=%fused_computation.6 | convolution fusion | flops 3642359808 | bytes 11010048 | tf_op jit(solution)/shard_map/dot_general | solution.py:140
  157.0 1.4 pad_maximum_fusion.9
  158.4 3.9 %all-to-all-start.3 = ((bf16[4,576,512]{2,1,0:T(8,128)(2,1)}), bf16[4,576,512]{2,1,0:T(8,128)(2,1)S(1)}, u32[]{:S(2)}, u32[]{:S(2)}) async-start(bf16[4,576,512]{2,1,0:T(8,128)(2,1)} %bitcast.81), calls=%async_computation.3 | async-start | bytes 4718592 | tf_op jit(solution)/shard_map/all_to_all | solution.py:145
  162.3 1.2 constant_dynamic-slice_fusion
  163.4 1.3 constant_dynamic-slice_fusion.3
  164.8 3.4 %convolution_convert_fusion.1 = bf16[192,2304]{1,0:T(8,128)(2,1)S(1)} fusion(bf16[192,1024]{1,0:T(8,128)(2,1)S(1)} %bitcast.91, bf16[2304,512]{1,0:T(8,128)(2,1)} %collective-permute-done.9, bf16[2304,512]{1,0:T(8,128)(2,1)S(1)} %bitcast.79), kind=kOutput, calls=%fused_computation.8 | convolution fusion | flops 915849216 | bytes 5996544 | tf_op jit(solution)/shard_map/dot_general | solution.py:133
  168.2 0.8 collective-permute-start.10
  169.1 2.5 %collective-permute-start.12 = (bf16[96,2304]{1,0:T(8,128)(2,1)S(1)}, bf16[96,2304]{1,0:T(8,128)(2,1)S(1)}, u32[]{:S(2)}, u32[]{:S(2)}) collective-permute-start(bf16[96,2304]{1,0:T(8,128)(2,1)S(1)} %get-tuple-element.32), channel_id=1, source_target_pairs={{0,48},{8,56},{16,0},{24,8},{32,16},{40,24},{48,32},{56,40},{1,49}... | collective-permute-start | bytes 1327112 | tf_op jit(solution)/shard_map/ppermute | solution.py:17
  171.5 4.6 %convolution_convert_fusion = bf16[576,2304]{1,0:T(8,128)(2,1)S(1)} fusion(bf16[2304,512]{1,0:T(8,128)(2,1)} %collective-permute-done.9, bf16[2304,512]{1,0:T(8,128)(2,1)S(1)} %bitcast.80, bf16[192,1024]{1,0:T(8,128)(2,1)S(1)} %bitcast.89, bf16[192,1024]{1,0:T(8,128)(2,1)S(1)} %bitcast.90, bf16[192,1024]{1,0:T(8,128)(2,1)S(1)} %bitcast.88), kind=kOutput, calls=%fused_computation.3 | convolution fusion | flops 2732212224 | bytes 8552448 | tf_op jit(solution)/shard_map/dot_general | solution.py:133
  176.2 5.9 %collective-permute-done.10 = bf16[96,2304]{1,0:T(8,128)(2,1)S(1)} collective-permute-done((bf16[96,2304]{1,0:T(8,128)(2,1)S(1)}, bf16[96,2304]{1,0:T(8,128)(2,1)S(1)}, u32[]{:S(2)}, u32[]{:S(2)}) %collective-permute-start.10) | collective-permute-done | bytes 442400 | tf_op jit(solution)/shard_map/ppermute | solution.py:17
  182.1 0.2 slice_add_fusion.1
  182.3 3.0 %collective-permute-start.13 = (bf16[192,2304]{1,0:T(8,128)(2,1)S(1)}, bf16[192,2304]{1,0:T(8,128)(2,1)S(1)}, u32[]{:S(2)}, u32[]{:S(2)}) collective-permute-start(bf16[192,2304]{1,0:T(8,128)(2,1)S(1)} %get-tuple-element.13), channel_id=1, source_target_pairs={{0,48},{8,56},{16,0},{24,8},{32,16},{40,24},{48,32},{56,40},{1,49}... | collective-permute-start | bytes 2654216 | tf_op jit(solution)/shard_map/ppermute | solution.py:17
  185.3 18.4 %collective-permute-done.13 = bf16[192,2304]{1,0:T(8,128)(2,1)S(1)} collective-permute-done((bf16[192,2304]{1,0:T(8,128)(2,1)S(1)}, bf16[192,2304]{1,0:T(8,128)(2,1)S(1)}, u32[]{:S(2)}, u32[]{:S(2)}) %collective-permute-start.13) | collective-permute-done | bytes 884768 | tf_op jit(solution)/shard_map/ppermute | solution.py:17
  203.8 3.4 %collective-permute-done.11 = bf16[192,2304]{1,0:T(8,128)(2,1)S(1)} collective-permute-done((bf16[192,2304]{1,0:T(8,128)(2,1)S(1)}, bf16[192,2304]{1,0:T(8,128)(2,1)S(1)}, u32[]{:S(2)}, u32[]{:S(2)}) %collective-permute-start.11) | collective-permute-done | bytes 884768 | tf_op jit(solution)/shard_map/ppermute | solution.py:17
  207.2 0.3 add_convert_fusion
  207.5 1.3 reshape.126
  208.8 5.6 %all-to-all-start.4 = ((bf16[32,6,2304]{2,1,0:T(8,128)(2,1)}), bf16[32,6,2304]{2,1,0:T(8,128)(2,1)S(1)}, u32[]{:S(2)}, u32[]{:S(2)}) async-start(bf16[32,6,2304]{2,1,0:T(8,128)(2,1)} %reshape.126), calls=%async_computation.4 | async-start | bytes 2359296 | tf_op jit(solution)/shard_map/all_to_all | solution.py:151
  214.4 0.2 slice_bitcast_fusion.3
  214.6 2.8 %convert_bitcast_fusion = f32[2048,576]{0,1:T(8,128)} fusion(bf16[576,512]{1,0:T(8,128)(2,1)S(1)} %get-tuple-element.15, bf16[576,512]{1,0:T(8,128)(2,1)S(1)} %get-tuple-element.16, bf16[576,512]{1,0:T(8,128)(2,1)S(1)} %get-tuple-element.17, bf16[576,512]{1,0:T(8,128)(2,1)S(1)} %get-tuple-element.14), kind=kLoop, calls=%fused_computation.2 | loop fusion | flops 9437184 | bytes 7077888 | tf_op jit(solution)/shard_map/transpose | solution.py:153
  217.4 26.8 %all-to-all-done.4 = bf16[32,6,2304]{2,1,0:T(8,128)(2,1)S(1)} async-done(((bf16[32,6,2304]{2,1,0:T(8,128)(2,1)}), bf16[32,6,2304]{2,1,0:T(8,128)(2,1)S(1)}, u32[]{:S(2)}, u32[]{:S(2)}) %all-to-all-start.4) | async-done | bytes 884768 | tf_op jit(solution)/shard_map/all_to_all | solution.py:151
  244.1 0.9 convert_reduce_fusion
  (48 shorter events, 0.7 us)
Async XLA Ops:
  0.6 8.7 %collective-permute-start = (bf16[48,2304]{1,0:T(8,128)(2,1)}, bf16[48,2304]{1,0:T(8,128)(2,1)S(1)}, u32[]{:S(2)}, u32[]{:S(2)}) collective-permute-start(bf16[48,2304]{1,0:T(8,128)(2,1)} %param.3), channel_id=1, source_target_pairs={{0,64},{64,128},{128,192},{192,0},{1,65},{65,129},{129,193},{193,1... | collective-permute-start | bytes 663560 | tf_op jit(solution)/shard_map/ppermute | solution.py:12
  2.3 11.3 %collective-permute-start.1 = (bf16[48,2304]{1,0:T(8,128)(2,1)}, bf16[48,2304]{1,0:T(8,128)(2,1)S(1)}, u32[]{:S(2)}, u32[]{:S(2)}) collective-permute-start(bf16[48,2304]{1,0:T(8,128)(2,1)} %param.3), channel_id=1, source_target_pairs={{0,192},{64,0},{128,64},{192,128},{1,193},{65,1},{129,65},{193,129... | collective-permute-start | bytes 663560 | tf_op jit(solution)/shard_map/ppermute | solution.py:12
  3.9 11.3 %collective-permute-start.2 = (bf16[48,2304]{1,0:T(8,128)(2,1)}, bf16[48,2304]{1,0:T(8,128)(2,1)S(1)}, u32[]{:S(2)}, u32[]{:S(2)}) collective-permute-start(bf16[48,2304]{1,0:T(8,128)(2,1)} %param.3), channel_id=1, source_target_pairs={{0,128},{64,192},{128,0},{192,64},{1,129},{65,193},{129,1},{193,65... | collective-permute-start | bytes 663560 | tf_op jit(solution)/shard_map/ppermute | solution.py:12
  7.0 11.6 %copy-start = (bf16[384,2048]{1,0:T(8,128)(2,1)S(1)}, bf16[384,2048]{1,0:T(8,128)(2,1)}, u32[]{:S(2)}) copy-start(bf16[384,2048]{1,0:T(8,128)(2,1)} %param.5) | copy-start | bytes 4718596
  15.3 24.9 %collective-permute-start.3 = (bf16[192,2304]{1,0:T(8,128)(2,1)S(1)}, bf16[192,2304]{1,0:T(8,128)(2,1)S(1)}, u32[]{:S(2)}, u32[]{:S(2)}) collective-permute-start(bf16[192,2304]{1,0:T(8,128)(2,1)S(1)} %bitcast.74), channel_id=1, source_target_pairs={{0,16},{8,24},{16,32},{24,40},{32,48},{40,56},{48,0},{56,8},{1,17}... | collective-permute-start | bytes 2654216 | tf_op jit(solution)/shard_map/ppermute | solution.py:17
  16.9 20.3 %collective-permute-start.4 = (bf16[192,2304]{1,0:T(8,128)(2,1)S(1)}, bf16[192,2304]{1,0:T(8,128)(2,1)S(1)}, u32[]{:S(2)}, u32[]{:S(2)}) collective-permute-start(bf16[192,2304]{1,0:T(8,128)(2,1)S(1)} %bitcast.75), channel_id=1, source_target_pairs={{0,48},{8,56},{16,0},{24,8},{32,16},{40,24},{48,32},{56,40},{1,49}... | collective-permute-start | bytes 2654216 | tf_op jit(solution)/shard_map/ppermute | solution.py:17
  37.2 10.5 %collective-permute-start.6 = (bf16[96,2304]{1,0:T(8,128)(2,1)S(1)}, bf16[96,2304]{1,0:T(8,128)(2,1)S(1)}, u32[]{:S(2)}, u32[]{:S(2)}) collective-permute-start(bf16[96,2304]{1,0:T(8,128)(2,1)S(1)} %slice.101), channel_id=1, source_target_pairs={{0,48},{8,56},{16,0},{24,8},{32,16},{40,24},{48,32},{56,40},{1,49}... | collective-permute-start | bytes 1327112 | tf_op jit(solution)/shard_map/ppermute | solution.py:17
  40.2 10.9 %collective-permute-start.5 = (bf16[96,2304]{1,0:T(8,128)(2,1)S(1)}, bf16[96,2304]{1,0:T(8,128)(2,1)S(1)}, u32[]{:S(2)}, u32[]{:S(2)}) collective-permute-start(bf16[96,2304]{1,0:T(8,128)(2,1)S(1)} %slice.100), channel_id=1, source_target_pairs={{0,16},{8,24},{16,32},{24,40},{32,48},{40,56},{48,0},{56,8},{1,17}... | collective-permute-start | bytes 1327112 | tf_op jit(solution)/shard_map/ppermute | solution.py:17
  52.2 56.1 %collective-permute-start.7 = (bf16[768,2304]{1,0:T(8,128)(2,1)}, bf16[768,2304]{1,0:T(8,128)(2,1)}, u32[]{:S(2)}, u32[]{:S(2)}) collective-permute-start(bf16[768,2304]{1,0:T(8,128)(2,1)} %bitcast.9), channel_id=1, source_target_pairs={{0,8},{8,0},{16,24},{24,16},{32,40},{40,32},{48,56},{56,48},{1,9},... | collective-permute-start | bytes 10616840 | tf_op jit(solution)/shard_map/ppermute | solution.py:22
  54.7 51.8 %all-to-all-start = ((bf16[4,960,512]{2,1,0:T(8,128)(2,1)}), bf16[4,960,512]{2,1,0:T(8,128)(2,1)}, u32[]{:S(2)}, u32[]{:S(2)}) async-start(bf16[4,960,512]{2,1,0:T(8,128)(2,1)} %pad_maximum_fusion.6), calls=%async_computation | async-start | bytes 7864320 | tf_op jit(solution)/shard_map/all_to_all | solution.py:89
  108.3 7.9 %copy-start.1 = (bf16[4,576,512]{2,1,0:T(8,128)(2,1)}, bf16[4,576,512]{2,1,0:T(8,128)(2,1)S(1)}, u32[]{:S(2)}) copy-start(bf16[4,576,512]{2,1,0:T(8,128)(2,1)S(1)} %slice.106) | copy-start | bytes 7077892
  129.8 16.0 %all-to-all-start.2 = ((f32[8,1,3072]{2,1,0:T(1,128)}), f32[8,1,3072]{2,1,0:T(1,128)S(1)}, u32[]{:S(2)}, u32[]{:S(2)}) async-start(f32[8,1,3072]{2,1,0:T(1,128)} %broadcast_in_dim.23), calls=%async_computation.2 | async-start | bytes 196608 | tf_op jit(solution)/shard_map/all_to_all | solution.py:57
  138.3 26.4 %collective-permute-start.9 = (bf16[2304,512]{1,0:T(8,128)(2,1)}, bf16[2304,512]{1,0:T(8,128)(2,1)}, u32[]{:S(2)}, u32[]{:S(2)}) collective-permute-start(bf16[2304,512]{1,0:T(8,128)(2,1)} %bitcast.78), channel_id=1, source_target_pairs={{0,8},{8,0},{16,24},{24,16},{32,40},{40,32},{48,56},{56,48},{1,9},... | collective-permute-start | bytes 7077896 | tf_op jit(solution)/shard_map/ppermute | solution.py:22
  148.5 8.5 %collective-permute-start.8 = (bf16[768,512]{1,0:T(8,128)(2,1)S(1)}, bf16[768,512]{1,0:T(8,128)(2,1)S(1)}, u32[]{:S(2)}, u32[]{:S(2)}) collective-permute-start(bf16[768,512]{1,0:T(8,128)(2,1)S(1)} %get-tuple-element.11), channel_id=1, source_target_pairs={{0,8},{8,0},{16,24},{24,16},{32,40},{40,32},{48,56},{56,48},{1,9},... | collective-permute-start | bytes 2359304 | tf_op jit(solution)/shard_map/ppermute | solution.py:22
  158.4 50.4 %all-to-all-start.3 = ((bf16[4,576,512]{2,1,0:T(8,128)(2,1)}), bf16[4,576,512]{2,1,0:T(8,128)(2,1)S(1)}, u32[]{:S(2)}, u32[]{:S(2)}) async-start(bf16[4,576,512]{2,1,0:T(8,128)(2,1)} %bitcast.81), calls=%async_computation.3 | async-start | bytes 4718592 | tf_op jit(solution)/shard_map/all_to_all | solution.py:145
  162.2 2.5 %copy-start.2 = (bf16[4,576,512]{2,1,0:T(8,128)(2,1)S(1)}, bf16[4,576,512]{2,1,0:T(8,128)(2,1)}, u32[]{:S(2)}) copy-start(bf16[4,576,512]{2,1,0:T(8,128)(2,1)} %copy-done.1) | copy-start | bytes 7077892
  168.2 13.9 %collective-permute-start.10 = (bf16[96,2304]{1,0:T(8,128)(2,1)S(1)}, bf16[96,2304]{1,0:T(8,128)(2,1)S(1)}, u32[]{:S(2)}, u32[]{:S(2)}) collective-permute-start(bf16[96,2304]{1,0:T(8,128)(2,1)S(1)} %get-tuple-element.31), channel_id=1, source_target_pairs={{0,16},{8,24},{16,32},{24,40},{32,48},{40,56},{48,0},{56,8},{1,17}... | collective-permute-start | bytes 1327112 | tf_op jit(solution)/shard_map/ppermute | solution.py:17
  169.1 13.0 %collective-permute-start.12 = (bf16[96,2304]{1,0:T(8,128)(2,1)S(1)}, bf16[96,2304]{1,0:T(8,128)(2,1)S(1)}, u32[]{:S(2)}, u32[]{:S(2)}) collective-permute-start(bf16[96,2304]{1,0:T(8,128)(2,1)S(1)} %get-tuple-element.32), channel_id=1, source_target_pairs={{0,48},{8,56},{16,0},{24,8},{32,16},{40,24},{48,32},{56,40},{1,49}... | collective-permute-start | bytes 1327112 | tf_op jit(solution)/shard_map/ppermute | solution.py:17
  182.3 21.5 %collective-permute-start.13 = (bf16[192,2304]{1,0:T(8,128)(2,1)S(1)}, bf16[192,2304]{1,0:T(8,128)(2,1)S(1)}, u32[]{:S(2)}, u32[]{:S(2)}) collective-permute-start(bf16[192,2304]{1,0:T(8,128)(2,1)S(1)} %get-tuple-element.13), channel_id=1, source_target_pairs={{0,48},{8,56},{16,0},{24,8},{32,16},{40,24},{48,32},{56,40},{1,49}... | collective-permute-start | bytes 2654216 | tf_op jit(solution)/shard_map/ppermute | solution.py:17
  185.3 21.8 %collective-permute-start.11 = (bf16[192,2304]{1,0:T(8,128)(2,1)S(1)}, bf16[192,2304]{1,0:T(8,128)(2,1)S(1)}, u32[]{:S(2)}, u32[]{:S(2)}) collective-permute-start(bf16[192,2304]{1,0:T(8,128)(2,1)S(1)} %get-tuple-element.12), channel_id=1, source_target_pairs={{0,16},{8,24},{16,32},{24,40},{32,48},{40,56},{48,0},{56,8},{1,17}... | collective-permute-start | bytes 2654216 | tf_op jit(solution)/shard_map/ppermute | solution.py:17
  208.8 35.3 %all-to-all-start.4 = ((bf16[32,6,2304]{2,1,0:T(8,128)(2,1)}), bf16[32,6,2304]{2,1,0:T(8,128)(2,1)S(1)}, u32[]{:S(2)}, u32[]{:S(2)}) async-start(bf16[32,6,2304]{2,1,0:T(8,128)(2,1)} %reshape.126), calls=%async_computation.4 | async-start | bytes 2359296 | tf_op jit(solution)/shard_map/all_to_all | solution.py:151

commit v5 on v4

--- a/solution.py
+++ b/solution.py
@@ -38,18 +38,27 @@
     return ((0, block), (3, back), (1, front), (2, jnp.concatenate(far)))
 
 
-def ring_sum_far(far, shift):
+def ring_exchange(piece, shift):
+    far = piece(2)
     half = far.shape[0] // 2
-    return shift(far[:half], 1), shift(far[half:], -1)
+    right, left = shift(far[:half], 1), shift(far[half:], -1)
+    back = shift(piece(1), 1)
+    front = shift(piece(3), -1)
+    far = (shift(right, 1), shift(left, -1))
+    return ((0, piece(0)), (3, back), (1, front), (2, jnp.concatenate(far)))
 
 
-def ring_sum(own, ahead, behind, far, shift):
-    right, left = far
-    none = jnp.zeros_like(right)
-    back = shift(ahead + jnp.concatenate([right, none]), 1)
-    front = shift(behind + jnp.concatenate([none, left]), -1)
+def ring_sum(parts, shift):
     f32 = jnp.float32
-    return own.astype(f32) + back.astype(f32) + front.astype(f32)
+    halves = lax.optimization_barrier(jnp.split(parts, 8))
+    far, ahead, behind, own = zip(halves[::2], halves[1::2])
+    right, left = shift(far[0], 1), shift(far[1], -1)
+    back_b = shift(ahead[1], 1)
+    front_a = shift(behind[0], -1)
+    back_a = shift(ahead[0] + right, 1)
+    front_b = shift(behind[1] + left, -1)
+    total = lambda a, b, c: a.astype(f32) + b.astype(f32) + c.astype(f32)
+    return jnp.concatenate([total(own[0], back_a, front_a), total(own[1], back_b, front_b)])
 
 
 def spread(x, axis):
@@ -134,23 +143,26 @@
             jnp.concatenate(picked), tables, (((1,), (1,)), ((), ())), preferred_element_type=f32
         ).astype(bf16)
 
-    far = ring_sum_far(part(2), shift_x)
+    summed = ring_sum(part(2, 1, 3, 0), shift_x).astype(bf16)
 
     grads = jnp.concatenate([grads_own, grads_other])
     grad_table = lax.dot_general(
         states, grads, (((0,), (0,)), ((), ())), preferred_element_type=f32
     ).astype(bf16)
-    both, grad_table = lax.optimization_barrier((both, grad_table))
     grad_table = grad_table.reshape(layers, quarter, block)
-    grad_table = lax.all_to_all(grad_table, "layer", 0, 0, tiled=True)
-    grad_table = jnp.concatenate([grad_table[k].astype(f32) for k in range(layers)], axis=1)
+    pieces = ring_exchange(lambda k: at(grad_table, (y + k) % layers), shift_y)
+    grad_embedding = jnp.zeros((quarter, layers * block), f32)
+    for k, p in pieces:
+        grad_embedding = lax.dynamic_update_slice_in_dim(
+            grad_embedding, p.astype(f32), ((y + k) % layers) * block, 1
+        )
 
-    ahead, behind, here = jnp.split(lax.optimization_barrier(part(1, 3, 0)), 3)
-    summed = ring_sum(here, ahead, behind, far, shift_x).astype(bf16)
-    summed = summed.reshape(layers * cols, strip // cols, width)
+    share = strip // cols
+    lanes = 128 if share * width % 128 == 0 else width
+    summed = summed.reshape(layers * cols, share * width // lanes, lanes)
     summed = lax.all_to_all(summed, ("layer", "col"), 0, 0, tiled=True)
-    grad_hidden = jnp.sum(summed.astype(f32), axis=0)
-    return grad_table.T, grad_hidden
+    grad_hidden = jnp.sum(summed.astype(f32), axis=0).reshape(share, width)
+    return grad_embedding.T, grad_hidden
 
 
 def solution(mesh):

time: 246 us -> 252 us (1.024)
  the two profiles are of different devices: /device:TPU:32 before, /device:TPU:1 now
where the time goes in v5:
time: 252 us; the launch traced here: 250 us
  waiting for transfers between devices  135 us (54%)
  starting transfers between devices  53.3 us (21%)
  local copies, waits for them, and re-layouts  26.1 us (10%)
  matrix products  20.3 us (8%)
  other arithmetic  13.6 us (5%)
    ppermute x10, waiting for transfers between devices, shift_x(): return lax.ppermute(x, 'row', [(i, (i + 2 * s) % n) for i in range(n)])  50.5 us
    all_to_all x1, waiting for transfers between devices, local(): sent = lax.all_to_all(jnp.stack(sent), 'layer', 0, 0, tiled=True)  46.2 us
    ppermute x9, waiting for transfers between devices, shift_y(): return lax.ppermute(x, 'layer', [(i, (i + s) % n) for i in range(n)])  23.3 us
    ppermute x9, starting transfers between devices, shift_y(): return lax.ppermute(x, 'layer', [(i, (i + s) % n) for i in range(n)])  14 us
    all_to_all x2, waiting for transfers between devices, spread(): lax.all_to_all(jnp.broadcast_to(x[None], (n, *x.shape)), axis, 0, 0, tile...  13.1 us
    all_to_all x2, starting transfers between devices, spread(): lax.all_to_all(jnp.broadcast_to(x[None], (n, *x.shape)), axis, 0, 0, tile...  12.3 us
    ppermute x10, starting transfers between devices, shift_x(): return lax.ppermute(x, 'row', [(i, (i + 2 * s) % n) for i in range(n)])  12 us
    dot_general x1, matrix products, local(): logits = jnp.dot(states, table, preferred_element_type=f32)  7.83 us
  transfers between devices with their start and end apart: 26, of which 15 were waited for; matrix products, arithmetic and copies ran while one was open for 15% of the time, Pallas kernels for 0%

profile of v5, /device:TPU:1, one launch (start us, length us, event | category | flops | bytes accessed | tf_op | source)
XLA Modules:
  0.0 249.5 jit_solution(4202673704055747532)
XLA Ops:
  0.6 2.2 collective-permute-start
  2.8 2.6 %collective-permute-start.2 = (bf16[48,2304]{1,0:T(8,128)(2,1)}, bf16[48,2304]{1,0:T(8,128)(2,1)S(1)}, u32[]{:S(2)}, u32[]{:S(2)}) collective-permute-start(bf16[48,2304]{1,0:T(8,128)(2,1)} %param.3), channel_id=1, source_target_pairs={{0,128},{64,192},{128,0},{192,64},{1,129},{65,193},{129,1},{193,65... | collective-permute-start | bytes 663560 | tf_op jit(solution)/shard_map/ppermute | solution.py:12
  5.4 1.1 collective-permute-start.1
  6.6 1.1 bitcast_dynamic-update-slice_fusion.4
  7.7 1.8 fusion.37
  9.5 4.6 %collective-permute-done.1 = bf16[48,2304]{1,0:T(8,128)(2,1)S(1)} collective-permute-done((bf16[48,2304]{1,0:T(8,128)(2,1)}, bf16[48,2304]{1,0:T(8,128)(2,1)S(1)}, u32[]{:S(2)}, u32[]{:S(2)}) %collective-permute-start.1) | collective-permute-done | bytes 221216 | tf_op jit(solution)/shard_map/ppermute | solution.py:12
  14.1 1.1 collective-permute-done.2
  15.3 2.6 %collective-permute-start.4 = (bf16[192,2304]{1,0:T(8,128)(2,1)S(1)}, bf16[192,2304]{1,0:T(8,128)(2,1)S(1)}, u32[]{:S(2)}, u32[]{:S(2)}) collective-permute-start(bf16[192,2304]{1,0:T(8,128)(2,1)S(1)} %bitcast.74), channel_id=1, source_target_pairs={{0,48},{8,56},{16,0},{24,8},{32,16},{40,24},{48,32},{56,40},{1,49}... | collective-permute-start | bytes 2654216 | tf_op jit(solution)/shard_map/ppermute | solution.py:17
  17.9 2.1 broadcast_in_dim.19
  20.1 1.0 bitcast_dynamic-update-slice_fusion
  21.0 14.3 %collective-permute-done.4 = bf16[192,2304]{1,0:T(8,128)(2,1)S(1)} collective-permute-done((bf16[192,2304]{1,0:T(8,128)(2,1)S(1)}, bf16[192,2304]{1,0:T(8,128)(2,1)S(1)}, u32[]{:S(2)}, u32[]{:S(2)}) %collective-permute-start.4) | collective-permute-done | bytes 884768 | tf_op jit(solution)/shard_map/ppermute | solution.py:17
  35.3 3.5 %collective-permute-start.6 = (bf16[96,2304]{1,0:T(8,128)(2,1)S(1)}, bf16[96,2304]{1,0:T(8,128)(2,1)S(1)}, u32[]{:S(2)}, u32[]{:S(2)}) collective-permute-start(bf16[96,2304]{1,0:T(8,128)(2,1)S(1)} %slice.93), channel_id=1, source_target_pairs={{0,48},{8,56},{16,0},{24,8},{32,16},{40,24},{48,32},{56,40},{1,49}... | collective-permute-start | bytes 1327112 | tf_op jit(solution)/shard_map/ppermute | solution.py:17
  38.9 1.0 constant_dynamic-update-slice_fusion.2
  40.0 1.0 constant_dynamic-update-slice_fusion.1
  41.0 5.0 %collective-permute-done.6 = bf16[96,2304]{1,0:T(8,128)(2,1)S(1)} collective-permute-done((bf16[96,2304]{1,0:T(8,128)(2,1)S(1)}, bf16[96,2304]{1,0:T(8,128)(2,1)S(1)}, u32[]{:S(2)}, u32[]{:S(2)}) %collective-permute-start.6) | collective-permute-done | bytes 442400 | tf_op jit(solution)/shard_map/ppermute | solution.py:17
  46.0 3.2 %collective-permute-done.5 = bf16[96,2304]{1,0:T(8,128)(2,1)S(1)} collective-permute-done((bf16[96,2304]{1,0:T(8,128)(2,1)S(1)}, bf16[96,2304]{1,0:T(8,128)(2,1)S(1)}, u32[]{:S(2)}, u32[]{:S(2)}) %collective-permute-start.5) | collective-permute-done | bytes 442400 | tf_op jit(solution)/shard_map/ppermute | solution.py:17
  49.3 1.0 constant_dynamic-update-slice_fusion
  50.3 3.5 %collective-permute-start.7 = (bf16[768,2304]{1,0:T(8,128)(2,1)}, bf16[768,2304]{1,0:T(8,128)(2,1)}, u32[]{:S(2)}, u32[]{:S(2)}) collective-permute-start(bf16[768,2304]{1,0:T(8,128)(2,1)} %bitcast.9), channel_id=1, source_target_pairs={{0,8},{8,0},{16,24},{24,16},{32,40},{40,32},{48,56},{56,48},{1,9},... | collective-permute-start | bytes 10616840 | tf_op jit(solution)/shard_map/ppermute | solution.py:22
  54.1 2.2 pad_maximum_fusion.5
  56.3 5.3 %all-to-all-start = ((bf16[4,960,512]{2,1,0:T(8,128)(2,1)}), bf16[4,960,512]{2,1,0:T(8,128)(2,1)}, u32[]{:S(2)}, u32[]{:S(2)}) async-start(bf16[4,960,512]{2,1,0:T(8,128)(2,1)} %pad_maximum_fusion.5), calls=%async_computation | async-start | bytes 7864320 | tf_op jit(solution)/shard_map/all_to_all | solution.py:98
  61.5 0.3 reduce_max.51
  61.8 0.7 exponential_reduce_fusion
  62.5 46.2 %all-to-all-done = bf16[4,960,512]{2,1,0:T(8,128)(2,1)} async-done(((bf16[4,960,512]{2,1,0:T(8,128)(2,1)}), bf16[4,960,512]{2,1,0:T(8,128)(2,1)}, u32[]{:S(2)}, u32[]{:S(2)}) %all-to-all-start) | async-done | bytes 3932192 | tf_op jit(solution)/shard_map/all_to_all | solution.py:98
  108.7 1.8 slice.98
  110.6 7.8 %fusion.41 = (f32[1536]{0:T(1024)S(1)}, f32[1536,512]{1,0:T(8,128)S(1)}) fusion(bf16[2304,512]{1,0:T(8,128)(2,1)S(1)} %bitcast.77, bf16[768,2304]{1,0:T(8,128)(2,1)} %collective-permute-done.7, bf16[768,2304]{1,0:T(8,128)(2,1)} %bitcast.9), kind=kOutput, calls=%fused_computation.100 | convolution fusion | flops 3638819328 | bytes 12589056 | tf_op jit(solution)/shard_map/dot_general | solution.py:111
  118.4 0.8 exponential_reduce_fusion.1
  119.4 0.8 broadcast_in_dim.49
  120.2 4.1 %all-to-all-start.1 = ((f32[32,1,1920]{2,1,0:T(1,128)}), f32[32,1,1920]{2,1,0:T(1,128)S(1)}, u32[]{:S(2)}, u32[]{:S(2)}) async-start(f32[32,1,1920]{2,1,0:T(1,128)} %broadcast_in_dim.49), calls=%async_computation.1 | async-start | bytes 491520 | tf_op jit(solution)/shard_map/all_to_all | solution.py:66
  124.3 0.4 collective-permute-start.15
  124.7 8.4 %all-to-all-done.1 = f32[32,1,1920]{2,1,0:T(1,128)S(1)} async-done(((f32[32,1,1920]{2,1,0:T(1,128)}), f32[32,1,1920]{2,1,0:T(1,128)S(1)}, u32[]{:S(2)}, u32[]{:S(2)}) %all-to-all-start.1) | async-done | bytes 245792 | tf_op jit(solution)/shard_map/all_to_all | solution.py:66
  133.4 0.7 broadcast_in_dim.50
  134.1 8.2 %all-to-all-start.2 = ((f32[8,1,3072]{2,1,0:T(1,128)}), f32[8,1,3072]{2,1,0:T(1,128)S(1)}, u32[]{:S(2)}, u32[]{:S(2)}) async-start(f32[8,1,3072]{2,1,0:T(1,128)} %broadcast_in_dim.50), calls=%async_computation.2 | async-start | bytes 196608 | tf_op jit(solution)/shard_map/all_to_all | solution.py:66
  142.2 1.5 slice.104
  143.8 1.3 constant_dynamic-slice_fusion.8
  145.0 4.8 %all-to-all-done.2 = f32[8,1,3072]{2,1,0:T(1,128)S(1)} async-done(((f32[8,1,3072]{2,1,0:T(1,128)}), f32[8,1,3072]{2,1,0:T(1,128)S(1)}, u32[]{:S(2)}, u32[]{:S(2)}) %all-to-all-start.2) | async-done | bytes 98336 | tf_op jit(solution)/shard_map/all_to_all | solution.py:66
  150.2 2.3 fusion.13
  152.5 1.9 collective-permute-start.14
  154.4 1.9 collective-permute-done.14
  156.7 1.2 copy-done.4
  158.0 5.5 %convolution_convert_fusion = bf16[768,2304]{1,0:T(8,128)(2,1)S(1)} fusion(bf16[2304,512]{1,0:T(8,128)(2,1)} %collective-permute-done.15, bf16[2304,512]{1,0:T(8,128)(2,1)S(1)} %bitcast.79, bf16[192,1024]{1,0:T(8,128)(2,1)S(1)} %bitcast.90, bf16[192,1024]{1,0:T(8,128)(2,1)S(1)} %bitcast.91, bf16[192,1024]{1,0:T(8,128)(2,1)S(1)} %bitcast.92, ...), kind=kOutput, calls=%fused_computation.1 | convolution fusion | flops 3641376768 | bytes 9830400 | tf_op jit(solution)/shard_map/dot_general | solution.py:142
  163.8 0.8 collective-permute-start.16
  164.5 2.2 collective-permute-start.20
  166.8 9.9 %collective-permute-done.16 = bf16[96,2304]{1,0:T(8,128)(2,1)S(1)} collective-permute-done((bf16[96,2304]{1,0:T(8,128)(2,1)S(1)}, bf16[96,2304]{1,0:T(8,128)(2,1)S(1)}, u32[]{:S(2)}, u32[]{:S(2)}) %collective-permute-start.16) | collective-permute-done | bytes 442400 | tf_op jit(solution)/shard_map/ppermute | solution.py:17
  177.0 2.7 %collective-permute-start.21 = (bf16[96,2304]{1,0:T(8,128)(2,1)S(1)}, bf16[96,2304]{1,0:T(8,128)(2,1)S(1)}, u32[]{:S(2)}, u32[]{:S(2)}) collective-permute-start(bf16[96,2304]{1,0:T(8,128)(2,1)S(1)} %add.207), channel_id=1, source_target_pairs={{0,48},{8,56},{16,0},{24,8},{32,16},{40,24},{48,32},{56,40},{1,49}... | collective-permute-start | bytes 1327112 | tf_op jit(solution)/shard_map/ppermute | solution.py:17
  179.8 5.3 %collective-permute-done.18 = bf16[96,2304]{1,0:T(8,128)(2,1)S(1)} collective-permute-done((bf16[96,2304]{1,0:T(8,128)(2,1)S(1)}, bf16[96,2304]{1,0:T(8,128)(2,1)S(1)}, u32[]{:S(2)}, u32[]{:S(2)}) %collective-permute-start.18) | collective-permute-done | bytes 442400 | tf_op jit(solution)/shard_map/ppermute | solution.py:17
  185.1 3.4 %collective-permute-done.17 = bf16[96,2304]{1,0:T(8,128)(2,1)S(1)} collective-permute-done((bf16[96,2304]{1,0:T(8,128)(2,1)S(1)}, bf16[96,2304]{1,0:T(8,128)(2,1)S(1)}, u32[]{:S(2)}, u32[]{:S(2)}) %collective-permute-start.17) | collective-permute-done | bytes 442400 | tf_op jit(solution)/shard_map/ppermute | solution.py:17
  188.7 9.3 %collective-permute-done.19 = bf16[96,2304]{1,0:T(8,128)(2,1)S(1)} collective-permute-done((bf16[96,2304]{1,0:T(8,128)(2,1)S(1)}, bf16[96,2304]{1,0:T(8,128)(2,1)S(1)}, u32[]{:S(2)}, u32[]{:S(2)}) %collective-permute-start.19) | collective-permute-done | bytes 442400 | tf_op jit(solution)/shard_map/ppermute | solution.py:17
  198.3 2.0 convert_element_type.88
  200.3 3.9 %all-to-all-start.3 = ((bf16[32,108,128]{2,1,0:T(8,128)(2,1)}), bf16[32,108,128]{2,1,0:T(8,128)(2,1)S(1)}, u32[]{:S(2)}, u32[]{:S(2)}) async-start(bf16[32,108,128]{2,1,0:T(8,128)(2,1)} %convert_element_type.88), calls=%async_computation.3 | async-start | bytes 1835008 | tf_op jit(solution)/shard_map/all_to_all | solution.py:163
  204.2 6.9 %fusion.5 = bf16[2304,512]{1,0:T(8,128)(2,1)S(1)} fusion(bf16[768,2304]{1,0:T(8,128)(2,1)} %collective-permute-done.7, bf16[768,2304]{1,0:T(8,128)(2,1)} %bitcast.9, bf16[768,512]{1,0:T(8,128)(2,1)S(1)} %copy-done.7, bf16[768,512]{1,0:T(8,128)(2,1)S(1)} %copy-done.2), kind=kOutput, calls=%fused_computation.7 | convolution fusion | flops 3642359808 | bytes 11010048 | tf_op jit(solution)/shard_map/dot_general | solution.py:149
  211.2 1.4 copy-done.5
  212.7 1.2 collective-permute-start.8
  213.9 1.5 collective-permute-start.9
  215.4 1.9 dynamic-slice_bitcast_fusion.3
  217.3 2.7 %collective-permute-start.12 = (bf16[288,512]{1,0:T(8,128)(2,1)}, bf16[288,512]{1,0:T(8,128)(2,1)}, u32[]{:S(2)}, u32[]{:S(2)}) collective-permute-start(bf16[288,512]{1,0:T(8,128)(2,1)} %get-tuple-element.33), channel_id=1, source_target_pairs={{0,192},{64,0},{128,64},{192,128},{1,193},{65,1},{129,65},{193,129... | collective-permute-start | bytes 884744 | tf_op jit(solution)/shard_map/ppermute | solution.py:12
  220.0 2.8 %broadcast_in_dim.18 = f32[576,2048]{1,0:T(8,128)} broadcast(f32[]{:T(128)} %constant.136.clone.1), dimensions={} | broadcast | bytes 4718596 | tf_op jit(solution)/shard_map/broadcast_in_dim | solution.py:154
  222.8 2.2 convert_dynamic-update-slice_fusion
  225.0 14.6 %collective-permute-done.10 = bf16[288,512]{1,0:T(8,128)(2,1)} collective-permute-done((bf16[288,512]{1,0:T(8,128)(2,1)}, bf16[288,512]{1,0:T(8,128)(2,1)}, u32[]{:S(2)}, u32[]{:S(2)}) %collective-permute-start.10) | collective-permute-done | bytes 294944 | tf_op jit(solution)/shard_map/ppermute | solution.py:12
  239.6 2.7 %collective-permute-start.13 = (bf16[288,512]{1,0:T(8,128)(2,1)}, bf16[288,512]{1,0:T(8,128)(2,1)S(1)}, u32[]{:S(2)}, u32[]{:S(2)}) collective-permute-start(bf16[288,512]{1,0:T(8,128)(2,1)} %collective-permute-done.12), channel_id=1, source_target_pairs={{0,192},{64,0},{128,64},{192,128},{1,193},{65,1},{129,65},{193,129... | collective-permute-start | bytes 884744 | tf_op jit(solution)/shard_map/ppermute | solution.py:12
  242.3 1.2 convert_dynamic-update-slice_fusion.3
  243.4 1.2 convert_dynamic-update-slice_fusion.2
  244.6 2.9 %collective-permute-done.11 = bf16[288,512]{1,0:T(8,128)(2,1)S(1)} collective-permute-done((bf16[288,512]{1,0:T(8,128)(2,1)}, bf16[288,512]{1,0:T(8,128)(2,1)S(1)}, u32[]{:S(2)}, u32[]{:S(2)}) %collective-permute-start.11) | collective-permute-done | bytes 294944 | tf_op jit(solution)/shard_map/ppermute | solution.py:12
  247.6 1.2 convert_dynamic-update-slice_fusion.1
  248.9 0.6 reshape.125
  (80 shorter events, 3.0 us)
Async XLA Ops:
  0.6 8.8 %collective-permute-start = (bf16[48,2304]{1,0:T(8,128)(2,1)}, bf16[48,2304]{1,0:T(8,128)(2,1)S(1)}, u32[]{:S(2)}, u32[]{:S(2)}) collective-permute-start(bf16[48,2304]{1,0:T(8,128)(2,1)} %param.3), channel_id=1, source_target_pairs={{0,64},{64,128},{128,192},{192,0},{1,65},{65,129},{129,193},{193,1... | collective-permute-start | bytes 663560 | tf_op jit(solution)/shard_map/ppermute | solution.py:12
  2.8 12.4 %collective-permute-start.2 = (bf16[48,2304]{1,0:T(8,128)(2,1)}, bf16[48,2304]{1,0:T(8,128)(2,1)S(1)}, u32[]{:S(2)}, u32[]{:S(2)}) collective-permute-start(bf16[48,2304]{1,0:T(8,128)(2,1)} %param.3), channel_id=1, source_target_pairs={{0,128},{64,192},{128,0},{192,64},{1,129},{65,193},{129,1},{193,65... | collective-permute-start | bytes 663560 | tf_op jit(solution)/shard_map/ppermute | solution.py:12
  5.4 8.6 %collective-permute-start.1 = (bf16[48,2304]{1,0:T(8,128)(2,1)}, bf16[48,2304]{1,0:T(8,128)(2,1)S(1)}, u32[]{:S(2)}, u32[]{:S(2)}) collective-permute-start(bf16[48,2304]{1,0:T(8,128)(2,1)} %param.3), channel_id=1, source_target_pairs={{0,192},{64,0},{128,64},{192,128},{1,193},{65,1},{129,65},{193,129... | collective-permute-start | bytes 663560 | tf_op jit(solution)/shard_map/ppermute | solution.py:12
  6.6 11.2 %copy-start = (bf16[384,2048]{1,0:T(8,128)(2,1)S(1)}, bf16[384,2048]{1,0:T(8,128)(2,1)}, u32[]{:S(2)}) copy-start(bf16[384,2048]{1,0:T(8,128)(2,1)} %param.5) | copy-start | bytes 4718596
  15.3 20.0 %collective-permute-start.4 = (bf16[192,2304]{1,0:T(8,128)(2,1)S(1)}, bf16[192,2304]{1,0:T(8,128)(2,1)S(1)}, u32[]{:S(2)}, u32[]{:S(2)}) collective-permute-start(bf16[192,2304]{1,0:T(8,128)(2,1)S(1)} %bitcast.74), channel_id=1, source_target_pairs={{0,48},{8,56},{16,0},{24,8},{32,16},{40,24},{48,32},{56,40},{1,49}... | collective-permute-start | bytes 2654216 | tf_op jit(solution)/shard_map/ppermute | solution.py:17
  17.8 21.0 %collective-permute-start.3 = (bf16[192,2304]{1,0:T(8,128)(2,1)S(1)}, bf16[192,2304]{1,0:T(8,128)(2,1)S(1)}, u32[]{:S(2)}, u32[]{:S(2)}) collective-permute-start(bf16[192,2304]{1,0:T(8,128)(2,1)S(1)} %bitcast.75), channel_id=1, source_target_pairs={{0,16},{8,24},{16,32},{24,40},{32,48},{40,56},{48,0},{56,8},{1,17}... | collective-permute-start | bytes 2654216 | tf_op jit(solution)/shard_map/ppermute | solution.py:17
  35.3 10.6 %collective-permute-start.6 = (bf16[96,2304]{1,0:T(8,128)(2,1)S(1)}, bf16[96,2304]{1,0:T(8,128)(2,1)S(1)}, u32[]{:S(2)}, u32[]{:S(2)}) collective-permute-start(bf16[96,2304]{1,0:T(8,128)(2,1)S(1)} %slice.93), channel_id=1, source_target_pairs={{0,48},{8,56},{16,0},{24,8},{32,16},{40,24},{48,32},{56,40},{1,49}... | collective-permute-start | bytes 1327112 | tf_op jit(solution)/shard_map/ppermute | solution.py:17
  38.9 10.3 %collective-permute-start.5 = (bf16[96,2304]{1,0:T(8,128)(2,1)S(1)}, bf16[96,2304]{1,0:T(8,128)(2,1)S(1)}, u32[]{:S(2)}, u32[]{:S(2)}) collective-permute-start(bf16[96,2304]{1,0:T(8,128)(2,1)S(1)} %slice.92), channel_id=1, source_target_pairs={{0,16},{8,24},{16,32},{24,40},{32,48},{40,56},{48,0},{56,8},{1,17}... | collective-permute-start | bytes 1327112 | tf_op jit(solution)/shard_map/ppermute | solution.py:17
  50.3 60.3 %collective-permute-start.7 = (bf16[768,2304]{1,0:T(8,128)(2,1)}, bf16[768,2304]{1,0:T(8,128)(2,1)}, u32[]{:S(2)}, u32[]{:S(2)}) collective-permute-start(bf16[768,2304]{1,0:T(8,128)(2,1)} %bitcast.9), channel_id=1, source_target_pairs={{0,8},{8,0},{16,24},{24,16},{32,40},{40,32},{48,56},{56,48},{1,9},... | collective-permute-start | bytes 10616840 | tf_op jit(solution)/shard_map/ppermute | solution.py:22
  56.3 52.5 %all-to-all-start = ((bf16[4,960,512]{2,1,0:T(8,128)(2,1)}), bf16[4,960,512]{2,1,0:T(8,128)(2,1)}, u32[]{:S(2)}, u32[]{:S(2)}) async-start(bf16[4,960,512]{2,1,0:T(8,128)(2,1)} %pad_maximum_fusion.5), calls=%async_computation | async-start | bytes 7864320 | tf_op jit(solution)/shard_map/all_to_all | solution.py:98
  110.5 7.9 %copy-start.3 = (bf16[4,576,512]{2,1,0:T(8,128)(2,1)}, bf16[4,576,512]{2,1,0:T(8,128)(2,1)S(1)}, u32[]{:S(2)}) copy-start(bf16[4,576,512]{2,1,0:T(8,128)(2,1)S(1)} %slice.98) | copy-start | bytes 7077892
  120.2 12.9 %all-to-all-start.1 = ((f32[32,1,1920]{2,1,0:T(1,128)}), f32[32,1,1920]{2,1,0:T(1,128)S(1)}, u32[]{:S(2)}, u32[]{:S(2)}) async-start(f32[32,1,1920]{2,1,0:T(1,128)} %broadcast_in_dim.49), calls=%async_computation.1 | async-start | bytes 491520 | tf_op jit(solution)/shard_map/all_to_all | solution.py:66
  124.3 32.4 %collective-permute-start.15 = (bf16[2304,512]{1,0:T(8,128)(2,1)}, bf16[2304,512]{1,0:T(8,128)(2,1)}, u32[]{:S(2)}, u32[]{:S(2)}) collective-permute-start(bf16[2304,512]{1,0:T(8,128)(2,1)} %bitcast.78), channel_id=1, source_target_pairs={{0,8},{8,0},{16,24},{24,16},{32,40},{40,32},{48,56},{56,48},{1,9},... | collective-permute-start | bytes 7077896 | tf_op jit(solution)/shard_map/ppermute | solution.py:22
  134.1 15.7 %all-to-all-start.2 = ((f32[8,1,3072]{2,1,0:T(1,128)}), f32[8,1,3072]{2,1,0:T(1,128)S(1)}, u32[]{:S(2)}, u32[]{:S(2)}) async-start(f32[8,1,3072]{2,1,0:T(1,128)} %broadcast_in_dim.50), calls=%async_computation.2 | async-start | bytes 196608 | tf_op jit(solution)/shard_map/all_to_all | solution.py:66
  152.5 3.8 %copy-start.6 = (bf16[768,512]{1,0:T(8,128)(2,1)}, bf16[768,512]{1,0:T(8,128)(2,1)S(1)}, u32[]{:S(2)}) copy-start(bf16[768,512]{1,0:T(8,128)(2,1)S(1)} %get-tuple-element.31) | copy-start | bytes 2359300
  152.5 4.2 %copy-start.1 = (bf16[768,512]{1,0:T(8,128)(2,1)}, bf16[768,512]{1,0:T(8,128)(2,1)S(1)}, u32[]{:S(2)}) copy-start(bf16[768,512]{1,0:T(8,128)(2,1)S(1)} %get-tuple-element.30) | copy-start | bytes 2359300
  152.5 3.8 %collective-permute-start.14 = (bf16[768,512]{1,0:T(8,128)(2,1)S(1)}, bf16[768,512]{1,0:T(8,128)(2,1)S(1)}, u32[]{:S(2)}, u32[]{:S(2)}) collective-permute-start(bf16[768,512]{1,0:T(8,128)(2,1)S(1)} %get-tuple-element.31), channel_id=1, source_target_pairs={{0,8},{8,0},{16,24},{24,16},{32,40},{40,32},{48,56},{56,48},{1,9},... | collective-permute-start | bytes 2359304 | tf_op jit(solution)/shard_map/ppermute | solution.py:22
  156.3 1.7 copy-start.4
  163.8 12.9 %collective-permute-start.16 = (bf16[96,2304]{1,0:T(8,128)(2,1)S(1)}, bf16[96,2304]{1,0:T(8,128)(2,1)S(1)}, u32[]{:S(2)}, u32[]{:S(2)}) collective-permute-start(bf16[96,2304]{1,0:T(8,128)(2,1)S(1)} %get-tuple-element.12), channel_id=1, source_target_pairs={{0,16},{8,24},{16,32},{24,40},{32,48},{40,56},{48,0},{56,8},{1,17}... | collective-permute-start | bytes 1327112 | tf_op jit(solution)/shard_map/ppermute | solution.py:17
  164.5 12.4 %collective-permute-start.20 = (bf16[96,2304]{1,0:T(8,128)(2,1)S(1)}, bf16[96,2304]{1,0:T(8,128)(2,1)S(1)}, u32[]{:S(2)}, u32[]{:S(2)}) collective-permute-start(bf16[96,2304]{1,0:T(8,128)(2,1)S(1)} %get-tuple-element.17), channel_id=1, source_target_pairs={{0,48},{8,56},{16,0},{24,8},{32,16},{40,24},{48,32},{56,40},{1,49}... | collective-permute-start | bytes 1327112 | tf_op jit(solution)/shard_map/ppermute | solution.py:17
  166.7 18.4 %collective-permute-start.18 = (bf16[96,2304]{1,0:T(8,128)(2,1)S(1)}, bf16[96,2304]{1,0:T(8,128)(2,1)S(1)}, u32[]{:S(2)}, u32[]{:S(2)}) collective-permute-start(bf16[96,2304]{1,0:T(8,128)(2,1)S(1)} %get-tuple-element.13), channel_id=1, source_target_pairs={{0,48},{8,56},{16,0},{24,8},{32,16},{40,24},{48,32},{56,40},{1,49}... | collective-permute-start | bytes 1327112 | tf_op jit(solution)/shard_map/ppermute | solution.py:17
  176.7 11.8 %collective-permute-start.17 = (bf16[96,2304]{1,0:T(8,128)(2,1)S(1)}, bf16[96,2304]{1,0:T(8,128)(2,1)S(1)}, u32[]{:S(2)}, u32[]{:S(2)}) collective-permute-start(bf16[96,2304]{1,0:T(8,128)(2,1)S(1)} %add.203), channel_id=1, source_target_pairs={{0,16},{8,24},{16,32},{24,40},{32,48},{40,56},{48,0},{56,8},{1,17}... | collective-permute-start | bytes 1327112 | tf_op jit(solution)/shard_map/ppermute | solution.py:17
  176.8 21.2 %collective-permute-start.19 = (bf16[96,2304]{1,0:T(8,128)(2,1)S(1)}, bf16[96,2304]{1,0:T(8,128)(2,1)S(1)}, u32[]{:S(2)}, u32[]{:S(2)}) collective-permute-start(bf16[96,2304]{1,0:T(8,128)(2,1)S(1)} %get-tuple-element.15), channel_id=1, source_target_pairs={{0,16},{8,24},{16,32},{24,40},{32,48},{40,56},{48,0},{56,8},{1,17}... | collective-permute-start | bytes 1327112 | tf_op jit(solution)/shard_map/ppermute | solution.py:17
  177.0 21.0 %collective-permute-start.21 = (bf16[96,2304]{1,0:T(8,128)(2,1)S(1)}, bf16[96,2304]{1,0:T(8,128)(2,1)S(1)}, u32[]{:S(2)}, u32[]{:S(2)}) collective-permute-start(bf16[96,2304]{1,0:T(8,128)(2,1)S(1)} %add.207), channel_id=1, source_target_pairs={{0,48},{8,56},{16,0},{24,8},{32,16},{40,24},{48,32},{56,40},{1,49}... | collective-permute-start | bytes 1327112 | tf_op jit(solution)/shard_map/ppermute | solution.py:17
  198.2 6.0 %copy-start.2 = (bf16[768,512]{1,0:T(8,128)(2,1)S(1)}, bf16[768,512]{1,0:T(8,128)(2,1)}, u32[]{:S(2)}) copy-start(bf16[768,512]{1,0:T(8,128)(2,1)} %copy-done.1) | copy-start | bytes 2359300
  198.2 6.0 %copy-start.7 = (bf16[768,512]{1,0:T(8,128)(2,1)S(1)}, bf16[768,512]{1,0:T(8,128)(2,1)}, u32[]{:S(2)}) copy-start(bf16[768,512]{1,0:T(8,128)(2,1)} %copy-done.6) | copy-start | bytes 2359300
  200.3 48.5 %all-to-all-start.3 = ((bf16[32,108,128]{2,1,0:T(8,128)(2,1)}), bf16[32,108,128]{2,1,0:T(8,128)(2,1)S(1)}, u32[]{:S(2)}, u32[]{:S(2)}) async-start(bf16[32,108,128]{2,1,0:T(8,128)(2,1)} %convert_element_type.88), calls=%async_computation.3 | async-start | bytes 1835008 | tf_op jit(solution)/shard_map/all_to_all | solution.py:163
  211.2 1.4 copy-start.5
  212.7 29.6 %collective-permute-start.8 = (bf16[576,512]{1,0:T(8,128)(2,1)S(1)}, bf16[576,512]{1,0:T(8,128)(2,1)S(1)}, u32[]{:S(2)}, u32[]{:S(2)}) collective-permute-start(bf16[576,512]{1,0:T(8,128)(2,1)S(1)} %get-tuple-element.35), channel_id=1, source_target_pairs={{0,64},{64,128},{128,192},{192,0},{1,65},{65,129},{129,193},{193,1... | collective-permute-start | bytes 1769480 | tf_op jit(solution)/shard_map/ppermute | solution.py:12
  213.9 29.5 %collective-permute-start.9 = (bf16[576,512]{1,0:T(8,128)(2,1)S(1)}, bf16[576,512]{1,0:T(8,128)(2,1)S(1)}, u32[]{:S(2)}, u32[]{:S(2)}) collective-permute-start(bf16[576,512]{1,0:T(8,128)(2,1)S(1)} %get-tuple-element.34), channel_id=1, source_target_pairs={{0,192},{64,0},{128,64},{192,128},{1,193},{65,1},{129,65},{193,129... | collective-permute-start | bytes 1769480 | tf_op jit(solution)/shard_map/ppermute | solution.py:12
  217.3 22.3 %collective-permute-start.10 = (bf16[288,512]{1,0:T(8,128)(2,1)}, bf16[288,512]{1,0:T(8,128)(2,1)}, u32[]{:S(2)}, u32[]{:S(2)}) collective-permute-start(bf16[288,512]{1,0:T(8,128)(2,1)} %get-tuple-element.32), channel_id=1, source_target_pairs={{0,64},{64,128},{128,192},{192,0},{1,65},{65,129},{129,193},{193,1... | collective-permute-start | bytes 884744 | tf_op jit(solution)/shard_map/ppermute | solution.py:12
  217.3 22.3 %collective-permute-start.12 = (bf16[288,512]{1,0:T(8,128)(2,1)}, bf16[288,512]{1,0:T(8,128)(2,1)}, u32[]{:S(2)}, u32[]{:S(2)}) collective-permute-start(bf16[288,512]{1,0:T(8,128)(2,1)} %get-tuple-element.33), channel_id=1, source_target_pairs={{0,192},{64,0},{128,64},{192,128},{1,193},{65,1},{129,65},{193,129... | collective-permute-start | bytes 884744 | tf_op jit(solution)/shard_map/ppermute | solution.py:12
  239.6 8.0 %collective-permute-start.11 = (bf16[288,512]{1,0:T(8,128)(2,1)}, bf16[288,512]{1,0:T(8,128)(2,1)S(1)}, u32[]{:S(2)}, u32[]{:S(2)}) collective-permute-start(bf16[288,512]{1,0:T(8,128)(2,1)} %collective-permute-done.10), channel_id=1, source_target_pairs={{0,64},{64,128},{128,192},{192,0},{1,65},{65,129},{129,193},{193,1... | collective-permute-start | bytes 884744 | tf_op jit(solution)/shard_map/ppermute | solution.py:12
  239.6 8.0 %collective-permute-start.13 = (bf16[288,512]{1,0:T(8,128)(2,1)}, bf16[288,512]{1,0:T(8,128)(2,1)S(1)}, u32[]{:S(2)}, u32[]{:S(2)}) collective-permute-start(bf16[288,512]{1,0:T(8,128)(2,1)} %collective-permute-done.12), channel_id=1, source_target_pairs={{0,192},{64,0},{128,64},{192,128},{1,193},{65,1},{129,65},{193,129... | collective-permute-start | bytes 884744 | tf_op jit(solution)/shard_map/ppermute | solution.py:12

commit v6 on v5

--- a/solution.py
+++ b/solution.py
@@ -92,12 +92,11 @@
     for k, p in ((0, hidden), (3, moved[0]), (1, moved[1]), (2, moved[2])):
         mine = put(mine, p, (y + k) % layers)
 
-    table = embedding.T
-    cut = lambda m, k: m[:, k * block : (k + 1) * block]
-    sent = [jnp.concatenate([cut(table, k), cut(teacher, k)]) for k in range(layers)]
-    sent = lax.all_to_all(jnp.stack(sent), "layer", 0, 0, tiled=True)
-    table = sent[:, :quarter].reshape(width, block)
-    taught = sent[:, quarter:].reshape(layers, xs, 2, strip, block)
+    cut = lambda m: jnp.stack([m[:, k * block : (k + 1) * block] for k in range(layers)])
+    table = lax.all_to_all(cut(embedding.T), "layer", 0, 0, tiled=True)
+    table = table.reshape(width, block)
+    taught = lax.all_to_all(cut(teacher), "layer", 0, 0, tiled=True)
+    taught = taught.reshape(layers, xs, 2, strip, block)
     taught = [at(taught, c, 2).reshape(half, block) for c in (core, 1 - core)]
 
     own = jnp.zeros((layers, xs, strip, width), bf16)
@@ -129,7 +128,8 @@
 
     grads_other = gradient(logits[half:], taught[1], 1 - core)
     crossed = swap_core(grads_other)
-    grads_own = gradient(logits[:half], taught[0], core)
+    logits_own, grads_other = lax.optimization_barrier((logits[:half], grads_other))
+    grads_own = gradient(logits_own, taught[0], core)
     other_table = swap_core(table)
 
 

time: 252 us -> 256 us (1.016)
  starting transfers between devices: 53.3 us -> 57.8 us
  local copies, waits for them, and re-layouts: 26.1 us -> 22.7 us
    slice x4 -> x0, local copies, waits for them, and re-layouts: 5.21 us -> none  [the longest x2 1.88 us: local(): cut = lambda m, k: m[:, k * block:(k + 1) * block]]
    all_to_all x1 -> x2, starting transfers between devices: 5.27 us -> 9 us  [the longest x1 4.64 us: local(): table = lax.all_to_all(cut(embedding.T), 'layer', 0, 0, tiled=True)]
    all_to_all x1 -> x2, waiting for transfers between devices: 46.2 us -> 48.6 us  [the longest x1 28.3 us: local(): table = lax.all_to_all(cut(embedding.T), 'layer', 0, 0, tiled=True)]
  transfers between devices with their start and end apart: 26 -> 27, of which waited for: 15 -> 16; matrix products, arithmetic and copies ran while one was open for 15% -> 14% of each run, Pallas kernels for 0% -> 0%
where the time goes in v6:
time: 256 us; the launch traced here: 254 us
  waiting for transfers between devices  137 us (54%)
  starting transfers between devices  57.8 us (23%)
  local copies, waits for them, and re-layouts  22.7 us (9%)
  matrix products  21 us (8%)
  other arithmetic  14.4 us (6%)
    ppermute x10, waiting for transfers between devices, shift_x(): return lax.ppermute(x, 'row', [(i, (i + 2 * s) % n) for i in range(n)])  48.7 us
    all_to_all x1, waiting for transfers between devices, local(): table = lax.all_to_all(cut(embedding.T), 'layer', 0, 0, tiled=True)  28.3 us
    ppermute x9, waiting for transfers between devices, shift_y(): return lax.ppermute(x, 'layer', [(i, (i + s) % n) for i in range(n)])  25.8 us
    all_to_all x1, waiting for transfers between devices, local(): taught = lax.all_to_all(cut(teacher), 'layer', 0, 0, tiled=True)  20.3 us
    all_to_all x2, starting transfers between devices, spread(): lax.all_to_all(jnp.broadcast_to(x[None], (n, *x.shape)), axis, 0, 0, tile...  14.1 us
    ppermute x9, starting transfers between devices, shift_y(): return lax.ppermute(x, 'layer', [(i, (i + s) % n) for i in range(n)])  13.4 us
    all_to_all x2, waiting for transfers between devices, spread(): lax.all_to_all(jnp.broadcast_to(x[None], (n, *x.shape)), axis, 0, 0, tile...  12.2 us
    ppermute x10, starting transfers between devices, shift_x(): return lax.ppermute(x, 'row', [(i, (i + 2 * s) % n) for i in range(n)])  11.5 us
  transfers between devices with their start and end apart: 27, of which 16 were waited for; matrix products, arithmetic and copies ran while one was open for 14% of the time, Pallas kernels for 0%

profile of v6, /device:TPU:1, one launch (start us, length us, event | category | flops | bytes accessed | tf_op | source)
XLA Modules:
  0.0 253.8 jit_solution(10741614041503190439)
XLA Ops:
  0.6 2.2 collective-permute-start
  2.8 1.5 collective-permute-start.1
  4.4 1.6 collective-permute-start.2
  6.0 1.0 bitcast_dynamic-update-slice_fusion.4
  7.0 0.8 collective-permute-done
  7.8 1.0 collective-permute-done.1
  8.9 6.4 %collective-permute-done.2 = bf16[48,2304]{1,0:T(8,128)(2,1)S(1)} collective-permute-done((bf16[48,2304]{1,0:T(8,128)(2,1)}, bf16[48,2304]{1,0:T(8,128)(2,1)S(1)}, u32[]{:S(2)}, u32[]{:S(2)}) %collective-permute-start.2) | collective-permute-done | bytes 221216 | tf_op jit(solution)/shard_map/ppermute | solution.py:12
  15.3 1.3 collective-permute-start.3
  16.6 1.5 collective-permute-start.4
  18.0 2.0 broadcast_in_dim.19
  20.0 1.0 bitcast_dynamic-update-slice_fusion
  21.0 15.2 %collective-permute-done.3 = bf16[192,2304]{1,0:T(8,128)(2,1)S(1)} collective-permute-done((bf16[192,2304]{1,0:T(8,128)(2,1)S(1)}, bf16[192,2304]{1,0:T(8,128)(2,1)S(1)}, u32[]{:S(2)}, u32[]{:S(2)}) %collective-permute-start.3) | collective-permute-done | bytes 884768 | tf_op jit(solution)/shard_map/ppermute | solution.py:17
  36.4 2.7 %collective-permute-start.6 = (bf16[96,2304]{1,0:T(8,128)(2,1)S(1)}, bf16[96,2304]{1,0:T(8,128)(2,1)S(1)}, u32[]{:S(2)}, u32[]{:S(2)}) collective-permute-start(bf16[96,2304]{1,0:T(8,128)(2,1)S(1)} %slice.85), channel_id=1, source_target_pairs={{0,48},{8,56},{16,0},{24,8},{32,16},{40,24},{48,32},{56,40},{1,49}... | collective-permute-start | bytes 1327112 | tf_op jit(solution)/shard_map/ppermute | solution.py:17
  39.1 1.0 constant_dynamic-update-slice_fusion.2
  40.1 1.0 constant_dynamic-update-slice_fusion.1
  41.1 5.8 %collective-permute-done.5 = bf16[96,2304]{1,0:T(8,128)(2,1)S(1)} collective-permute-done((bf16[96,2304]{1,0:T(8,128)(2,1)S(1)}, bf16[96,2304]{1,0:T(8,128)(2,1)S(1)}, u32[]{:S(2)}, u32[]{:S(2)}) %collective-permute-start.5) | collective-permute-done | bytes 442400 | tf_op jit(solution)/shard_map/ppermute | solution.py:17
  47.0 1.0 constant_dynamic-update-slice_fusion
  47.9 3.2 %collective-permute-start.7 = (bf16[768,2304]{1,0:T(8,128)(2,1)}, bf16[768,2304]{1,0:T(8,128)(2,1)}, u32[]{:S(2)}, u32[]{:S(2)}) collective-permute-start(bf16[768,2304]{1,0:T(8,128)(2,1)} %bitcast.9), channel_id=1, source_target_pairs={{0,8},{8,0},{16,24},{24,16},{32,40},{40,32},{48,56},{56,48},{1,9},... | collective-permute-start | bytes 10616840 | tf_op jit(solution)/shard_map/ppermute | solution.py:22
  51.4 1.7 pad_maximum_fusion.5
  53.1 4.6 %all-to-all-start = ((bf16[4,576,512]{2,1,0:T(8,128)(2,1)}), bf16[4,576,512]{2,1,0:T(8,128)(2,1)}, u32[]{:S(2)}, u32[]{:S(2)}) async-start(bf16[4,576,512]{2,1,0:T(8,128)(2,1)} %pad_maximum_fusion.5), calls=%async_computation | async-start | bytes 4718592 | tf_op jit(solution)/shard_map/all_to_all | solution.py:96
  58.1 0.7 exponential_reduce_fusion
  58.7 28.3 %all-to-all-done = bf16[4,576,512]{2,1,0:T(8,128)(2,1)} async-done(((bf16[4,576,512]{2,1,0:T(8,128)(2,1)}), bf16[4,576,512]{2,1,0:T(8,128)(2,1)}, u32[]{:S(2)}, u32[]{:S(2)}) %all-to-all-start) | async-done | bytes 2359328 | tf_op jit(solution)/shard_map/all_to_all | solution.py:96
  87.0 7.8 %fusion.38 = (f32[1536]{0:T(1024)S(1)}, f32[1536,512]{1,0:T(8,128)S(1)}) fusion(bf16[2304,512]{1,0:T(8,128)(2,1)} %bitcast.15, bf16[768,2304]{1,0:T(8,128)(2,1)} %collective-permute-done.7, bf16[768,2304]{1,0:T(8,128)(2,1)} %bitcast.9), kind=kOutput, calls=%fused_computation.101 | convolution fusion | flops 3638819328 | bytes 12589056 | tf_op jit(solution)/shard_map/dot_general | solution.py:110
  94.8 1.7 copy-done.1
  96.5 0.9 exponential_reduce_fusion.1
  97.5 0.9 broadcast_in_dim.49
  98.4 6.0 %all-to-all-start.1 = ((f32[32,1,1920]{2,1,0:T(1,128)}), f32[32,1,1920]{2,1,0:T(1,128)S(1)}, u32[]{:S(2)}, u32[]{:S(2)}) async-start(f32[32,1,1920]{2,1,0:T(1,128)} %broadcast_in_dim.49), calls=%async_computation.1 | async-start | bytes 491520 | tf_op jit(solution)/shard_map/all_to_all | solution.py:66
  104.5 1.4 pad_maximum_fusion.6
  105.8 7.2 %all-to-all-done.1 = f32[32,1,1920]{2,1,0:T(1,128)S(1)} async-done(((f32[32,1,1920]{2,1,0:T(1,128)}), f32[32,1,1920]{2,1,0:T(1,128)S(1)}, u32[]{:S(2)}, u32[]{:S(2)}) %all-to-all-start.1) | async-done | bytes 245792 | tf_op jit(solution)/shard_map/all_to_all | solution.py:66
  113.1 4.4 %all-to-all-start.3 = ((bf16[4,384,512]{2,1,0:T(8,128)(2,1)}), bf16[4,384,512]{2,1,0:T(8,128)(2,1)}, u32[]{:S(2)}, u32[]{:S(2)}) async-start(bf16[4,384,512]{2,1,0:T(8,128)(2,1)} %pad_maximum_fusion.6), calls=%async_computation.3 | async-start | bytes 3145728 | tf_op jit(solution)/shard_map/all_to_all | solution.py:98
  117.9 20.3 %all-to-all-done.3 = bf16[4,384,512]{2,1,0:T(8,128)(2,1)} async-done(((bf16[4,384,512]{2,1,0:T(8,128)(2,1)}), bf16[4,384,512]{2,1,0:T(8,128)(2,1)}, u32[]{:S(2)}, u32[]{:S(2)}) %all-to-all-start.3) | async-done | bytes 1572896 | tf_op jit(solution)/shard_map/all_to_all | solution.py:98
  138.2 0.7 broadcast_in_dim.50
  138.9 8.2 %all-to-all-start.2 = ((f32[8,1,3072]{2,1,0:T(1,128)}), f32[8,1,3072]{2,1,0:T(1,128)S(1)}, u32[]{:S(2)}, u32[]{:S(2)}) async-start(f32[8,1,3072]{2,1,0:T(1,128)} %broadcast_in_dim.50), calls=%async_computation.2 | async-start | bytes 196608 | tf_op jit(solution)/shard_map/all_to_all | solution.py:66
  147.0 2.7 %constant_dynamic-slice_fusion.5 = (bf16[4,4,1,48,512]{4,3,2,1,0:T(8,128)(2,1)}, bf16[4,4,1,48,512]{4,3,2,1,0:T(8,128)(2,1)}) fusion(bf16[4,4,2,48,512]{4,3,2,1,0:T(8,128)(2,1)} %bitcast.21, s32[]{:T(128)S(6)} %select_n.159, s32[]{:T(128)S(6)} %select_n.158), kind=kLoop, calls=%fused_computation.80 | loop fusion | bytes 3145736 | tf_op jit(solution)/shard_map/jit(dynamic_index_in_dim)/dynamic_slice | solution.py:26
  149.7 4.9 %all-to-all-done.2 = f32[8,1,3072]{2,1,0:T(1,128)S(1)} async-done(((f32[8,1,3072]{2,1,0:T(1,128)}), f32[8,1,3072]{2,1,0:T(1,128)S(1)}, u32[]{:S(2)}, u32[]{:S(2)}) %all-to-all-start.2) | async-done | bytes 98336 | tf_op jit(solution)/shard_map/all_to_all | solution.py:66
  155.1 1.9 fusion.9
  157.0 2.5 collective-permute-start.14
  159.4 0.6 fusion.23
  160.0 1.3 collective-permute-done.14
  161.8 6.3 %convolution_convert_fusion = bf16[768,2304]{1,0:T(8,128)(2,1)S(1)} fusion(bf16[2304,512]{1,0:T(8,128)(2,1)} %collective-permute-done.15, bf16[2304,512]{1,0:T(8,128)(2,1)} %bitcast.15, bf16[192,1024]{1,0:T(8,128)(2,1)S(1)} %bitcast.94, bf16[192,1024]{1,0:T(8,128)(2,1)S(1)} %bitcast.95, bf16[192,1024]{1,0:T(8,128)(2,1)S(1)} %bitcast.96, ...), kind=kOutput, calls=%fused_computation.1 | convolution fusion | flops 3641376768 | bytes 9830400 | tf_op jit(solution)/shard_map/dot_general | solution.py:142
  168.3 0.5 collective-permute-start.16
  168.8 2.2 collective-permute-start.20
  171.0 9.9 %collective-permute-done.16 = bf16[96,2304]{1,0:T(8,128)(2,1)S(1)} collective-permute-done((bf16[96,2304]{1,0:T(8,128)(2,1)S(1)}, bf16[96,2304]{1,0:T(8,128)(2,1)S(1)}, u32[]{:S(2)}, u32[]{:S(2)}) %collective-permute-start.16) | collective-permute-done | bytes 442400 | tf_op jit(solution)/shard_map/ppermute | solution.py:17
  181.3 2.9 %collective-permute-start.21 = (bf16[96,2304]{1,0:T(8,128)(2,1)S(1)}, bf16[96,2304]{1,0:T(8,128)(2,1)S(1)}, u32[]{:S(2)}, u32[]{:S(2)}) collective-permute-start(bf16[96,2304]{1,0:T(8,128)(2,1)S(1)} %add.207), channel_id=1, source_target_pairs={{0,48},{8,56},{16,0},{24,8},{32,16},{40,24},{48,32},{56,40},{1,49}... | collective-permute-start | bytes 1327112 | tf_op jit(solution)/shard_map/ppermute | solution.py:17
  184.3 5.1 %collective-permute-done.18 = bf16[96,2304]{1,0:T(8,128)(2,1)S(1)} collective-permute-done((bf16[96,2304]{1,0:T(8,128)(2,1)S(1)}, bf16[96,2304]{1,0:T(8,128)(2,1)S(1)}, u32[]{:S(2)}, u32[]{:S(2)}) %collective-permute-start.18) | collective-permute-done | bytes 442400 | tf_op jit(solution)/shard_map/ppermute | solution.py:17
  189.4 3.4 %collective-permute-done.17 = bf16[96,2304]{1,0:T(8,128)(2,1)S(1)} collective-permute-done((bf16[96,2304]{1,0:T(8,128)(2,1)S(1)}, bf16[96,2304]{1,0:T(8,128)(2,1)S(1)}, u32[]{:S(2)}, u32[]{:S(2)}) %collective-permute-start.17) | collective-permute-done | bytes 442400 | tf_op jit(solution)/shard_map/ppermute | solution.py:17
  193.0 9.3 %collective-permute-done.19 = bf16[96,2304]{1,0:T(8,128)(2,1)S(1)} collective-permute-done((bf16[96,2304]{1,0:T(8,128)(2,1)S(1)}, bf16[96,2304]{1,0:T(8,128)(2,1)S(1)}, u32[]{:S(2)}, u32[]{:S(2)}) %collective-permute-start.19) | collective-permute-done | bytes 442400 | tf_op jit(solution)/shard_map/ppermute | solution.py:17
  202.5 2.0 convert_element_type.88
  204.5 3.9 %all-to-all-start.4 = ((bf16[32,108,128]{2,1,0:T(8,128)(2,1)}), bf16[32,108,128]{2,1,0:T(8,128)(2,1)S(1)}, u32[]{:S(2)}, u32[]{:S(2)}) async-start(bf16[32,108,128]{2,1,0:T(8,128)(2,1)} %convert_element_type.88), calls=%async_computation.4 | async-start | bytes 1835008 | tf_op jit(solution)/shard_map/all_to_all | solution.py:163
  208.5 7.0 %fusion.5 = bf16[2304,512]{1,0:T(8,128)(2,1)S(1)} fusion(bf16[768,2304]{1,0:T(8,128)(2,1)} %collective-permute-done.7, bf16[768,2304]{1,0:T(8,128)(2,1)} %bitcast.9, bf16[768,512]{1,0:T(8,128)(2,1)S(1)} %copy-done.7, bf16[768,512]{1,0:T(8,128)(2,1)S(1)} %fusion.23), kind=kOutput, calls=%fused_computation.7 | convolution fusion | flops 3642359808 | bytes 11010048 | tf_op jit(solution)/shard_map/dot_general | solution.py:149
  215.4 1.4 copy-done.5
  216.9 1.2 collective-permute-start.8
  218.1 1.5 collective-permute-start.9
  219.7 1.9 dynamic-slice_bitcast_fusion.3
  221.6 2.7 %collective-permute-start.12 = (bf16[288,512]{1,0:T(8,128)(2,1)}, bf16[288,512]{1,0:T(8,128)(2,1)}, u32[]{:S(2)}, u32[]{:S(2)}) collective-permute-start(bf16[288,512]{1,0:T(8,128)(2,1)} %get-tuple-element.37), channel_id=1, source_target_pairs={{0,192},{64,0},{128,64},{192,128},{1,193},{65,1},{129,65},{193,129... | collective-permute-start | bytes 884744 | tf_op jit(solution)/shard_map/ppermute | solution.py:12
  224.2 2.8 %broadcast_in_dim.18 = f32[576,2048]{1,0:T(8,128)} broadcast(f32[]{:T(128)} %constant.136.clone.1), dimensions={} | broadcast | bytes 4718596 | tf_op jit(solution)/shard_map/broadcast_in_dim | solution.py:154
  227.0 2.2 convert_dynamic-update-slice_fusion
  229.2 14.6 %collective-permute-done.10 = bf16[288,512]{1,0:T(8,128)(2,1)} collective-permute-done((bf16[288,512]{1,0:T(8,128)(2,1)}, bf16[288,512]{1,0:T(8,128)(2,1)}, u32[]{:S(2)}, u32[]{:S(2)}) %collective-permute-start.10) | collective-permute-done | bytes 294944 | tf_op jit(solution)/shard_map/ppermute | solution.py:12
  243.8 2.7 %collective-permute-start.13 = (bf16[288,512]{1,0:T(8,128)(2,1)}, bf16[288,512]{1,0:T(8,128)(2,1)S(1)}, u32[]{:S(2)}, u32[]{:S(2)}) collective-permute-start(bf16[288,512]{1,0:T(8,128)(2,1)} %collective-permute-done.12), channel_id=1, source_target_pairs={{0,192},{64,0},{128,64},{192,128},{1,193},{65,1},{129,65},{193,129... | collective-permute-start | bytes 884744 | tf_op jit(solution)/shard_map/ppermute | solution.py:12
  246.5 1.2 convert_dynamic-update-slice_fusion.3
  247.7 1.2 convert_dynamic-update-slice_fusion.2
  248.9 2.9 %collective-permute-done.11 = bf16[288,512]{1,0:T(8,128)(2,1)S(1)} collective-permute-done((bf16[288,512]{1,0:T(8,128)(2,1)}, bf16[288,512]{1,0:T(8,128)(2,1)S(1)}, u32[]{:S(2)}, u32[]{:S(2)}) %collective-permute-start.11) | collective-permute-done | bytes 294944 | tf_op jit(solution)/shard_map/ppermute | solution.py:12
  251.8 1.2 convert_dynamic-update-slice_fusion.1
  253.1 0.6 reshape.125
  (79 shorter events, 3.4 us)
Async XLA Ops:
  0.6 7.2 %collective-permute-start = (bf16[48,2304]{1,0:T(8,128)(2,1)}, bf16[48,2304]{1,0:T(8,128)(2,1)S(1)}, u32[]{:S(2)}, u32[]{:S(2)}) collective-permute-start(bf16[48,2304]{1,0:T(8,128)(2,1)} %param.3), channel_id=1, source_target_pairs={{0,64},{64,128},{128,192},{192,0},{1,65},{65,129},{129,193},{193,1... | collective-permute-start | bytes 663560 | tf_op jit(solution)/shard_map/ppermute | solution.py:12
  2.8 6.0 %collective-permute-start.1 = (bf16[48,2304]{1,0:T(8,128)(2,1)}, bf16[48,2304]{1,0:T(8,128)(2,1)S(1)}, u32[]{:S(2)}, u32[]{:S(2)}) collective-permute-start(bf16[48,2304]{1,0:T(8,128)(2,1)} %param.3), channel_id=1, source_target_pairs={{0,192},{64,0},{128,64},{192,128},{1,193},{65,1},{129,65},{193,129... | collective-permute-start | bytes 663560 | tf_op jit(solution)/shard_map/ppermute | solution.py:12
  4.4 10.9 %collective-permute-start.2 = (bf16[48,2304]{1,0:T(8,128)(2,1)}, bf16[48,2304]{1,0:T(8,128)(2,1)S(1)}, u32[]{:S(2)}, u32[]{:S(2)}) collective-permute-start(bf16[48,2304]{1,0:T(8,128)(2,1)} %param.3), channel_id=1, source_target_pairs={{0,128},{64,192},{128,0},{192,64},{1,129},{65,193},{129,1},{193,65... | collective-permute-start | bytes 663560 | tf_op jit(solution)/shard_map/ppermute | solution.py:12
  15.3 21.0 %collective-permute-start.3 = (bf16[192,2304]{1,0:T(8,128)(2,1)S(1)}, bf16[192,2304]{1,0:T(8,128)(2,1)S(1)}, u32[]{:S(2)}, u32[]{:S(2)}) collective-permute-start(bf16[192,2304]{1,0:T(8,128)(2,1)S(1)} %bitcast.81), channel_id=1, source_target_pairs={{0,16},{8,24},{16,32},{24,40},{32,48},{40,56},{48,0},{56,8},{1,17}... | collective-permute-start | bytes 2654216 | tf_op jit(solution)/shard_map/ppermute | solution.py:17
  16.6 19.8 %collective-permute-start.4 = (bf16[192,2304]{1,0:T(8,128)(2,1)S(1)}, bf16[192,2304]{1,0:T(8,128)(2,1)S(1)}, u32[]{:S(2)}, u32[]{:S(2)}) collective-permute-start(bf16[192,2304]{1,0:T(8,128)(2,1)S(1)} %bitcast.82), channel_id=1, source_target_pairs={{0,48},{8,56},{16,0},{24,8},{32,16},{40,24},{48,32},{56,40},{1,49}... | collective-permute-start | bytes 2654216 | tf_op jit(solution)/shard_map/ppermute | solution.py:17
  36.3 10.6 %collective-permute-start.5 = (bf16[96,2304]{1,0:T(8,128)(2,1)S(1)}, bf16[96,2304]{1,0:T(8,128)(2,1)S(1)}, u32[]{:S(2)}, u32[]{:S(2)}) collective-permute-start(bf16[96,2304]{1,0:T(8,128)(2,1)S(1)} %slice.84), channel_id=1, source_target_pairs={{0,16},{8,24},{16,32},{24,40},{32,48},{40,56},{48,0},{56,8},{1,17}... | collective-permute-start | bytes 1327112 | tf_op jit(solution)/shard_map/ppermute | solution.py:17
  36.4 10.5 %collective-permute-start.6 = (bf16[96,2304]{1,0:T(8,128)(2,1)S(1)}, bf16[96,2304]{1,0:T(8,128)(2,1)S(1)}, u32[]{:S(2)}, u32[]{:S(2)}) collective-permute-start(bf16[96,2304]{1,0:T(8,128)(2,1)S(1)} %slice.85), channel_id=1, source_target_pairs={{0,48},{8,56},{16,0},{24,8},{32,16},{40,24},{48,32},{56,40},{1,49}... | collective-permute-start | bytes 1327112 | tf_op jit(solution)/shard_map/ppermute | solution.py:17
  40.1 11.1 %copy-start.4 = (bf16[2048,576]{0,1:T(8,128)(2,1)S(1)}, bf16[2048,576]{0,1:T(8,128)(2,1)}, u32[]{:S(2)}) copy-start(bf16[2048,576]{0,1:T(8,128)(2,1)} %param.4) | copy-start | bytes 7077892
  47.9 39.1 %collective-permute-start.7 = (bf16[768,2304]{1,0:T(8,128)(2,1)}, bf16[768,2304]{1,0:T(8,128)(2,1)}, u32[]{:S(2)}, u32[]{:S(2)}) collective-permute-start(bf16[768,2304]{1,0:T(8,128)(2,1)} %bitcast.9), channel_id=1, source_target_pairs={{0,8},{8,0},{16,24},{24,16},{32,40},{40,32},{48,56},{56,48},{1,9},... | collective-permute-start | bytes 10616840 | tf_op jit(solution)/shard_map/ppermute | solution.py:22
  53.1 4.7 %copy-start = (bf16[384,2048]{1,0:T(8,128)(2,1)S(1)}, bf16[384,2048]{1,0:T(8,128)(2,1)}, u32[]{:S(2)}) copy-start(bf16[384,2048]{1,0:T(8,128)(2,1)} %param.5) | copy-start | bytes 4718596
  53.1 33.9 %all-to-all-start = ((bf16[4,576,512]{2,1,0:T(8,128)(2,1)}), bf16[4,576,512]{2,1,0:T(8,128)(2,1)}, u32[]{:S(2)}, u32[]{:S(2)}) async-start(bf16[4,576,512]{2,1,0:T(8,128)(2,1)} %pad_maximum_fusion.5), calls=%async_computation | async-start | bytes 4718592 | tf_op jit(solution)/shard_map/all_to_all | solution.py:96
  94.8 1.7 copy-start.1
  98.4 14.7 %all-to-all-start.1 = ((f32[32,1,1920]{2,1,0:T(1,128)}), f32[32,1,1920]{2,1,0:T(1,128)S(1)}, u32[]{:S(2)}, u32[]{:S(2)}) async-start(f32[32,1,1920]{2,1,0:T(1,128)} %broadcast_in_dim.49), calls=%async_computation.1 | async-start | bytes 491520 | tf_op jit(solution)/shard_map/all_to_all | solution.py:66
  113.1 25.1 %all-to-all-start.3 = ((bf16[4,384,512]{2,1,0:T(8,128)(2,1)}), bf16[4,384,512]{2,1,0:T(8,128)(2,1)}, u32[]{:S(2)}, u32[]{:S(2)}) async-start(bf16[4,384,512]{2,1,0:T(8,128)(2,1)} %pad_maximum_fusion.6), calls=%async_computation.3 | async-start | bytes 3145728 | tf_op jit(solution)/shard_map/all_to_all | solution.py:98
  117.4 44.3 %collective-permute-start.15 = (bf16[2304,512]{1,0:T(8,128)(2,1)}, bf16[2304,512]{1,0:T(8,128)(2,1)}, u32[]{:S(2)}, u32[]{:S(2)}) collective-permute-start(bf16[2304,512]{1,0:T(8,128)(2,1)} %bitcast.15), channel_id=1, source_target_pairs={{0,8},{8,0},{16,24},{24,16},{32,40},{40,32},{48,56},{56,48},{1,9},... | collective-permute-start | bytes 7077896 | tf_op jit(solution)/shard_map/ppermute | solution.py:22
  117.7 37.4 %copy-start.2 = (f32[1536,512]{1,0:T(8,128)S(1)}, f32[1536,512]{1,0:T(8,128)}, u32[]{:S(2)}) copy-start(f32[1536,512]{1,0:T(8,128)} %copy-done.1) | copy-start | bytes 9437188
  138.9 15.8 %all-to-all-start.2 = ((f32[8,1,3072]{2,1,0:T(1,128)}), f32[8,1,3072]{2,1,0:T(1,128)S(1)}, u32[]{:S(2)}, u32[]{:S(2)}) async-start(f32[8,1,3072]{2,1,0:T(1,128)} %broadcast_in_dim.50), calls=%async_computation.2 | async-start | bytes 196608 | tf_op jit(solution)/shard_map/all_to_all | solution.py:66
  155.1 4.4 %copy-start.3 = (bf16[4,4,1,48,512]{4,3,2,1,0:T(8,128)(2,1)S(1)}, bf16[4,4,1,48,512]{4,3,2,1,0:T(8,128)(2,1)}, u32[]{:S(2)}) copy-start(bf16[4,4,1,48,512]{4,3,2,1,0:T(8,128)(2,1)} %get-tuple-element.48) | copy-start | bytes 2359300
  156.9 4.6 %copy-start.6 = (bf16[768,512]{1,0:T(8,128)(2,1)}, bf16[768,512]{1,0:T(8,128)(2,1)S(1)}, u32[]{:S(2)}) copy-start(bf16[768,512]{1,0:T(8,128)(2,1)S(1)} %get-tuple-element.13) | copy-start | bytes 2359300
  157.0 4.4 %collective-permute-start.14 = (bf16[768,512]{1,0:T(8,128)(2,1)S(1)}, bf16[768,512]{1,0:T(8,128)(2,1)S(1)}, u32[]{:S(2)}, u32[]{:S(2)}) collective-permute-start(bf16[768,512]{1,0:T(8,128)(2,1)S(1)} %get-tuple-element.13), channel_id=1, source_target_pairs={{0,8},{8,0},{16,24},{24,16},{32,40},{40,32},{48,56},{56,48},{1,9},... | collective-permute-start | bytes 2359304 | tf_op jit(solution)/shard_map/ppermute | solution.py:22
  168.3 12.6 %collective-permute-start.16 = (bf16[96,2304]{1,0:T(8,128)(2,1)S(1)}, bf16[96,2304]{1,0:T(8,128)(2,1)S(1)}, u32[]{:S(2)}, u32[]{:S(2)}) collective-permute-start(bf16[96,2304]{1,0:T(8,128)(2,1)S(1)} %get-tuple-element.16), channel_id=1, source_target_pairs={{0,16},{8,24},{16,32},{24,40},{32,48},{40,56},{48,0},{56,8},{1,17}... | collective-permute-start | bytes 1327112 | tf_op jit(solution)/shard_map/ppermute | solution.py:17
  168.8 12.4 %collective-permute-start.20 = (bf16[96,2304]{1,0:T(8,128)(2,1)S(1)}, bf16[96,2304]{1,0:T(8,128)(2,1)S(1)}, u32[]{:S(2)}, u32[]{:S(2)}) collective-permute-start(bf16[96,2304]{1,0:T(8,128)(2,1)S(1)} %get-tuple-element.21), channel_id=1, source_target_pairs={{0,48},{8,56},{16,0},{24,8},{32,16},{40,24},{48,32},{56,40},{1,49}... | collective-permute-start | bytes 1327112 | tf_op jit(solution)/shard_map/ppermute | solution.py:17
  171.0 18.3 %collective-permute-start.18 = (bf16[96,2304]{1,0:T(8,128)(2,1)S(1)}, bf16[96,2304]{1,0:T(8,128)(2,1)S(1)}, u32[]{:S(2)}, u32[]{:S(2)}) collective-permute-start(bf16[96,2304]{1,0:T(8,128)(2,1)S(1)} %get-tuple-element.17), channel_id=1, source_target_pairs={{0,48},{8,56},{16,0},{24,8},{32,16},{40,24},{48,32},{56,40},{1,49}... | collective-permute-start | bytes 1327112 | tf_op jit(solution)/shard_map/ppermute | solution.py:17
  181.0 11.8 %collective-permute-start.17 = (bf16[96,2304]{1,0:T(8,128)(2,1)S(1)}, bf16[96,2304]{1,0:T(8,128)(2,1)S(1)}, u32[]{:S(2)}, u32[]{:S(2)}) collective-permute-start(bf16[96,2304]{1,0:T(8,128)(2,1)S(1)} %add.203), channel_id=1, source_target_pairs={{0,16},{8,24},{16,32},{24,40},{32,48},{40,56},{48,0},{56,8},{1,17}... | collective-permute-start | bytes 1327112 | tf_op jit(solution)/shard_map/ppermute | solution.py:17
  181.1 21.2 %collective-permute-start.19 = (bf16[96,2304]{1,0:T(8,128)(2,1)S(1)}, bf16[96,2304]{1,0:T(8,128)(2,1)S(1)}, u32[]{:S(2)}, u32[]{:S(2)}) collective-permute-start(bf16[96,2304]{1,0:T(8,128)(2,1)S(1)} %get-tuple-element.19), channel_id=1, source_target_pairs={{0,16},{8,24},{16,32},{24,40},{32,48},{40,56},{48,0},{56,8},{1,17}... | collective-permute-start | bytes 1327112 | tf_op jit(solution)/shard_map/ppermute | solution.py:17
  181.3 21.0 %collective-permute-start.21 = (bf16[96,2304]{1,0:T(8,128)(2,1)S(1)}, bf16[96,2304]{1,0:T(8,128)(2,1)S(1)}, u32[]{:S(2)}, u32[]{:S(2)}) collective-permute-start(bf16[96,2304]{1,0:T(8,128)(2,1)S(1)} %add.207), channel_id=1, source_target_pairs={{0,48},{8,56},{16,0},{24,8},{32,16},{40,24},{48,32},{56,40},{1,49}... | collective-permute-start | bytes 1327112 | tf_op jit(solution)/shard_map/ppermute | solution.py:17
  202.4 6.0 %copy-start.7 = (bf16[768,512]{1,0:T(8,128)(2,1)S(1)}, bf16[768,512]{1,0:T(8,128)(2,1)}, u32[]{:S(2)}) copy-start(bf16[768,512]{1,0:T(8,128)(2,1)} %copy-done.6) | copy-start | bytes 2359300
  204.5 48.5 %all-to-all-start.4 = ((bf16[32,108,128]{2,1,0:T(8,128)(2,1)}), bf16[32,108,128]{2,1,0:T(8,128)(2,1)S(1)}, u32[]{:S(2)}, u32[]{:S(2)}) async-start(bf16[32,108,128]{2,1,0:T(8,128)(2,1)} %convert_element_type.88), calls=%async_computation.4 | async-start | bytes 1835008 | tf_op jit(solution)/shard_map/all_to_all | solution.py:163
  215.4 1.4 copy-start.5
  216.9 29.6 %collective-permute-start.8 = (bf16[576,512]{1,0:T(8,128)(2,1)S(1)}, bf16[576,512]{1,0:T(8,128)(2,1)S(1)}, u32[]{:S(2)}, u32[]{:S(2)}) collective-permute-start(bf16[576,512]{1,0:T(8,128)(2,1)S(1)} %get-tuple-element.39), channel_id=1, source_target_pairs={{0,64},{64,128},{128,192},{192,0},{1,65},{65,129},{129,193},{193,1... | collective-permute-start | bytes 1769480 | tf_op jit(solution)/shard_map/ppermute | solution.py:12
  218.1 29.6 %collective-permute-start.9 = (bf16[576,512]{1,0:T(8,128)(2,1)S(1)}, bf16[576,512]{1,0:T(8,128)(2,1)S(1)}, u32[]{:S(2)}, u32[]{:S(2)}) collective-permute-start(bf16[576,512]{1,0:T(8,128)(2,1)S(1)} %get-tuple-element.38), channel_id=1, source_target_pairs={{0,192},{64,0},{128,64},{192,128},{1,193},{65,1},{129,65},{193,129... | collective-permute-start | bytes 1769480 | tf_op jit(solution)/shard_map/ppermute | solution.py:12
  221.6 22.3 %collective-permute-start.10 = (bf16[288,512]{1,0:T(8,128)(2,1)}, bf16[288,512]{1,0:T(8,128)(2,1)}, u32[]{:S(2)}, u32[]{:S(2)}) collective-permute-start(bf16[288,512]{1,0:T(8,128)(2,1)} %get-tuple-element.36), channel_id=1, source_target_pairs={{0,64},{64,128},{128,192},{192,0},{1,65},{65,129},{129,193},{193,1... | collective-permute-start | bytes 884744 | tf_op jit(solution)/shard_map/ppermute | solution.py:12
  221.6 22.3 %collective-permute-start.12 = (bf16[288,512]{1,0:T(8,128)(2,1)}, bf16[288,512]{1,0:T(8,128)(2,1)}, u32[]{:S(2)}, u32[]{:S(2)}) collective-permute-start(bf16[288,512]{1,0:T(8,128)(2,1)} %get-tuple-element.37), channel_id=1, source_target_pairs={{0,192},{64,0},{128,64},{192,128},{1,193},{65,1},{129,65},{193,129... | collective-permute-start | bytes 884744 | tf_op jit(solution)/shard_map/ppermute | solution.py:12
  243.8 8.0 %collective-permute-start.11 = (bf16[288,512]{1,0:T(8,128)(2,1)}, bf16[288,512]{1,0:T(8,128)(2,1)S(1)}, u32[]{:S(2)}, u32[]{:S(2)}) collective-permute-start(bf16[288,512]{1,0:T(8,128)(2,1)} %collective-permute-done.10), channel_id=1, source_target_pairs={{0,64},{64,128},{128,192},{192,0},{1,65},{65,129},{129,193},{193,1... | collective-permute-start | bytes 884744 | tf_op jit(solution)/shard_map/ppermute | solution.py:12
  243.8 8.0 %collective-permute-start.13 = (bf16[288,512]{1,0:T(8,128)(2,1)}, bf16[288,512]{1,0:T(8,128)(2,1)S(1)}, u32[]{:S(2)}, u32[]{:S(2)}) collective-permute-start(bf16[288,512]{1,0:T(8,128)(2,1)} %collective-permute-done.12), channel_id=1, source_target_pairs={{0,192},{64,0},{128,64},{192,128},{1,193},{65,1},{129,65},{193,129... | collective-permute-start | bytes 884744 | tf_op jit(solution)/shard_map/ppermute | solution.py:12

commit v7 on v6

--- a/solution.py
+++ b/solution.py
@@ -48,10 +48,12 @@
     return ((0, piece(0)), (3, back), (1, front), (2, jnp.concatenate(far)))
 
 
-def ring_sum(parts, shift):
+def ring_sum(part, shift):
     f32 = jnp.float32
-    halves = lax.optimization_barrier(jnp.split(parts, 8))
-    far, ahead, behind, own = zip(halves[::2], halves[1::2])
+    far = lax.optimization_barrier(jnp.split(part(2), 2))
+    rest = part(1, 3, 0)
+    halves = lax.optimization_barrier(jnp.split(rest, 6))
+    ahead, behind, own = zip(halves[::2], halves[1::2])
     right, left = shift(far[0], 1), shift(far[1], -1)
     back_b = shift(ahead[1], 1)
     front_a = shift(behind[0], -1)
@@ -106,11 +108,13 @@
     own = own.reshape(half, width)
     other = swap_core(own)
 
-    states = jnp.concatenate([own, other])
-    logits = jnp.dot(states, table, preferred_element_type=f32)
-    logits = with_layout_constraint(logits, Layout((0, 1)))
-    lse_s = logsum(logits, 1)
-    lse_s = ordered(core, lse_s[:half], lse_s[half:])
+    def scores(states):
+        logits = jnp.dot(states, table, preferred_element_type=f32)
+        return with_layout_constraint(logits, Layout((0, 1)))
+
+    logits_own = scores(own)
+    logits_other = scores(other)
+    lse_s = ordered(core, logsum(logits_own, 1), logsum(logits_other, 1))
     lse_t = logsum(teacher.astype(f32), 1)
     got = spread(jnp.concatenate([lse_s.reshape(2 * half), lse_t]), ("layer", "row"))
     lse_s = logsum(got[:, : 2 * half], 0)
@@ -126,9 +130,9 @@
         prob_t = jnp.exp(taught_c - at(lse_t, c)[:, None])
         return ((prob_s - prob_t) * LOSS_SCALE).astype(bf16)
 
-    grads_other = gradient(logits[half:], taught[1], 1 - core)
+    grads_other = gradient(logits_other, taught[1], 1 - core)
     crossed = swap_core(grads_other)
-    logits_own, grads_other = lax.optimization_barrier((logits[:half], grads_other))
+    logits_own, grads_other = lax.optimization_barrier((logits_own, grads_other))
     grads_own = gradient(logits_own, taught[0], core)
     other_table = swap_core(table)
 
@@ -143,11 +147,12 @@
             jnp.concatenate(picked), tables, (((1,), (1,)), ((), ())), preferred_element_type=f32
         ).astype(bf16)
 
-    summed = ring_sum(part(2, 1, 3, 0), shift_x).astype(bf16)
+    summed = ring_sum(part, shift_x).astype(bf16)
 
     grads = jnp.concatenate([grads_own, grads_other])
     grad_table = lax.dot_general(
-        states, grads, (((0,), (0,)), ((), ())), preferred_element_type=f32
+        jnp.concatenate([own, other]), grads, (((0,), (0,)), ((), ())),
+        preferred_element_type=f32,
     ).astype(bf16)
     grad_table = grad_table.reshape(layers, quarter, block)
     pieces = ring_exchange(lambda k: at(grad_table, (y + k) % layers), shift_y)

time: 256 us -> 260 us (1.016)
  matrix products: 21 us -> 26 us
  waiting for transfers between devices: 137 us -> 134 us
    dot_general x1 -> x2, matrix products: 6.25 us -> 9.39 us  [part(): lax.dot_general(jnp.concatenate(picked), tables, (((1,), (1,)), ((), ()))...]
    dot_general x2 -> x3, matrix products: 14.8 us -> 16.6 us  [the longest x2 9.61 us: scores(): logits = jnp.dot(states, table, preferred_element_type=f32)]
  transfers between devices with their start and end apart: 27 -> 27, of which waited for: 16 -> 18; matrix products, arithmetic and copies ran while one was open for 14% -> 18% of each run, Pallas kernels for 0% -> 0%
where the time goes in v7:
time: 260 us; the launch traced here: 258 us
  waiting for transfers between devices  134 us (52%)
  starting transfers between devices  60.3 us (23%)
  matrix products  26 us (10%)
  local copies, waits for them, and re-layouts  22.3 us (9%)
  other arithmetic  14.3 us (6%)
    ppermute x10, waiting for transfers between devices, shift_x(): return lax.ppermute(x, 'row', [(i, (i + 2 * s) % n) for i in range(n)])  46.3 us
    all_to_all x1, waiting for transfers between devices, local(): table = lax.all_to_all(cut(embedding.T), 'layer', 0, 0, tiled=True)  28.1 us
    ppermute x9, waiting for transfers between devices, shift_y(): return lax.ppermute(x, 'layer', [(i, (i + s) % n) for i in range(n)])  25.4 us
    all_to_all x1, waiting for transfers between devices, local(): taught = lax.all_to_all(cut(teacher), 'layer', 0, 0, tiled=True)  20.1 us
    ppermute x9, starting transfers between devices, shift_y(): return lax.ppermute(x, 'layer', [(i, (i + s) % n) for i in range(n)])  14.2 us
    all_to_all x2, starting transfers between devices, spread(): lax.all_to_all(jnp.broadcast_to(x[None], (n, *x.shape)), axis, 0, 0, tile...  13.1 us
    ppermute x10, starting transfers between devices, shift_x(): return lax.ppermute(x, 'row', [(i, (i + 2 * s) % n) for i in range(n)])  12.9 us
    all_to_all x2, waiting for transfers between devices, spread(): lax.all_to_all(jnp.broadcast_to(x[None], (n, *x.shape)), axis, 0, 0, tile...  12.3 us
  transfers between devices with their start and end apart: 27, of which 18 were waited for; matrix products, arithmetic and copies ran while one was open for 18% of the time, Pallas kernels for 0%

profile of v7, /device:TPU:1, one launch (start us, length us, event | category | flops | bytes accessed | tf_op | source)
XLA Modules:
  0.0 257.5 jit_solution(2799903646413407125)
XLA Ops:
  0.6 2.2 collective-permute-start
  2.8 2.6 %collective-permute-start.2 = (bf16[48,2304]{1,0:T(8,128)(2,1)}, bf16[48,2304]{1,0:T(8,128)(2,1)S(1)}, u32[]{:S(2)}, u32[]{:S(2)}) collective-permute-start(bf16[48,2304]{1,0:T(8,128)(2,1)} %param.3), channel_id=1, source_target_pairs={{0,128},{64,192},{128,0},{192,64},{1,129},{65,193},{129,1},{193,65... | collective-permute-start | bytes 663560 | tf_op jit(solution)/shard_map/ppermute | solution.py:12
  5.4 1.1 collective-permute-start.1
  6.6 1.0 bitcast_dynamic-update-slice_fusion.4
  7.8 6.3 %collective-permute-done.1 = bf16[48,2304]{1,0:T(8,128)(2,1)S(1)} collective-permute-done((bf16[48,2304]{1,0:T(8,128)(2,1)}, bf16[48,2304]{1,0:T(8,128)(2,1)S(1)}, u32[]{:S(2)}, u32[]{:S(2)}) %collective-permute-start.1) | collective-permute-done | bytes 221216 | tf_op jit(solution)/shard_map/ppermute | solution.py:12
  14.1 1.1 collective-permute-done.2
  15.3 2.6 collective-permute-start.4
  17.8 2.0 broadcast_in_dim.19
  19.9 1.0 bitcast_dynamic-update-slice_fusion
  20.8 14.5 %collective-permute-done.4 = bf16[192,2304]{1,0:T(8,128)(2,1)S(1)} collective-permute-done((bf16[192,2304]{1,0:T(8,128)(2,1)S(1)}, bf16[192,2304]{1,0:T(8,128)(2,1)S(1)}, u32[]{:S(2)}, u32[]{:S(2)}) %collective-permute-start.4) | collective-permute-done | bytes 884768 | tf_op jit(solution)/shard_map/ppermute | solution.py:17
  35.3 3.5 %collective-permute-start.6 = (bf16[96,2304]{1,0:T(8,128)(2,1)S(1)}, bf16[96,2304]{1,0:T(8,128)(2,1)S(1)}, u32[]{:S(2)}, u32[]{:S(2)}) collective-permute-start(bf16[96,2304]{1,0:T(8,128)(2,1)S(1)} %slice.69), channel_id=1, source_target_pairs={{0,48},{8,56},{16,0},{24,8},{32,16},{40,24},{48,32},{56,40},{1,49}... | collective-permute-start | bytes 1327112 | tf_op jit(solution)/shard_map/ppermute | solution.py:17
  38.9 1.0 constant_dynamic-update-slice_fusion.2
  39.9 1.0 constant_dynamic-update-slice_fusion.1
  40.9 5.1 %collective-permute-done.6 = bf16[96,2304]{1,0:T(8,128)(2,1)S(1)} collective-permute-done((bf16[96,2304]{1,0:T(8,128)(2,1)S(1)}, bf16[96,2304]{1,0:T(8,128)(2,1)S(1)}, u32[]{:S(2)}, u32[]{:S(2)}) %collective-permute-start.6) | collective-permute-done | bytes 442400 | tf_op jit(solution)/shard_map/ppermute | solution.py:17
  46.0 3.2 %collective-permute-done.5 = bf16[96,2304]{1,0:T(8,128)(2,1)S(1)} collective-permute-done((bf16[96,2304]{1,0:T(8,128)(2,1)S(1)}, bf16[96,2304]{1,0:T(8,128)(2,1)S(1)}, u32[]{:S(2)}, u32[]{:S(2)}) %collective-permute-start.5) | collective-permute-done | bytes 442400 | tf_op jit(solution)/shard_map/ppermute | solution.py:17
  49.3 1.0 constant_dynamic-update-slice_fusion
  50.2 3.5 %collective-permute-start.7 = (bf16[768,2304]{1,0:T(8,128)(2,1)}, bf16[768,2304]{1,0:T(8,128)(2,1)}, u32[]{:S(2)}, u32[]{:S(2)}) collective-permute-start(bf16[768,2304]{1,0:T(8,128)(2,1)} %bitcast.9), channel_id=1, source_target_pairs={{0,8},{8,0},{16,24},{24,16},{32,40},{40,32},{48,56},{56,48},{1,9},... | collective-permute-start | bytes 10616840 | tf_op jit(solution)/shard_map/ppermute | solution.py:22
  53.9 1.7 pad_maximum_fusion.3
  55.7 5.4 %all-to-all-start = ((bf16[4,576,512]{2,1,0:T(8,128)(2,1)}), bf16[4,576,512]{2,1,0:T(8,128)(2,1)}, u32[]{:S(2)}, u32[]{:S(2)}) async-start(bf16[4,576,512]{2,1,0:T(8,128)(2,1)} %pad_maximum_fusion.3), calls=%async_computation | async-start | bytes 4718592 | tf_op jit(solution)/shard_map/all_to_all | solution.py:98
  61.4 0.7 exponential_reduce_fusion
  62.0 28.1 %all-to-all-done = bf16[4,576,512]{2,1,0:T(8,128)(2,1)} async-done(((bf16[4,576,512]{2,1,0:T(8,128)(2,1)}), bf16[4,576,512]{2,1,0:T(8,128)(2,1)}, u32[]{:S(2)}, u32[]{:S(2)}) %all-to-all-start) | async-done | bytes 2359328 | tf_op jit(solution)/shard_map/all_to_all | solution.py:98
  90.2 4.8 %fusion.37 = (f32[768]{0:T(1024)S(1)}, f32[768,512]{1,0:T(8,128)S(1)}) fusion(bf16[768,2304]{1,0:T(8,128)(2,1)} %bitcast.9, bf16[2304,512]{1,0:T(8,128)(2,1)} %bitcast.15), kind=kOutput, calls=%fused_computation.100 | convolution fusion | flops 1812331776 | bytes 7474176 | tf_op jit(solution)/shard_map/dot_general | solution.py:112
  95.5 4.8 %fusion.36 = (f32[768]{0:T(1024)S(1)}, f32[768,512]{1,0:T(8,128)S(1)}) fusion(bf16[768,2304]{1,0:T(8,128)(2,1)} %collective-permute-done.7, bf16[2304,512]{1,0:T(8,128)(2,1)} %bitcast.15), kind=kOutput, calls=%fused_computation.99 | convolution fusion | flops 1812331776 | bytes 7474176 | tf_op jit(solution)/shard_map/dot_general | solution.py:112
  100.3 1.3 copy-done.1
  102.1 0.8 broadcast_in_dim.50
  102.9 4.9 %all-to-all-start.1 = ((f32[32,1,1920]{2,1,0:T(1,128)}), f32[32,1,1920]{2,1,0:T(1,128)S(1)}, u32[]{:S(2)}, u32[]{:S(2)}) async-start(f32[32,1,1920]{2,1,0:T(1,128)} %broadcast_in_dim.50), calls=%async_computation.1 | async-start | bytes 491520 | tf_op jit(solution)/shard_map/all_to_all | solution.py:68
  107.9 1.4 pad_maximum_fusion.4
  109.3 7.3 %all-to-all-done.1 = f32[32,1,1920]{2,1,0:T(1,128)S(1)} async-done(((f32[32,1,1920]{2,1,0:T(1,128)}), f32[32,1,1920]{2,1,0:T(1,128)S(1)}, u32[]{:S(2)}, u32[]{:S(2)}) %all-to-all-start.1) | async-done | bytes 245792 | tf_op jit(solution)/shard_map/all_to_all | solution.py:68
  116.6 4.4 %all-to-all-start.3 = ((bf16[4,384,512]{2,1,0:T(8,128)(2,1)}), bf16[4,384,512]{2,1,0:T(8,128)(2,1)}, u32[]{:S(2)}, u32[]{:S(2)}) async-start(bf16[4,384,512]{2,1,0:T(8,128)(2,1)} %pad_maximum_fusion.4), calls=%async_computation.3 | async-start | bytes 3145728 | tf_op jit(solution)/shard_map/all_to_all | solution.py:100
  121.6 20.1 %all-to-all-done.3 = bf16[4,384,512]{2,1,0:T(8,128)(2,1)} async-done(((bf16[4,384,512]{2,1,0:T(8,128)(2,1)}), bf16[4,384,512]{2,1,0:T(8,128)(2,1)}, u32[]{:S(2)}, u32[]{:S(2)}) %all-to-all-start.3) | async-done | bytes 1572896 | tf_op jit(solution)/shard_map/all_to_all | solution.py:100
  141.7 0.7 broadcast_in_dim.51
  142.4 8.2 %all-to-all-start.2 = ((f32[8,1,3072]{2,1,0:T(1,128)}), f32[8,1,3072]{2,1,0:T(1,128)S(1)}, u32[]{:S(2)}, u32[]{:S(2)}) async-start(f32[8,1,3072]{2,1,0:T(1,128)} %broadcast_in_dim.51), calls=%async_computation.2 | async-start | bytes 196608 | tf_op jit(solution)/shard_map/all_to_all | solution.py:68
  150.6 2.7 %constant_dynamic-slice_fusion.5 = (bf16[4,4,1,48,512]{4,3,2,1,0:T(8,128)(2,1)}, bf16[4,4,1,48,512]{4,3,2,1,0:T(8,128)(2,1)}) fusion(bf16[4,4,2,48,512]{4,3,2,1,0:T(8,128)(2,1)} %bitcast.21, s32[]{:T(128)S(6)} %select_n.159, s32[]{:T(128)S(6)} %select_n.158), kind=kLoop, calls=%fused_computation.76 | loop fusion | bytes 3145736 | tf_op jit(solution)/shard_map/jit(dynamic_index_in_dim)/dynamic_slice | solution.py:26
  153.2 4.9 %all-to-all-done.2 = f32[8,1,3072]{2,1,0:T(1,128)S(1)} async-done(((f32[8,1,3072]{2,1,0:T(1,128)}), f32[8,1,3072]{2,1,0:T(1,128)S(1)}, u32[]{:S(2)}, u32[]{:S(2)}) %all-to-all-start.2) | async-done | bytes 98336 | tf_op jit(solution)/shard_map/all_to_all | solution.py:68
  158.6 1.7 fusion.17
  160.4 2.5 collective-permute-start.14
  162.9 0.6 fusion.13
  163.4 1.3 collective-permute-done.14
  165.2 4.1 %convolution_convert_fusion.1 = bf16[192,2304]{1,0:T(8,128)(2,1)S(1)} fusion(bf16[192,1024]{1,0:T(8,128)(2,1)S(1)} %bitcast.100, bf16[2304,512]{1,0:T(8,128)(2,1)} %collective-permute-done.15, bf16[2304,512]{1,0:T(8,128)(2,1)} %bitcast.15), kind=kOutput, calls=%fused_computation.7 | convolution fusion | flops 915849216 | bytes 5996544 | tf_op jit(solution)/shard_map/dot_general | solution.py:146
  169.9 5.3 %convolution_convert_fusion = bf16[576,2304]{1,0:T(8,128)(2,1)S(1)} fusion(bf16[2304,512]{1,0:T(8,128)(2,1)} %collective-permute-done.15, bf16[2304,512]{1,0:T(8,128)(2,1)} %bitcast.15, bf16[192,1024]{1,0:T(8,128)(2,1)S(1)} %bitcast.97, bf16[192,1024]{1,0:T(8,128)(2,1)S(1)} %bitcast.98, bf16[192,1024]{1,0:T(8,128)(2,1)S(1)} %bitcast.99), kind=kOutput, calls=%fused_computation.5 | convolution fusion | flops 2732212224 | bytes 8552448 | tf_op jit(solution)/shard_map/dot_general | solution.py:146
  175.4 2.3 collective-permute-start.20
  177.8 4.2 %collective-permute-done.16 = bf16[96,2304]{1,0:T(8,128)(2,1)S(1)} collective-permute-done((bf16[96,2304]{1,0:T(8,128)(2,1)S(1)}, bf16[96,2304]{1,0:T(8,128)(2,1)S(1)}, u32[]{:S(2)}, u32[]{:S(2)}) %collective-permute-start.16) | collective-permute-done | bytes 442400 | tf_op jit(solution)/shard_map/ppermute | solution.py:17
  182.3 4.3 %collective-permute-done.20 = bf16[96,2304]{1,0:T(8,128)(2,1)S(1)} collective-permute-done((bf16[96,2304]{1,0:T(8,128)(2,1)S(1)}, bf16[96,2304]{1,0:T(8,128)(2,1)S(1)}, u32[]{:S(2)}, u32[]{:S(2)}) %collective-permute-start.20) | collective-permute-done | bytes 442400 | tf_op jit(solution)/shard_map/ppermute | solution.py:17
  186.7 3.7 %collective-permute-start.21 = (bf16[96,2304]{1,0:T(8,128)(2,1)S(1)}, bf16[96,2304]{1,0:T(8,128)(2,1)S(1)}, u32[]{:S(2)}, u32[]{:S(2)}) collective-permute-start(bf16[96,2304]{1,0:T(8,128)(2,1)S(1)} %add.233), channel_id=1, source_target_pairs={{0,48},{8,56},{16,0},{24,8},{32,16},{40,24},{48,32},{56,40},{1,49}... | collective-permute-start | bytes 1327112 | tf_op jit(solution)/shard_map/ppermute | solution.py:17
  190.4 5.7 %collective-permute-done.18 = bf16[96,2304]{1,0:T(8,128)(2,1)S(1)} collective-permute-done((bf16[96,2304]{1,0:T(8,128)(2,1)S(1)}, bf16[96,2304]{1,0:T(8,128)(2,1)S(1)}, u32[]{:S(2)}, u32[]{:S(2)}) %collective-permute-start.18) | collective-permute-done | bytes 442400 | tf_op jit(solution)/shard_map/ppermute | solution.py:17
  196.2 7.1 %collective-permute-done.19 = bf16[96,2304]{1,0:T(8,128)(2,1)S(1)} collective-permute-done((bf16[96,2304]{1,0:T(8,128)(2,1)S(1)}, bf16[96,2304]{1,0:T(8,128)(2,1)S(1)}, u32[]{:S(2)}, u32[]{:S(2)}) %collective-permute-start.19) | collective-permute-done | bytes 442400 | tf_op jit(solution)/shard_map/ppermute | solution.py:17
  203.3 2.2 collective-permute-done.21
  205.8 2.0 convert_element_type.92
  207.8 3.9 %all-to-all-start.4 = ((bf16[32,108,128]{2,1,0:T(8,128)(2,1)}), bf16[32,108,128]{2,1,0:T(8,128)(2,1)S(1)}, u32[]{:S(2)}, u32[]{:S(2)}) async-start(bf16[32,108,128]{2,1,0:T(8,128)(2,1)} %convert_element_type.92), calls=%async_computation.4 | async-start | bytes 1835008 | tf_op jit(solution)/shard_map/all_to_all | solution.py:168
  211.7 7.0 %fusion.4 = bf16[2304,512]{1,0:T(8,128)(2,1)S(1)} fusion(bf16[768,2304]{1,0:T(8,128)(2,1)} %collective-permute-done.7, bf16[768,2304]{1,0:T(8,128)(2,1)} %bitcast.9, bf16[768,512]{1,0:T(8,128)(2,1)S(1)} %copy-done.9, bf16[768,512]{1,0:T(8,128)(2,1)S(1)} %copy-done.4), kind=kOutput, calls=%fused_computation.6 | convolution fusion | flops 3642359808 | bytes 11010048 | tf_op jit(solution)/shard_map/dot_general | solution.py:153
  218.7 1.4 copy-done.7
  220.2 1.2 collective-permute-start.8
  221.4 1.5 collective-permute-start.9
  222.9 1.9 dynamic-slice_bitcast_fusion.3
  224.8 2.7 %collective-permute-start.12 = (bf16[288,512]{1,0:T(8,128)(2,1)}, bf16[288,512]{1,0:T(8,128)(2,1)}, u32[]{:S(2)}, u32[]{:S(2)}) collective-permute-start(bf16[288,512]{1,0:T(8,128)(2,1)} %get-tuple-element.33), channel_id=1, source_target_pairs={{0,192},{64,0},{128,64},{192,128},{1,193},{65,1},{129,65},{193,129... | collective-permute-start | bytes 884744 | tf_op jit(solution)/shard_map/ppermute | solution.py:12
  227.5 2.8 %broadcast_in_dim.18 = f32[576,2048]{1,0:T(8,128)} broadcast(f32[]{:T(128)} %constant.136.clone.1), dimensions={} | broadcast | bytes 4718596 | tf_op jit(solution)/shard_map/broadcast_in_dim | solution.py:159
  230.3 2.2 convert_dynamic-update-slice_fusion
  232.5 14.9 %collective-permute-done.10 = bf16[288,512]{1,0:T(8,128)(2,1)} collective-permute-done((bf16[288,512]{1,0:T(8,128)(2,1)}, bf16[288,512]{1,0:T(8,128)(2,1)}, u32[]{:S(2)}, u32[]{:S(2)}) %collective-permute-start.10) | collective-permute-done | bytes 294944 | tf_op jit(solution)/shard_map/ppermute | solution.py:12
  247.4 2.9 %collective-permute-start.13 = (bf16[288,512]{1,0:T(8,128)(2,1)}, bf16[288,512]{1,0:T(8,128)(2,1)S(1)}, u32[]{:S(2)}, u32[]{:S(2)}) collective-permute-start(bf16[288,512]{1,0:T(8,128)(2,1)} %collective-permute-done.12), channel_id=1, source_target_pairs={{0,192},{64,0},{128,64},{192,128},{1,193},{65,1},{129,65},{193,129... | collective-permute-start | bytes 884744 | tf_op jit(solution)/shard_map/ppermute | solution.py:12
  250.3 1.2 convert_dynamic-update-slice_fusion.3
  251.5 1.2 convert_dynamic-update-slice_fusion.2
  252.7 2.9 %collective-permute-done.11 = bf16[288,512]{1,0:T(8,128)(2,1)S(1)} collective-permute-done((bf16[288,512]{1,0:T(8,128)(2,1)}, bf16[288,512]{1,0:T(8,128)(2,1)S(1)}, u32[]{:S(2)}, u32[]{:S(2)}) %collective-permute-start.11) | collective-permute-done | bytes 294944 | tf_op jit(solution)/shard_map/ppermute | solution.py:12
  255.6 1.2 convert_dynamic-update-slice_fusion.1
  256.9 0.6 reshape.158
  (87 shorter events, 5.3 us)
Async XLA Ops:
  0.6 7.2 %collective-permute-start = (bf16[48,2304]{1,0:T(8,128)(2,1)}, bf16[48,2304]{1,0:T(8,128)(2,1)S(1)}, u32[]{:S(2)}, u32[]{:S(2)}) collective-permute-start(bf16[48,2304]{1,0:T(8,128)(2,1)} %param.3), channel_id=1, source_target_pairs={{0,64},{64,128},{128,192},{192,0},{1,65},{65,129},{129,193},{193,1... | collective-permute-start | bytes 663560 | tf_op jit(solution)/shard_map/ppermute | solution.py:12
  2.8 12.4 %collective-permute-start.2 = (bf16[48,2304]{1,0:T(8,128)(2,1)}, bf16[48,2304]{1,0:T(8,128)(2,1)S(1)}, u32[]{:S(2)}, u32[]{:S(2)}) collective-permute-start(bf16[48,2304]{1,0:T(8,128)(2,1)} %param.3), channel_id=1, source_target_pairs={{0,128},{64,192},{128,0},{192,64},{1,129},{65,193},{129,1},{193,65... | collective-permute-start | bytes 663560 | tf_op jit(solution)/shard_map/ppermute | solution.py:12
  5.4 8.6 %collective-permute-start.1 = (bf16[48,2304]{1,0:T(8,128)(2,1)}, bf16[48,2304]{1,0:T(8,128)(2,1)S(1)}, u32[]{:S(2)}, u32[]{:S(2)}) collective-permute-start(bf16[48,2304]{1,0:T(8,128)(2,1)} %param.3), channel_id=1, source_target_pairs={{0,192},{64,0},{128,64},{192,128},{1,193},{65,1},{129,65},{193,129... | collective-permute-start | bytes 663560 | tf_op jit(solution)/shard_map/ppermute | solution.py:12
  15.3 20.0 %collective-permute-start.4 = (bf16[192,2304]{1,0:T(8,128)(2,1)S(1)}, bf16[192,2304]{1,0:T(8,128)(2,1)S(1)}, u32[]{:S(2)}, u32[]{:S(2)}) collective-permute-start(bf16[192,2304]{1,0:T(8,128)(2,1)S(1)} %bitcast.85), channel_id=1, source_target_pairs={{0,48},{8,56},{16,0},{24,8},{32,16},{40,24},{48,32},{56,40},{1,49}... | collective-permute-start | bytes 2654216 | tf_op jit(solution)/shard_map/ppermute | solution.py:17
  17.8 21.0 %collective-permute-start.3 = (bf16[192,2304]{1,0:T(8,128)(2,1)S(1)}, bf16[192,2304]{1,0:T(8,128)(2,1)S(1)}, u32[]{:S(2)}, u32[]{:S(2)}) collective-permute-start(bf16[192,2304]{1,0:T(8,128)(2,1)S(1)} %bitcast.86), channel_id=1, source_target_pairs={{0,16},{8,24},{16,32},{24,40},{32,48},{40,56},{48,0},{56,8},{1,17}... | collective-permute-start | bytes 2654216 | tf_op jit(solution)/shard_map/ppermute | solution.py:17
  35.3 10.6 %collective-permute-start.6 = (bf16[96,2304]{1,0:T(8,128)(2,1)S(1)}, bf16[96,2304]{1,0:T(8,128)(2,1)S(1)}, u32[]{:S(2)}, u32[]{:S(2)}) collective-permute-start(bf16[96,2304]{1,0:T(8,128)(2,1)S(1)} %slice.69), channel_id=1, source_target_pairs={{0,48},{8,56},{16,0},{24,8},{32,16},{40,24},{48,32},{56,40},{1,49}... | collective-permute-start | bytes 1327112 | tf_op jit(solution)/shard_map/ppermute | solution.py:17
  38.9 10.3 %collective-permute-start.5 = (bf16[96,2304]{1,0:T(8,128)(2,1)S(1)}, bf16[96,2304]{1,0:T(8,128)(2,1)S(1)}, u32[]{:S(2)}, u32[]{:S(2)}) collective-permute-start(bf16[96,2304]{1,0:T(8,128)(2,1)S(1)} %slice.68), channel_id=1, source_target_pairs={{0,16},{8,24},{16,32},{24,40},{32,48},{40,56},{48,0},{56,8},{1,17}... | collective-permute-start | bytes 1327112 | tf_op jit(solution)/shard_map/ppermute | solution.py:17
  39.9 13.8 %copy-start.6 = (bf16[2048,576]{0,1:T(8,128)(2,1)S(1)}, bf16[2048,576]{0,1:T(8,128)(2,1)}, u32[]{:S(2)}) copy-start(bf16[2048,576]{0,1:T(8,128)(2,1)} %param.4) | copy-start | bytes 7077892
  50.2 45.2 %collective-permute-start.7 = (bf16[768,2304]{1,0:T(8,128)(2,1)}, bf16[768,2304]{1,0:T(8,128)(2,1)}, u32[]{:S(2)}, u32[]{:S(2)}) collective-permute-start(bf16[768,2304]{1,0:T(8,128)(2,1)} %bitcast.9), channel_id=1, source_target_pairs={{0,8},{8,0},{16,24},{24,16},{32,40},{40,32},{48,56},{56,48},{1,9},... | collective-permute-start | bytes 10616840 | tf_op jit(solution)/shard_map/ppermute | solution.py:22
  55.7 5.4 %copy-start = (bf16[384,2048]{1,0:T(8,128)(2,1)S(1)}, bf16[384,2048]{1,0:T(8,128)(2,1)}, u32[]{:S(2)}) copy-start(bf16[384,2048]{1,0:T(8,128)(2,1)} %param.5) | copy-start | bytes 4718596
  55.7 34.5 %all-to-all-start = ((bf16[4,576,512]{2,1,0:T(8,128)(2,1)}), bf16[4,576,512]{2,1,0:T(8,128)(2,1)}, u32[]{:S(2)}, u32[]{:S(2)}) async-start(bf16[4,576,512]{2,1,0:T(8,128)(2,1)} %pad_maximum_fusion.3), calls=%async_computation | async-start | bytes 4718592 | tf_op jit(solution)/shard_map/all_to_all | solution.py:98
  100.3 1.3 copy-start.1
  102.9 13.7 %all-to-all-start.1 = ((f32[32,1,1920]{2,1,0:T(1,128)}), f32[32,1,1920]{2,1,0:T(1,128)S(1)}, u32[]{:S(2)}, u32[]{:S(2)}) async-start(f32[32,1,1920]{2,1,0:T(1,128)} %broadcast_in_dim.50), calls=%async_computation.1 | async-start | bytes 491520 | tf_op jit(solution)/shard_map/all_to_all | solution.py:68
  116.6 25.1 %all-to-all-start.3 = ((bf16[4,384,512]{2,1,0:T(8,128)(2,1)}), bf16[4,384,512]{2,1,0:T(8,128)(2,1)}, u32[]{:S(2)}, u32[]{:S(2)}) async-start(bf16[4,384,512]{2,1,0:T(8,128)(2,1)} %pad_maximum_fusion.4), calls=%async_computation.3 | async-start | bytes 3145728 | tf_op jit(solution)/shard_map/all_to_all | solution.py:100
  121.0 44.2 %collective-permute-start.15 = (bf16[2304,512]{1,0:T(8,128)(2,1)}, bf16[2304,512]{1,0:T(8,128)(2,1)}, u32[]{:S(2)}, u32[]{:S(2)}) collective-permute-start(bf16[2304,512]{1,0:T(8,128)(2,1)} %bitcast.15), channel_id=1, source_target_pairs={{0,8},{8,0},{16,24},{24,16},{32,40},{40,32},{48,56},{56,48},{1,9},... | collective-permute-start | bytes 7077896 | tf_op jit(solution)/shard_map/ppermute | solution.py:22
  121.4 37.2 %copy-start.2 = (f32[768,512]{1,0:T(8,128)S(1)}, f32[768,512]{1,0:T(8,128)}, u32[]{:S(2)}) copy-start(f32[768,512]{1,0:T(8,128)} %copy-done.1) | copy-start | bytes 4718596
  142.4 15.8 %all-to-all-start.2 = ((f32[8,1,3072]{2,1,0:T(1,128)}), f32[8,1,3072]{2,1,0:T(1,128)S(1)}, u32[]{:S(2)}, u32[]{:S(2)}) async-start(f32[8,1,3072]{2,1,0:T(1,128)} %broadcast_in_dim.51), calls=%async_computation.2 | async-start | bytes 196608 | tf_op jit(solution)/shard_map/all_to_all | solution.py:68
  158.5 4.3 %copy-start.5 = (bf16[4,4,1,48,512]{4,3,2,1,0:T(8,128)(2,1)S(1)}, bf16[4,4,1,48,512]{4,3,2,1,0:T(8,128)(2,1)}, u32[]{:S(2)}) copy-start(bf16[4,4,1,48,512]{4,3,2,1,0:T(8,128)(2,1)} %get-tuple-element.44) | copy-start | bytes 2359300
  160.4 3.1 %copy-start.8 = (bf16[768,512]{1,0:T(8,128)(2,1)}, bf16[768,512]{1,0:T(8,128)(2,1)S(1)}, u32[]{:S(2)}) copy-start(bf16[768,512]{1,0:T(8,128)(2,1)S(1)} %fusion.17) | copy-start | bytes 2359300
  160.4 4.4 %collective-permute-start.14 = (bf16[768,512]{1,0:T(8,128)(2,1)S(1)}, bf16[768,512]{1,0:T(8,128)(2,1)S(1)}, u32[]{:S(2)}, u32[]{:S(2)}) collective-permute-start(bf16[768,512]{1,0:T(8,128)(2,1)S(1)} %fusion.17), channel_id=1, source_target_pairs={{0,8},{8,0},{16,24},{24,16},{32,40},{40,32},{48,56},{56,48},{1,9},... | collective-permute-start | bytes 2359304 | tf_op jit(solution)/shard_map/ppermute | solution.py:22
  163.4 1.7 copy-start.3
  169.3 12.6 %collective-permute-start.16 = (bf16[96,2304]{1,0:T(8,128)(2,1)S(1)}, bf16[96,2304]{1,0:T(8,128)(2,1)S(1)}, u32[]{:S(2)}, u32[]{:S(2)}) collective-permute-start(bf16[96,2304]{1,0:T(8,128)(2,1)S(1)} %get-tuple-element.16), channel_id=1, source_target_pairs={{0,16},{8,24},{16,32},{24,40},{32,48},{40,56},{48,0},{56,8},{1,17}... | collective-permute-start | bytes 1327112 | tf_op jit(solution)/shard_map/ppermute | solution.py:17
  175.4 11.2 %collective-permute-start.20 = (bf16[96,2304]{1,0:T(8,128)(2,1)S(1)}, bf16[96,2304]{1,0:T(8,128)(2,1)S(1)}, u32[]{:S(2)}, u32[]{:S(2)}) collective-permute-start(bf16[96,2304]{1,0:T(8,128)(2,1)S(1)} %get-tuple-element.21), channel_id=1, source_target_pairs={{0,48},{8,56},{16,0},{24,8},{32,16},{40,24},{48,32},{56,40},{1,49}... | collective-permute-start | bytes 1327112 | tf_op jit(solution)/shard_map/ppermute | solution.py:17
  177.7 18.4 %collective-permute-start.18 = (bf16[96,2304]{1,0:T(8,128)(2,1)S(1)}, bf16[96,2304]{1,0:T(8,128)(2,1)S(1)}, u32[]{:S(2)}, u32[]{:S(2)}) collective-permute-start(bf16[96,2304]{1,0:T(8,128)(2,1)S(1)} %get-tuple-element.17), channel_id=1, source_target_pairs={{0,48},{8,56},{16,0},{24,8},{32,16},{40,24},{48,32},{56,40},{1,49}... | collective-permute-start | bytes 1327112 | tf_op jit(solution)/shard_map/ppermute | solution.py:17
  182.1 14.0 %collective-permute-start.17 = (bf16[96,2304]{1,0:T(8,128)(2,1)S(1)}, bf16[96,2304]{1,0:T(8,128)(2,1)S(1)}, u32[]{:S(2)}, u32[]{:S(2)}) collective-permute-start(bf16[96,2304]{1,0:T(8,128)(2,1)S(1)} %add.229), channel_id=1, source_target_pairs={{0,16},{8,24},{16,32},{24,40},{32,48},{40,56},{48,0},{56,8},{1,17}... | collective-permute-start | bytes 1327112 | tf_op jit(solution)/shard_map/ppermute | solution.py:17
  182.2 21.2 %collective-permute-start.19 = (bf16[96,2304]{1,0:T(8,128)(2,1)S(1)}, bf16[96,2304]{1,0:T(8,128)(2,1)S(1)}, u32[]{:S(2)}, u32[]{:S(2)}) collective-permute-start(bf16[96,2304]{1,0:T(8,128)(2,1)S(1)} %get-tuple-element.19), channel_id=1, source_target_pairs={{0,16},{8,24},{16,32},{24,40},{32,48},{40,56},{48,0},{56,8},{1,17}... | collective-permute-start | bytes 1327112 | tf_op jit(solution)/shard_map/ppermute | solution.py:17
  186.7 18.8 %collective-permute-start.21 = (bf16[96,2304]{1,0:T(8,128)(2,1)S(1)}, bf16[96,2304]{1,0:T(8,128)(2,1)S(1)}, u32[]{:S(2)}, u32[]{:S(2)}) collective-permute-start(bf16[96,2304]{1,0:T(8,128)(2,1)S(1)} %add.233), channel_id=1, source_target_pairs={{0,48},{8,56},{16,0},{24,8},{32,16},{40,24},{48,32},{56,40},{1,49}... | collective-permute-start | bytes 1327112 | tf_op jit(solution)/shard_map/ppermute | solution.py:17
  205.7 6.0 %copy-start.4 = (bf16[768,512]{1,0:T(8,128)(2,1)S(1)}, bf16[768,512]{1,0:T(8,128)(2,1)}, u32[]{:S(2)}) copy-start(bf16[768,512]{1,0:T(8,128)(2,1)} %copy-done.3) | copy-start | bytes 2359300
  205.7 6.0 %copy-start.9 = (bf16[768,512]{1,0:T(8,128)(2,1)S(1)}, bf16[768,512]{1,0:T(8,128)(2,1)}, u32[]{:S(2)}) copy-start(bf16[768,512]{1,0:T(8,128)(2,1)} %copy-done.8) | copy-start | bytes 2359300
  207.8 49.0 %all-to-all-start.4 = ((bf16[32,108,128]{2,1,0:T(8,128)(2,1)}), bf16[32,108,128]{2,1,0:T(8,128)(2,1)S(1)}, u32[]{:S(2)}, u32[]{:S(2)}) async-start(bf16[32,108,128]{2,1,0:T(8,128)(2,1)} %convert_element_type.92), calls=%async_computation.4 | async-start | bytes 1835008 | tf_op jit(solution)/shard_map/all_to_all | solution.py:168
  218.7 1.4 copy-start.7
  220.2 30.1 %collective-permute-start.8 = (bf16[576,512]{1,0:T(8,128)(2,1)S(1)}, bf16[576,512]{1,0:T(8,128)(2,1)S(1)}, u32[]{:S(2)}, u32[]{:S(2)}) collective-permute-start(bf16[576,512]{1,0:T(8,128)(2,1)S(1)} %get-tuple-element.35), channel_id=1, source_target_pairs={{0,64},{64,128},{128,192},{192,0},{1,65},{65,129},{129,193},{193,1... | collective-permute-start | bytes 1769480 | tf_op jit(solution)/shard_map/ppermute | solution.py:12
  221.4 30.1 %collective-permute-start.9 = (bf16[576,512]{1,0:T(8,128)(2,1)S(1)}, bf16[576,512]{1,0:T(8,128)(2,1)S(1)}, u32[]{:S(2)}, u32[]{:S(2)}) collective-permute-start(bf16[576,512]{1,0:T(8,128)(2,1)S(1)} %get-tuple-element.34), channel_id=1, source_target_pairs={{0,192},{64,0},{128,64},{192,128},{1,193},{65,1},{129,65},{193,129... | collective-permute-start | bytes 1769480 | tf_op jit(solution)/shard_map/ppermute | solution.py:12
  224.8 22.6 %collective-permute-start.10 = (bf16[288,512]{1,0:T(8,128)(2,1)}, bf16[288,512]{1,0:T(8,128)(2,1)}, u32[]{:S(2)}, u32[]{:S(2)}) collective-permute-start(bf16[288,512]{1,0:T(8,128)(2,1)} %get-tuple-element.32), channel_id=1, source_target_pairs={{0,64},{64,128},{128,192},{192,0},{1,65},{65,129},{129,193},{193,1... | collective-permute-start | bytes 884744 | tf_op jit(solution)/shard_map/ppermute | solution.py:12
  224.8 22.6 %collective-permute-start.12 = (bf16[288,512]{1,0:T(8,128)(2,1)}, bf16[288,512]{1,0:T(8,128)(2,1)}, u32[]{:S(2)}, u32[]{:S(2)}) collective-permute-start(bf16[288,512]{1,0:T(8,128)(2,1)} %get-tuple-element.33), channel_id=1, source_target_pairs={{0,192},{64,0},{128,64},{192,128},{1,193},{65,1},{129,65},{193,129... | collective-permute-start | bytes 884744 | tf_op jit(solution)/shard_map/ppermute | solution.py:12
  247.4 8.2 %collective-permute-start.11 = (bf16[288,512]{1,0:T(8,128)(2,1)}, bf16[288,512]{1,0:T(8,128)(2,1)S(1)}, u32[]{:S(2)}, u32[]{:S(2)}) collective-permute-start(bf16[288,512]{1,0:T(8,128)(2,1)} %collective-permute-done.10), channel_id=1, source_target_pairs={{0,64},{64,128},{128,192},{192,0},{1,65},{65,129},{129,193},{193,1... | collective-permute-start | bytes 884744 | tf_op jit(solution)/shard_map/ppermute | solution.py:12
  247.4 8.2 %collective-permute-start.13 = (bf16[288,512]{1,0:T(8,128)(2,1)}, bf16[288,512]{1,0:T(8,128)(2,1)S(1)}, u32[]{:S(2)}, u32[]{:S(2)}) collective-permute-start(bf16[288,512]{1,0:T(8,128)(2,1)} %collective-permute-done.12), channel_id=1, source_target_pairs={{0,192},{64,0},{128,64},{192,128},{1,193},{65,1},{129,65},{193,129... | collective-permute-start | bytes 884744 | tf_op jit(solution)/shard_map/ppermute | solution.py:12
